TPU v7x, 32 devices: a whole 2x2x4 slice. The times are simulated.
32 devices in a mesh: strata: 8 (over z, x), users: 4 (over y, core).
Axes of the slice: x: 2, y: 2, z: 4, core: 2. Of those that a mesh axis runs over, the one named last changes fastest.
Arguments:
- user_factors: float32 [65536, 256], P(('strata', 'users')), may hold values from -1.5 to 1.5
- item_factors: float32 [8192, 256], P(('strata', 'users')), may hold values from -1.5 to 1.5
- tile_rows: int32 [8, 4, 2, 64], P('strata', 'users'), may hold values from 0 to 15, as said below
- tile_columns: int32 [8, 4, 2, 64], P('strata', 'users'), may hold values from 0 to 7, as said below
- tile_counts: int32 [8, 4, 2], P('strata', 'users'), may hold values from 8 to 64, as said below
- ratings: int32 [8, 4, 2, 64, 128, 128], P('strata', 'users'), may hold values from 0 to 5
Outputs:
- updated_users: float32 [65536, 256], P(('strata', 'users'))
- updated_items: float32 [8192, 256], P(('strata', 'users'))
Inputs may be any that keep to these rules, and one draw needn't show every extreme that they name: `tile_rows`: row tile of each slot within the device's users. `tile_columns`: item tile of each slot within the step's item block; a device's slots of one step name distinct pairs of user tile and item tile, padding slots included. `tile_counts`: in every step some device uses all 64 slots.
All inputs are finite; a program needn't handle non-finite values.
Results may differ from a plain program's by a relative error of at most 0.0004.
Values may be sent and summed in bfloat16 or wider, within the bound.
No kernel may reach another device: no remote copies, remote signals or barrier semaphores. Data moves between devices by JAX's collectives and lax.ppermute only.
A program may use at most 128 MiB of HBM per device.

v0:
```python
import functools

import jax
import jax.numpy as jnp
from jax import lax
from jax.experimental import pallas as pl
from jax.experimental.pallas import tpu as pltpu
from jax.sharding import PartitionSpec as P

F32 = jnp.float32
BF16 = jnp.bfloat16
VMEM = pl.BlockSpec(memory_space=pltpu.VMEM)
SMEM = pl.BlockSpec(memory_space=pltpu.SMEM)
ANY = pl.BlockSpec(memory_space=pl.ANY)
BOTH_ROWS = (((0,), (0,)), ((), ()))
BOTH_COLUMNS = (((1,), (1,)), ((), ()))
MIB = 1 << 20


def route(block, strata_shift, users_flip):
    strata, users = lax.axis_size("strata"), lax.axis_size("users")
    pairs = [
        (s * users + u, ((s + strata_shift) % strata) * users + (u ^ users_flip))
        for s in range(strata)
        for u in range(users)
    ]
    return lax.ppermute(block, ("strata", "users"), pairs)


def dense_kernel(step, tiles_per_shard, rows_ref, columns_ref, counts_ref, ratings_ref, dense_ref, tiles, arrived):
    count = counts_ref[0, 0, step]
    flip = lax.axis_index("users") * tiles_per_shard
    tile = tiles.shape[1]

    def copy(m):
        return pltpu.make_async_copy(ratings_ref.at[0, 0, step, m], tiles.at[m], arrived.at[m])

    @pl.loop(0, count)
    def _(m):
        copy(m).start()

    @pl.loop(0, dense_ref.shape[0])
    def _(j):
        @pl.loop(0, dense_ref.shape[1] // tile)
        def _(r):
            dense_ref[j, pl.ds(r * tile, tile), :] = jnp.zeros((tile, tile), BF16)

    @pl.loop(0, count)
    def _(m):
        j = columns_ref[0, 0, step, m] ^ flip
        r = rows_ref[0, 0, step, m]
        copy(m).wait()
        dense_ref[j, pl.ds(pl.multiple_of(r * tile, tile), tile), :] = (
            tiles[m].astype(F32).astype(BF16)
        )


def dense_ratings(step, tiles_per_shard, column_tiles, user_rows, tile_rows, tile_columns, tile_counts, ratings):
    slots, tile = ratings.shape[3], ratings.shape[4]
    return pl.pallas_call(
        functools.partial(dense_kernel, step, tiles_per_shard),
        out_shape=jax.ShapeDtypeStruct((column_tiles, user_rows, tile), BF16),
        in_specs=[SMEM, SMEM, SMEM, ANY],
        out_specs=VMEM,
        scratch_shapes=[
            pltpu.VMEM((slots, tile, tile), jnp.int32),
            pltpu.SemaphoreType.DMA((slots,)),
        ],
        compiler_params=pltpu.CompilerParams(vmem_limit_bytes=12 * MIB),
        cost_estimate=pl.CostEstimate(flops=2 * 10**9, bytes_accessed=8 * MIB, transcendentals=0),
        name=f"dense_{step}",
    )(tile_rows, tile_columns, tile_counts, ratings)


def terms_kernel(columns, chunk, users_ref, dense_ref, *refs):
    number = len(columns)
    item_refs, residual_refs, grad_refs = refs[:number], refs[number : 2 * number], refs[2 * number :]
    tile = item_refs[0].shape[0]
    items = jnp.concatenate([ref[...] for ref in item_refs], axis=0)
    for ref in grad_refs:
        ref[...] = jnp.zeros_like(ref)

    @pl.loop(0, users_ref.shape[0] // chunk)
    def _(i):
        rows = pl.ds(pl.multiple_of(i * chunk, chunk), chunk)
        users = users_ref[rows, :]
        predicted = lax.dot_general(users, items, BOTH_COLUMNS, preferred_element_type=F32)
        for k, j in enumerate(columns):
            rating = dense_ref[j, rows, :].astype(F32)
            residual = jnp.where(
                rating > 0, rating - predicted[:, k * tile : (k + 1) * tile], 0.0
            ).astype(BF16)
            residual_refs[k][rows, :] = residual
            grad_refs[k][...] += lax.dot_general(
                residual, users, BOTH_ROWS, preferred_element_type=F32
            )


def terms(columns, users_low, dense, items):
    user_rows, width = users_low.shape
    tile = items[0].shape[0]
    number = len(columns)
    return pl.pallas_call(
        functools.partial(terms_kernel, columns, min(512, user_rows)),
        out_shape=[jax.ShapeDtypeStruct((user_rows, tile), BF16)] * number
        + [jax.ShapeDtypeStruct((tile, width), F32)] * number,
        in_specs=[VMEM] * (2 + number),
        out_specs=[VMEM] * (2 * number),
        compiler_params=pltpu.CompilerParams(vmem_limit_bytes=16 * MIB),
        cost_estimate=pl.CostEstimate(
            flops=4 * user_rows * tile * width * number, bytes_accessed=MIB, transcendentals=0
        ),
        name="terms_" + "_".join(map(str, columns)),
    )(users_low, dense, *items)


def users_kernel(number, low_out, users_ref, *refs):
    item_refs, residual_refs, outs = refs[:number], refs[number : 2 * number], refs[2 * number :]
    total = None
    for k in range(0, number, 2):
        two = slice(k, k + 2)
        residual = jnp.concatenate([ref[...] for ref in residual_refs[two]], axis=1)
        items = jnp.concatenate([ref[...] for ref in item_refs[two]], axis=0)
        part = jnp.dot(residual, items, preferred_element_type=F32)
        total = part if total is None else total + part
    users = users_ref[...]
    updated = users + 0.01 * (total - 0.05 * users)
    outs[0][...] = updated
    if low_out:
        outs[1][...] = updated.astype(BF16)


def update_users(users, items, residuals, low_out):
    user_rows, width = users.shape
    number = len(items)
    tile = items[0].shape[0]
    chunk = min(256, user_rows)
    block = pl.BlockSpec((chunk, width), lambda i: (i, 0))
    out_types = [jax.ShapeDtypeStruct(users.shape, F32)]
    if low_out:
        out_types.append(jax.ShapeDtypeStruct(users.shape, BF16))
    return pl.pallas_call(
        functools.partial(users_kernel, number, low_out),
        grid=(user_rows // chunk,),
        out_shape=out_types,
        in_specs=[block]
        + [pl.BlockSpec((tile, width), lambda i: (0, 0))] * number
        + [pl.BlockSpec((chunk, tile), lambda i: (i, 0))] * number,
        out_specs=[block] * len(out_types),
        compiler_params=pltpu.CompilerParams(vmem_limit_bytes=12 * MIB),
        cost_estimate=pl.CostEstimate(
            flops=2 * user_rows * tile * number * width, bytes_accessed=4 * MIB, transcendentals=0
        ),
        name="users",
    )(users, *items, *residuals)


def updated_items(items, grad):
    return items + 0.003 * (grad - 0.05 * items)


def paired_shards(user_factors, item_factors, tile_rows, tile_columns, tile_counts, ratings):
    step_total, tile = ratings.shape[2], ratings.shape[-1]
    per_shard = item_factors.shape[0] // tile
    column_tiles = per_shard * lax.axis_size("users")
    halves = range(per_shard)
    parts = [item_factors[h * tile : (h + 1) * tile] for h in halves]
    low = [part.astype(BF16) for part in parts]
    users_now = user_factors
    users_low = user_factors.astype(BF16)
    held = {0: low, 2: [route(block, 0, 2) for block in low]}
    for step in range(step_total):
        dense = dense_ratings(
            step, per_shard, column_tiles, users_now.shape[0], tile_rows, tile_columns, tile_counts, ratings
        )
        for d in (0, 2):
            held[d + 1] = [route(block, 0, 1) for block in held[d]]
        residuals, grads = {}, {}
        for h in halves:
            for d in (2, 3, 0, 1):
                residuals[d, h], grads[d, h] = terms(
                    (d * per_shard + h,), users_low, dense, [held[d][h]]
                )
        sums = []
        for h in halves:
            far = grads[3, h] + route(grads[2, h], 0, 1)
            near = grads[0, h] + route(grads[1, h], 0, 1)
            sums.append(near + route(far, 0, 3))
        parts = [updated_items(part, grad) for part, grad in zip(parts, sums)]
        last = step == step_total - 1
        order = [(d, h) for h in halves for d in range(4)]
        results = update_users(
            users_now, [held[d][h] for d, h in order], [residuals[k] for k in order], not last
        )
        users_now = results[0]
        if not last:
            users_low = results[1]
            low = [part.astype(BF16) for part in parts]
            held = {0: [], 2: []}
            for block in low:
                held[0].append(route(block, 1, 0))
                held[2].append(route(block, 1, 2))
            parts = [route(part, 1, 0) for part in parts]
    return users_now, jnp.concatenate(parts, axis=0)


def gathered_shards(user_factors, item_factors, tile_rows, tile_columns, tile_counts, ratings):
    step_total, tile = ratings.shape[2], ratings.shape[-1]
    users_now, item_part = user_factors, item_factors
    for step in range(step_total):
        block = lax.all_gather(item_part.astype(BF16), "users", axis=0, tiled=True)
        column_tiles = block.shape[0] // tile
        items = [block[j * tile : (j + 1) * tile] for j in range(column_tiles)]
        dense = dense_ratings(
            step, 0, column_tiles, users_now.shape[0], tile_rows, tile_columns, tile_counts, ratings
        )
        users_low = users_now.astype(BF16)
        residuals, grads = [], []
        for j in range(column_tiles):
            residual, grad = terms((j,), users_low, dense, [items[j]])
            residuals.append(residual)
            grads.append(grad)
        grad_part = lax.psum_scatter(
            jnp.concatenate(grads, axis=0), "users", scatter_dimension=0, tiled=True
        )
        users_now = update_users(users_now, items, residuals, False)[0]
        item_part = updated_items(item_part, grad_part)
        if step < step_total - 1:
            item_part = route(item_part, 1, 0)
    return users_now, item_part


def solution(mesh):
    placed = (
        P(("strata", "users"), None),
        P(("strata", "users"), None),
        P("strata", "users", None, None),
        P("strata", "users", None, None),
        P("strata", "users", None),
        P("strata", "users", None, None, None, None),
    )

    def shards(user_factors, item_factors, *lists):
        tile = lists[-1].shape[-1]
        paired = mesh.shape["users"] == 4 and item_factors.shape[0] % tile == 0
        body = paired_shards if paired else gathered_shards
        return body(user_factors, item_factors, *lists)

    return jax.shard_map(
        shards,
        mesh=mesh,
        in_specs=placed,
        out_specs=(P(("strata", "users"), None), P(("strata", "users"), None)),
        check_vma=False,
    )
```

profile of v0, /device:TPU:17, one launch (start us, length us, event | category | flops | bytes accessed | tf_op | source)
XLA Modules:
  0.0 84.1 jit_solution(100657224081595275)
XLA Ops:
  0.6 1.0 %fusion.2 = (bf16[128,256]{1,0:T(8,128)(2,1)S(1)}, bf16[128,256]{1,0:T(8,128)(2,1)S(1)}) fusion(f32[256,256]{1,0:T(8,128)} %param.7), kind=kLoop, calls=%fused_computation.9 | loop fusion | bytes 262144 | tf_op jit(solution)/shard_map/slice | solution.py:167
  1.6 1.3 %collective-permute-start.4 = (bf16[128,256]{1,0:T(8,128)(2,1)S(1)}, bf16[128,256]{1,0:T(8,128)(2,1)S(1)}, u32[]{:S(2)}, u32[]{:S(2)}) collective-permute-start(bf16[128,256]{1,0:T(8,128)(2,1)S(1)} %get-tuple-element.76.refs_0_.refs_4_), channel_id=1, source_target_pairs={{0,2},{1,3},{2,0},{3,1},{4,6},{5,7},{6,4},{7,5},{8,10},{9,11},{10,... | collective-permute-start | bytes 196616 | tf_op jit(solution)/shard_map/ppermute | solution.py:27
  2.9 1.0 %collective-permute-start.3 = (bf16[128,256]{1,0:T(8,128)(2,1)S(1)}, bf16[128,256]{1,0:T(8,128)(2,1)S(1)}, u32[]{:S(2)}, u32[]{:S(2)}) collective-permute-start(bf16[128,256]{1,0:T(8,128)(2,1)S(1)} %get-tuple-element.76.refs_0_.refs_4_), channel_id=1, source_target_pairs={{0,1},{1,0},{2,3},{3,2},{4,5},{5,4},{6,7},{7,6},{8,9},{9,8},{10,11... | collective-permute-start | bytes 196616 | tf_op jit(solution)/shard_map/ppermute | solution.py:27
  3.9 0.2 collective-permute-start.1
  4.1 0.3 collective-permute-start
  4.4 3.4 %copy-done = s32[1,1,2,64,128,128]{5,4,3,2,1,0:T(8,128)S(1)} copy-done((s32[1,1,2,64,128,128]{5,4,3,2,1,0:T(8,128)S(1)}, s32[1,1,2,64,128,128]{5,4,3,2,1,0:T(8,128)}, u32[]{:S(2)}) %copy-start) | copy-done | bytes 8388632
  7.8 0.7 copy-done.2
  8.5 0.7 copy-done.4
  9.1 0.7 copy-done.6
  9.8 3.4 %dense_0.1.dense_ref = bf16[8,2048,128]{2,1,0:T(8,128)(2,1)S(1)} custom-call(s32[1,1,2,64]{3,2,1,0:T(2,128)S(1)} %copy-done.2, s32[1,1,2,64]{3,2,1,0:T(2,128)S(1)} %copy-done.4, s32[1,1,2]{2,1,0:T(1,128)S(1)} %copy-done.6, s32[1,1,2,64,128,128]{5,4,3,2,1,0:T(8,128)S(1)} %copy-done), custom_call_target="tpu_custom_call" | custom-call | flops 2000000000 | bytes 8388608 | tf_op jit(solution)/shard_map/dense_0/pallas_call | solution.py:60
  13.2 0.1 convert_element_type.17.users_ref
  13.3 1.8 %terms_5.2 = (bf16[2048,128]{1,0:T(8,128)(2,1)S(1)}, f32[128,256]{1,0:T(8,128)S(1)}) custom-call(bf16[2048,256]{1,0:T(8,128)(2,1)S(1)} %convert_element_type.17.users_ref, bf16[8,2048,128]{2,1,0:T(8,128)(2,1)S(1)} %dense_0.1.dense_ref, bf16[128,256]{1,0:T(8,128)(2,1)S(1)} %collective-permute-done.4.refs_0_.refs_6_), custom_call_target="tpu_custom_call" | custom-call | flops 268435456 | bytes 1048576 | tf_op jit(solution)/shard_map/terms_5/pallas_call | solution.py:103
  15.2 2.6 %collective-permute-start.14 = (f32[128,256]{1,0:T(8,128)S(1)}, f32[128,256]{1,0:T(8,128)S(1)}, u32[]{:S(2)}, u32[]{:S(2)}) collective-permute-start(f32[128,256]{1,0:T(8,128)S(1)} %get-tuple-element.52), channel_id=1, source_target_pairs={{0,1},{1,0},{2,3},{3,2},{4,5},{5,4},{6,7},{7,6},{8,9},{9,8},{10,11... | collective-permute-start | bytes 393224 | tf_op jit(solution)/shard_map/ppermute | solution.py:27
  17.8 1.8 %terms_4.2 = (bf16[2048,128]{1,0:T(8,128)(2,1)S(1)}, f32[128,256]{1,0:T(8,128)S(1)}) custom-call(bf16[2048,256]{1,0:T(8,128)(2,1)S(1)} %convert_element_type.17.users_ref, bf16[8,2048,128]{2,1,0:T(8,128)(2,1)S(1)} %dense_0.1.dense_ref, bf16[128,256]{1,0:T(8,128)(2,1)S(1)} %collective-permute-done.1.refs_0_.refs_2_), custom_call_target="tpu_custom_call" | custom-call | flops 268435456 | bytes 1048576 | tf_op jit(solution)/shard_map/terms_4/pallas_call | solution.py:103
  19.6 0.1 collective-permute-start.7
  19.7 1.8 %terms_0.2 = (bf16[2048,128]{1,0:T(8,128)(2,1)S(1)}, f32[128,256]{1,0:T(8,128)S(1)}) custom-call(bf16[2048,256]{1,0:T(8,128)(2,1)S(1)} %convert_element_type.17.users_ref, bf16[8,2048,128]{2,1,0:T(8,128)(2,1)S(1)} %dense_0.1.dense_ref, bf16[128,256]{1,0:T(8,128)(2,1)S(1)} %get-tuple-element.77.refs_0_), custom_call_target="tpu_custom_call" | custom-call | flops 268435456 | bytes 1048576 | tf_op jit(solution)/shard_map/terms_0/pallas_call | solution.py:103
  21.5 0.6 collective-permute-start.5
  22.1 1.8 %terms_1.2 = (bf16[2048,128]{1,0:T(8,128)(2,1)S(1)}, f32[128,256]{1,0:T(8,128)S(1)}) custom-call(bf16[2048,256]{1,0:T(8,128)(2,1)S(1)} %convert_element_type.17.users_ref, bf16[8,2048,128]{2,1,0:T(8,128)(2,1)S(1)} %dense_0.1.dense_ref, bf16[128,256]{1,0:T(8,128)(2,1)S(1)} %get-tuple-element.76.refs_0_.refs_4_), custom_call_target="tpu_custom_call" | custom-call | flops 268435456 | bytes 1048576 | tf_op jit(solution)/shard_map/terms_1/pallas_call | solution.py:103
  23.9 0.1 collective-permute-start.2
  24.0 1.8 %terms_3.2 = (bf16[2048,128]{1,0:T(8,128)(2,1)S(1)}, f32[128,256]{1,0:T(8,128)S(1)}) custom-call(bf16[2048,256]{1,0:T(8,128)(2,1)S(1)} %convert_element_type.17.users_ref, bf16[8,2048,128]{2,1,0:T(8,128)(2,1)S(1)} %dense_0.1.dense_ref, bf16[128,256]{1,0:T(8,128)(2,1)S(1)} %collective-permute-done.3.refs_0_.refs_5_), custom_call_target="tpu_custom_call" | custom-call | flops 268435456 | bytes 1048576 | tf_op jit(solution)/shard_map/terms_3/pallas_call | solution.py:103
  25.9 0.6 collective-permute-start.13
  26.4 1.8 %terms_2.2 = (bf16[2048,128]{1,0:T(8,128)(2,1)S(1)}, f32[128,256]{1,0:T(8,128)S(1)}) custom-call(bf16[2048,256]{1,0:T(8,128)(2,1)S(1)} %convert_element_type.17.users_ref, bf16[8,2048,128]{2,1,0:T(8,128)(2,1)S(1)} %dense_0.1.dense_ref, bf16[128,256]{1,0:T(8,128)(2,1)S(1)} %collective-permute-done.refs_0_.refs_1_), custom_call_target="tpu_custom_call" | custom-call | flops 268435456 | bytes 1048576 | tf_op jit(solution)/shard_map/terms_2/pallas_call | solution.py:103
  28.3 0.0 slice-start.1
  28.3 0.1 collective-permute-start.6
  28.4 1.8 %terms_7.2 = (bf16[2048,128]{1,0:T(8,128)(2,1)S(1)}, f32[128,256]{1,0:T(8,128)S(1)}) custom-call(bf16[2048,256]{1,0:T(8,128)(2,1)S(1)} %convert_element_type.17.users_ref, bf16[8,2048,128]{2,1,0:T(8,128)(2,1)S(1)} %dense_0.1.dense_ref, bf16[128,256]{1,0:T(8,128)(2,1)S(1)} %collective-permute-done.5.refs_0_.refs_7_), custom_call_target="tpu_custom_call" | custom-call | flops 268435456 | bytes 1048576 | tf_op jit(solution)/shard_map/terms_7/pallas_call | solution.py:103
  30.2 0.0 copy-start.3
  30.2 0.0 copy-start.5
  30.2 0.0 copy-start.7
  30.3 0.0 collective-permute-done.2.refs_0_.refs_3_
  30.3 1.8 %terms_6.2 = (bf16[2048,128]{1,0:T(8,128)(2,1)S(1)}, f32[128,256]{1,0:T(8,128)S(1)}) custom-call(bf16[2048,256]{1,0:T(8,128)(2,1)S(1)} %convert_element_type.17.users_ref, bf16[8,2048,128]{2,1,0:T(8,128)(2,1)S(1)} %dense_0.1.dense_ref, bf16[128,256]{1,0:T(8,128)(2,1)S(1)} %collective-permute-done.2.refs_0_.refs_3_), custom_call_target="tpu_custom_call" | custom-call | flops 268435456 | bytes 1048576 | tf_op jit(solution)/shard_map/terms_6/pallas_call | solution.py:103
  32.1 0.0 collective-permute-done.14
  32.1 0.2 collective-permute-start.15
  32.3 0.0 collective-permute-done.7
  32.3 0.0 copy-start.8
  32.4 1.7 %collective-permute-start.8 = (f32[128,256]{1,0:T(8,128)S(1)}, f32[128,256]{1,0:T(8,128)S(1)}, u32[]{:S(2)}, u32[]{:S(2)}) collective-permute-start(f32[128,256]{1,0:T(8,128)S(1)} %add.49), channel_id=1, source_target_pairs={{0,3},{1,2},{2,1},{3,0},{4,7},{5,6},{6,5},{7,4},{8,11},{9,10},{10,... | collective-permute-start | bytes 393224 | tf_op jit(solution)/shard_map/ppermute | solution.py:27
  34.1 7.6 %dense_1.1.dense_ref = bf16[8,2048,128]{2,1,0:T(8,128)(2,1)S(1)} custom-call(s32[1,1,2,64]{3,2,1,0:T(2,128)S(1)} %copy-done.3, s32[1,1,2,64]{3,2,1,0:T(2,128)S(1)} %copy-done.5, s32[1,1,2]{2,1,0:T(1,128)S(1)} %copy-done.7, s32[1,1,2,64,128,128]{5,4,3,2,1,0:T(8,128)S(1)} %bitcast.1), custom_call_target="tpu_custom_call" | custom-call | flops 2000000000 | bytes 8388608 | tf_op jit(solution)/shard_map/dense_1/pallas_call | solution.py:60
  41.7 0.0 collective-permute-done.13
  41.7 0.1 fusion
  41.8 1.9 %collective-permute-start.11 = (bf16[128,256]{1,0:T(8,128)(2,1)S(1)}, bf16[128,256]{1,0:T(8,128)(2,1)S(1)}, u32[]{:S(2)}, u32[]{:S(2)}) collective-permute-start(bf16[128,256]{1,0:T(8,128)(2,1)S(1)} %get-tuple-element.74), channel_id=1, source_target_pairs={{0,6},{1,7},{2,4},{3,5},{4,10},{5,11},{6,8},{7,9},{8,14},{9,15},{1... | collective-permute-start | bytes 196616 | tf_op jit(solution)/shard_map/ppermute | solution.py:27
  43.7 4.2 %collective-permute-start.18 = (bf16[128,256]{1,0:T(8,128)(2,1)S(1)}, bf16[128,256]{1,0:T(8,128)(2,1)S(1)}, u32[]{:S(2)}, u32[]{:S(2)}) collective-permute-start(bf16[128,256]{1,0:T(8,128)(2,1)S(1)} %get-tuple-element.70), channel_id=1, source_target_pairs={{0,6},{1,7},{2,4},{3,5},{4,10},{5,11},{6,8},{7,9},{8,14},{9,15},{1... | collective-permute-start | bytes 196616 | tf_op jit(solution)/shard_map/ppermute | solution.py:27
  47.9 2.5 %users.2 = (f32[2048,256]{1,0:T(8,128)S(1)}, bf16[2048,256]{1,0:T(8,128)(2,1)S(1)}) custom-call(f32[2048,256]{1,0:T(8,128)S(1)} %copy-done.1, bf16[128,256]{1,0:T(8,128)(2,1)S(1)} %get-tuple-element.77.refs_0_, bf16[128,256]{1,0:T(8,128)(2,1)S(1)} %collective-permute-done.refs_0_.refs_1_, bf16[128,256]{1,0:T(8,128)(2,1)S(1)} %collective-permute-done.1.refs_0_.refs_2_, ...), custom_call_target="tpu_custom_call" | custom-call | flops 1073741824 | bytes 4194304 | tf_op jit(solution)/shard_map/users/pallas_call | solution.py:142
  50.4 0.2 collective-permute-start.16
  50.6 1.8 %terms_4.3 = (bf16[2048,128]{1,0:T(8,128)(2,1)S(1)}, f32[128,256]{1,0:T(8,128)S(1)}) custom-call(bf16[2048,256]{1,0:T(8,128)(2,1)S(1)} %get-tuple-element.53.users_ref, bf16[8,2048,128]{2,1,0:T(8,128)(2,1)S(1)} %dense_1.1.dense_ref, bf16[128,256]{1,0:T(8,128)(2,1)S(1)} %collective-permute-done.11.refs_0_.refs_2_), custom_call_target="tpu_custom_call" | custom-call | flops 268435456 | bytes 1048576 | tf_op jit(solution)/shard_map/terms_4/pallas_call | solution.py:103
  52.5 1.2 %collective-permute-start.22 = (f32[128,256]{1,0:T(8,128)S(1)}, f32[128,256]{1,0:T(8,128)S(1)}, u32[]{:S(2)}, u32[]{:S(2)}) collective-permute-start(f32[128,256]{1,0:T(8,128)S(1)} %get-tuple-element.65), channel_id=1, source_target_pairs={{0,1},{1,0},{2,3},{3,2},{4,5},{5,4},{6,7},{7,6},{8,9},{9,8},{10,11... | collective-permute-start | bytes 393224 | tf_op jit(solution)/shard_map/ppermute | solution.py:27
  53.6 0.1 collective-permute-start.12
  53.8 1.8 %terms_0.3 = (bf16[2048,128]{1,0:T(8,128)(2,1)S(1)}, f32[128,256]{1,0:T(8,128)S(1)}) custom-call(bf16[2048,256]{1,0:T(8,128)(2,1)S(1)} %get-tuple-element.53.users_ref, bf16[8,2048,128]{2,1,0:T(8,128)(2,1)S(1)} %dense_1.1.dense_ref, bf16[128,256]{1,0:T(8,128)(2,1)S(1)} %collective-permute-done.9.refs_0_), custom_call_target="tpu_custom_call" | custom-call | flops 268435456 | bytes 1048576 | tf_op jit(solution)/shard_map/terms_0/pallas_call | solution.py:103
  55.6 0.4 collective-permute-start.10
  56.1 1.8 %terms_5.3 = (bf16[2048,128]{1,0:T(8,128)(2,1)S(1)}, f32[128,256]{1,0:T(8,128)S(1)}) custom-call(bf16[2048,256]{1,0:T(8,128)(2,1)S(1)} %get-tuple-element.53.users_ref, bf16[8,2048,128]{2,1,0:T(8,128)(2,1)S(1)} %dense_1.1.dense_ref, bf16[128,256]{1,0:T(8,128)(2,1)S(1)} %collective-permute-done.18.refs_0_.refs_6_), custom_call_target="tpu_custom_call" | custom-call | flops 268435456 | bytes 1048576 | tf_op jit(solution)/shard_map/terms_5/pallas_call | solution.py:103
  57.9 0.2 collective-permute-start.19
  58.1 1.8 %terms_1.3 = (bf16[2048,128]{1,0:T(8,128)(2,1)S(1)}, f32[128,256]{1,0:T(8,128)S(1)}) custom-call(bf16[2048,256]{1,0:T(8,128)(2,1)S(1)} %get-tuple-element.53.users_ref, bf16[8,2048,128]{2,1,0:T(8,128)(2,1)S(1)} %dense_1.1.dense_ref, bf16[128,256]{1,0:T(8,128)(2,1)S(1)} %collective-permute-done.16.refs_0_.refs_4_), custom_call_target="tpu_custom_call" | custom-call | flops 268435456 | bytes 1048576 | tf_op jit(solution)/shard_map/terms_1/pallas_call | solution.py:103
  60.0 0.4 collective-permute-start.17
  60.4 1.8 %terms_6.3 = (bf16[2048,128]{1,0:T(8,128)(2,1)S(1)}, f32[128,256]{1,0:T(8,128)S(1)}) custom-call(bf16[2048,256]{1,0:T(8,128)(2,1)S(1)} %get-tuple-element.53.users_ref, bf16[8,2048,128]{2,1,0:T(8,128)(2,1)S(1)} %dense_1.1.dense_ref, bf16[128,256]{1,0:T(8,128)(2,1)S(1)} %collective-permute-done.12.refs_0_.refs_3_), custom_call_target="tpu_custom_call" | custom-call | flops 268435456 | bytes 1048576 | tf_op jit(solution)/shard_map/terms_6/pallas_call | solution.py:103
  62.2 0.2 collective-permute-start.26
  62.5 1.8 %terms_2.3 = (bf16[2048,128]{1,0:T(8,128)(2,1)S(1)}, f32[128,256]{1,0:T(8,128)S(1)}) custom-call(bf16[2048,256]{1,0:T(8,128)(2,1)S(1)} %get-tuple-element.53.users_ref, bf16[8,2048,128]{2,1,0:T(8,128)(2,1)S(1)} %dense_1.1.dense_ref, bf16[128,256]{1,0:T(8,128)(2,1)S(1)} %collective-permute-done.10.refs_0_.refs_1_), custom_call_target="tpu_custom_call" | custom-call | flops 268435456 | bytes 1048576 | tf_op jit(solution)/shard_map/terms_2/pallas_call | solution.py:103
  64.3 0.4 collective-permute-start.21
  64.8 1.0 %collective-permute-start.23 = (f32[128,256]{1,0:T(8,128)S(1)}, f32[128,256]{1,0:T(8,128)S(1)}, u32[]{:S(2)}, u32[]{:S(2)}) collective-permute-start(f32[128,256]{1,0:T(8,128)S(1)} %add.57), channel_id=1, source_target_pairs={{0,3},{1,2},{2,1},{3,0},{4,7},{5,6},{6,5},{7,4},{8,11},{9,10},{10,... | collective-permute-start | bytes 393224 | tf_op jit(solution)/shard_map/ppermute | solution.py:27
  65.8 1.8 %terms_7.3 = (bf16[2048,128]{1,0:T(8,128)(2,1)S(1)}, f32[128,256]{1,0:T(8,128)S(1)}) custom-call(bf16[2048,256]{1,0:T(8,128)(2,1)S(1)} %get-tuple-element.53.users_ref, bf16[8,2048,128]{2,1,0:T(8,128)(2,1)S(1)} %dense_1.1.dense_ref, bf16[128,256]{1,0:T(8,128)(2,1)S(1)} %collective-permute-done.19.refs_0_.refs_7_), custom_call_target="tpu_custom_call" | custom-call | flops 268435456 | bytes 1048576 | tf_op jit(solution)/shard_map/terms_7/pallas_call | solution.py:103
  67.6 3.5 %collective-permute-start.24 = (f32[128,256]{1,0:T(8,128)S(1)}, f32[128,256]{1,0:T(8,128)S(1)}, u32[]{:S(2)}, u32[]{:S(2)}) collective-permute-start(f32[128,256]{1,0:T(8,128)S(1)} %get-tuple-element.71), channel_id=1, source_target_pairs={{0,4},{1,5},{2,6},{3,7},{4,8},{5,9},{6,10},{7,11},{8,12},{9,13},{1... | collective-permute-start | bytes 393224 | tf_op jit(solution)/shard_map/ppermute | solution.py:27
  71.1 1.8 %terms_3.3 = (bf16[2048,128]{1,0:T(8,128)(2,1)S(1)}, f32[128,256]{1,0:T(8,128)S(1)}) custom-call(bf16[2048,256]{1,0:T(8,128)(2,1)S(1)} %get-tuple-element.53.users_ref, bf16[8,2048,128]{2,1,0:T(8,128)(2,1)S(1)} %dense_1.1.dense_ref, bf16[128,256]{1,0:T(8,128)(2,1)S(1)} %collective-permute-done.17.refs_0_.refs_5_), custom_call_target="tpu_custom_call" | custom-call | flops 268435456 | bytes 1048576 | tf_op jit(solution)/shard_map/terms_3/pallas_call | solution.py:103
  72.9 4.4 %users.3 = f32[2048,256]{1,0:T(8,128)} custom-call(f32[2048,256]{1,0:T(8,128)S(1)} %get-tuple-element.44.users_ref, bf16[128,256]{1,0:T(8,128)(2,1)S(1)} %collective-permute-done.9.refs_0_, bf16[128,256]{1,0:T(8,128)(2,1)S(1)} %collective-permute-done.10.refs_0_.refs_1_, bf16[128,256]{1,0:T(8,128)(2,1)S(1)} %collective-permute-done.11.refs_0_.refs_2_, ...), custom_call_target="tpu_custom_call" | custom-call | flops 1073741824 | bytes 4194304 | tf_op jit(solution)/shard_map/users/pallas_call | solution.py:142
  77.4 0.6 collective-permute-start.25
  78.0 1.5 %collective-permute-start.27 = (f32[128,256]{1,0:T(8,128)S(1)}, f32[128,256]{1,0:T(8,128)S(1)}, u32[]{:S(2)}, u32[]{:S(2)}) collective-permute-start(f32[128,256]{1,0:T(8,128)S(1)} %add.61), channel_id=1, source_target_pairs={{0,3},{1,2},{2,1},{3,0},{4,7},{5,6},{6,5},{7,4},{8,11},{9,10},{10,... | collective-permute-start | bytes 393224 | tf_op jit(solution)/shard_map/ppermute | solution.py:27
  79.6 3.7 %collective-permute-done.27 = f32[128,256]{1,0:T(8,128)S(1)} collective-permute-done((f32[128,256]{1,0:T(8,128)S(1)}, f32[128,256]{1,0:T(8,128)S(1)}, u32[]{:S(2)}, u32[]{:S(2)}) %collective-permute-start.27) | collective-permute-done | bytes 131104 | tf_op jit(solution)/shard_map/ppermute | solution.py:27
  83.4 0.7 pad_maximum_fusion
  (45 shorter events, 0.2 us)
Async XLA Ops:
  1.6 11.7 %collective-permute-start.4 = (bf16[128,256]{1,0:T(8,128)(2,1)S(1)}, bf16[128,256]{1,0:T(8,128)(2,1)S(1)}, u32[]{:S(2)}, u32[]{:S(2)}) collective-permute-start(bf16[128,256]{1,0:T(8,128)(2,1)S(1)} %get-tuple-element.76.refs_0_.refs_4_), channel_id=1, source_target_pairs={{0,2},{1,3},{2,0},{3,1},{4,6},{5,7},{6,4},{7,5},{8,10},{9,11},{10,... | collective-permute-start | bytes 196616 | tf_op jit(solution)/shard_map/ppermute | solution.py:27
  2.9 21.0 %collective-permute-start.3 = (bf16[128,256]{1,0:T(8,128)(2,1)S(1)}, bf16[128,256]{1,0:T(8,128)(2,1)S(1)}, u32[]{:S(2)}, u32[]{:S(2)}) collective-permute-start(bf16[128,256]{1,0:T(8,128)(2,1)S(1)} %get-tuple-element.76.refs_0_.refs_4_), channel_id=1, source_target_pairs={{0,1},{1,0},{2,3},{3,2},{4,5},{5,4},{6,7},{7,6},{8,9},{9,8},{10,11... | collective-permute-start | bytes 196616 | tf_op jit(solution)/shard_map/ppermute | solution.py:27
  3.9 13.9 %collective-permute-start.1 = (bf16[128,256]{1,0:T(8,128)(2,1)S(1)}, bf16[128,256]{1,0:T(8,128)(2,1)S(1)}, u32[]{:S(2)}, u32[]{:S(2)}) collective-permute-start(bf16[128,256]{1,0:T(8,128)(2,1)S(1)} %get-tuple-element.77.refs_0_), channel_id=1, source_target_pairs={{0,2},{1,3},{2,0},{3,1},{4,6},{5,7},{6,4},{7,5},{8,10},{9,11},{10,... | collective-permute-start | bytes 196616 | tf_op jit(solution)/shard_map/ppermute | solution.py:27
  4.1 21.8 %collective-permute-start = (bf16[128,256]{1,0:T(8,128)(2,1)S(1)}, bf16[128,256]{1,0:T(8,128)(2,1)S(1)}, u32[]{:S(2)}, u32[]{:S(2)}) collective-permute-start(bf16[128,256]{1,0:T(8,128)(2,1)S(1)} %get-tuple-element.77.refs_0_), channel_id=1, source_target_pairs={{0,1},{1,0},{2,3},{3,2},{4,5},{5,4},{6,7},{7,6},{8,9},{9,8},{10,11... | collective-permute-start | bytes 196616 | tf_op jit(solution)/shard_map/ppermute | solution.py:27
  4.4 3.4 %copy-start = (s32[1,1,2,64,128,128]{5,4,3,2,1,0:T(8,128)S(1)}, s32[1,1,2,64,128,128]{5,4,3,2,1,0:T(8,128)}, u32[]{:S(2)}) copy-start(s32[1,1,2,64,128,128]{5,4,3,2,1,0:T(8,128)} %ratings_ref.3) | copy-start | bytes 25165828
  7.8 0.7 copy-start.2
  8.5 0.7 copy-start.4
  9.1 0.7 copy-start.6
  9.8 3.4 %copy-start.1 = (f32[2048,256]{1,0:T(8,128)S(1)}, f32[2048,256]{1,0:T(8,128)}, u32[]{:S(2)}) copy-start(f32[2048,256]{1,0:T(8,128)} %users_ref.1) | copy-start | bytes 6291460
  15.2 16.9 %collective-permute-start.14 = (f32[128,256]{1,0:T(8,128)S(1)}, f32[128,256]{1,0:T(8,128)S(1)}, u32[]{:S(2)}, u32[]{:S(2)}) collective-permute-start(f32[128,256]{1,0:T(8,128)S(1)} %get-tuple-element.52), channel_id=1, source_target_pairs={{0,1},{1,0},{2,3},{3,2},{4,5},{5,4},{6,7},{7,6},{8,9},{9,8},{10,11... | collective-permute-start | bytes 393224 | tf_op jit(solution)/shard_map/ppermute | solution.py:27
  19.6 12.7 %collective-permute-start.7 = (f32[128,256]{1,0:T(8,128)S(1)}, f32[128,256]{1,0:T(8,128)S(1)}, u32[]{:S(2)}, u32[]{:S(2)}) collective-permute-start(f32[128,256]{1,0:T(8,128)S(1)} %get-tuple-element.48), channel_id=1, source_target_pairs={{0,1},{1,0},{2,3},{3,2},{4,5},{5,4},{6,7},{7,6},{8,9},{9,8},{10,11... | collective-permute-start | bytes 393224 | tf_op jit(solution)/shard_map/ppermute | solution.py:27
  21.5 6.7 %collective-permute-start.5 = (bf16[128,256]{1,0:T(8,128)(2,1)S(1)}, bf16[128,256]{1,0:T(8,128)(2,1)S(1)}, u32[]{:S(2)}, u32[]{:S(2)}) collective-permute-start(bf16[128,256]{1,0:T(8,128)(2,1)S(1)} %collective-permute-done.4.refs_0_.refs_6_), channel_id=1, source_target_pairs={{0,1},{1,0},{2,3},{3,2},{4,5},{5,4},{6,7},{7,6},{8,9},{9,8},{10,11... | collective-permute-start | bytes 196616 | tf_op jit(solution)/shard_map/ppermute | solution.py:27
  23.9 6.3 %collective-permute-start.2 = (bf16[128,256]{1,0:T(8,128)(2,1)S(1)}, bf16[128,256]{1,0:T(8,128)(2,1)S(1)}, u32[]{:S(2)}, u32[]{:S(2)}) collective-permute-start(bf16[128,256]{1,0:T(8,128)(2,1)S(1)} %collective-permute-done.1.refs_0_.refs_2_), channel_id=1, source_target_pairs={{0,1},{1,0},{2,3},{3,2},{4,5},{5,4},{6,7},{7,6},{8,9},{9,8},{10,11... | collective-permute-start | bytes 196616 | tf_op jit(solution)/shard_map/ppermute | solution.py:27
  25.9 15.8 %collective-permute-start.13 = (f32[128,256]{1,0:T(8,128)S(1)}, f32[128,256]{1,0:T(8,128)S(1)}, u32[]{:S(2)}, u32[]{:S(2)}) collective-permute-start(f32[128,256]{1,0:T(8,128)S(1)} %get-tuple-element.50), channel_id=1, source_target_pairs={{0,1},{1,0},{2,3},{3,2},{4,5},{5,4},{6,7},{7,6},{8,9},{9,8},{10,11... | collective-permute-start | bytes 393224 | tf_op jit(solution)/shard_map/ppermute | solution.py:27
  26.4 7.6 %slice-start = ((s8[8388608]{0:T(1024)(128)(4,1)}), s8[4194304]{0:T(1024)(128)(4,1)S(1)}, s32[]{:S(2)}) async-start(s8[8388608]{0:T(1024)(128)(4,1)} %bitcast), calls=%async_computation | async-start | bytes 8388608
  28.3 5.8 %slice-start.1 = ((s8[8388608]{0:T(1024)(128)(4,1)}), s8[4194304]{0:T(1024)(128)(4,1)S(1)}, s32[]{:S(2)}) async-start(s8[8388608]{0:T(1024)(128)(4,1)} %bitcast), calls=%async_computation.1 | async-start | bytes 8388608
  28.3 13.4 %collective-permute-start.6 = (f32[128,256]{1,0:T(8,128)S(1)}, f32[128,256]{1,0:T(8,128)S(1)}, u32[]{:S(2)}, u32[]{:S(2)}) collective-permute-start(f32[128,256]{1,0:T(8,128)S(1)} %get-tuple-element.46), channel_id=1, source_target_pairs={{0,1},{1,0},{2,3},{3,2},{4,5},{5,4},{6,7},{7,6},{8,9},{9,8},{10,11... | collective-permute-start | bytes 393224 | tf_op jit(solution)/shard_map/ppermute | solution.py:27
  30.2 3.8 %copy-start.3 = (s32[1,1,2,64]{3,2,1,0:T(2,128)S(1)}, s32[1,1,2,64]{3,2,1,0:T(2,128)}, u32[]{:S(2)}) copy-start(s32[1,1,2,64]{3,2,1,0:T(2,128)} %rows_ref.3) | copy-start | bytes 1540
  30.2 3.8 %copy-start.5 = (s32[1,1,2,64]{3,2,1,0:T(2,128)S(1)}, s32[1,1,2,64]{3,2,1,0:T(2,128)}, u32[]{:S(2)}) copy-start(s32[1,1,2,64]{3,2,1,0:T(2,128)} %columns_ref.3) | copy-start | bytes 1540
  30.2 3.8 %copy-start.7 = (s32[1,1,2]{2,1,0:T(1,128)S(1)}, s32[1,1,2]{2,1,0:T(1,128)}, u32[]{:S(2)}) copy-start(s32[1,1,2]{2,1,0:T(1,128)} %counts_ref.3) | copy-start | bytes 28
  32.1 9.6 %collective-permute-start.15 = (f32[128,256]{1,0:T(8,128)S(1)}, f32[128,256]{1,0:T(8,128)S(1)}, u32[]{:S(2)}, u32[]{:S(2)}) collective-permute-start(f32[128,256]{1,0:T(8,128)S(1)} %add.53), channel_id=1, source_target_pairs={{0,3},{1,2},{2,1},{3,0},{4,7},{5,6},{6,5},{7,4},{8,11},{9,10},{10,... | collective-permute-start | bytes 393224 | tf_op jit(solution)/shard_map/ppermute | solution.py:27
  32.3 9.4 %copy-start.8 = (f32[256,256]{1,0:T(8,128)S(1)}, f32[256,256]{1,0:T(8,128)}, u32[]{:S(2)}) copy-start(f32[256,256]{1,0:T(8,128)} %param.7) | copy-start | bytes 786436
  32.4 9.4 %collective-permute-start.8 = (f32[128,256]{1,0:T(8,128)S(1)}, f32[128,256]{1,0:T(8,128)S(1)}, u32[]{:S(2)}, u32[]{:S(2)}) collective-permute-start(f32[128,256]{1,0:T(8,128)S(1)} %add.49), channel_id=1, source_target_pairs={{0,3},{1,2},{2,1},{3,0},{4,7},{5,6},{6,5},{7,4},{8,11},{9,10},{10,... | collective-permute-start | bytes 393224 | tf_op jit(solution)/shard_map/ppermute | solution.py:27
  41.8 8.8 %collective-permute-start.11 = (bf16[128,256]{1,0:T(8,128)(2,1)S(1)}, bf16[128,256]{1,0:T(8,128)(2,1)S(1)}, u32[]{:S(2)}, u32[]{:S(2)}) collective-permute-start(bf16[128,256]{1,0:T(8,128)(2,1)S(1)} %get-tuple-element.74), channel_id=1, source_target_pairs={{0,6},{1,7},{2,4},{3,5},{4,10},{5,11},{6,8},{7,9},{8,14},{9,15},{1... | collective-permute-start | bytes 196616 | tf_op jit(solution)/shard_map/ppermute | solution.py:27
  43.7 9.9 %collective-permute-start.9 = (bf16[128,256]{1,0:T(8,128)(2,1)S(1)}, bf16[128,256]{1,0:T(8,128)(2,1)S(1)}, u32[]{:S(2)}, u32[]{:S(2)}) collective-permute-start(bf16[128,256]{1,0:T(8,128)(2,1)S(1)} %get-tuple-element.74), channel_id=1, source_target_pairs={{0,4},{1,5},{2,6},{3,7},{4,8},{5,9},{6,10},{7,11},{8,12},{9,13},{1... | collective-permute-start | bytes 196616 | tf_op jit(solution)/shard_map/ppermute | solution.py:27
  43.7 11.9 %collective-permute-start.18 = (bf16[128,256]{1,0:T(8,128)(2,1)S(1)}, bf16[128,256]{1,0:T(8,128)(2,1)S(1)}, u32[]{:S(2)}, u32[]{:S(2)}) collective-permute-start(bf16[128,256]{1,0:T(8,128)(2,1)S(1)} %get-tuple-element.70), channel_id=1, source_target_pairs={{0,6},{1,7},{2,4},{3,5},{4,10},{5,11},{6,8},{7,9},{8,14},{9,15},{1... | collective-permute-start | bytes 196616 | tf_op jit(solution)/shard_map/ppermute | solution.py:27
  50.4 7.5 %collective-permute-start.16 = (bf16[128,256]{1,0:T(8,128)(2,1)S(1)}, bf16[128,256]{1,0:T(8,128)(2,1)S(1)}, u32[]{:S(2)}, u32[]{:S(2)}) collective-permute-start(bf16[128,256]{1,0:T(8,128)(2,1)S(1)} %get-tuple-element.70), channel_id=1, source_target_pairs={{0,4},{1,5},{2,6},{3,7},{4,8},{5,9},{6,10},{7,11},{8,12},{9,13},{1... | collective-permute-start | bytes 196616 | tf_op jit(solution)/shard_map/ppermute | solution.py:27
  52.5 11.8 %collective-permute-start.22 = (f32[128,256]{1,0:T(8,128)S(1)}, f32[128,256]{1,0:T(8,128)S(1)}, u32[]{:S(2)}, u32[]{:S(2)}) collective-permute-start(f32[128,256]{1,0:T(8,128)S(1)} %get-tuple-element.65), channel_id=1, source_target_pairs={{0,1},{1,0},{2,3},{3,2},{4,5},{5,4},{6,7},{7,6},{8,9},{9,8},{10,11... | collective-permute-start | bytes 393224 | tf_op jit(solution)/shard_map/ppermute | solution.py:27
  53.6 24.4 %collective-permute-start.20 = (f32[128,256]{1,0:T(8,128)S(1)}, f32[128,256]{1,0:T(8,128)S(1)}, u32[]{:S(2)}, u32[]{:S(2)}) collective-permute-start(f32[128,256]{1,0:T(8,128)S(1)} %get-tuple-element.75), channel_id=1, source_target_pairs={{0,4},{1,5},{2,6},{3,7},{4,8},{5,9},{6,10},{7,11},{8,12},{9,13},{1... | collective-permute-start | bytes 393224 | tf_op jit(solution)/shard_map/ppermute | solution.py:27
  53.6 6.3 %collective-permute-start.12 = (bf16[128,256]{1,0:T(8,128)(2,1)S(1)}, bf16[128,256]{1,0:T(8,128)(2,1)S(1)}, u32[]{:S(2)}, u32[]{:S(2)}) collective-permute-start(bf16[128,256]{1,0:T(8,128)(2,1)S(1)} %collective-permute-done.11.refs_0_.refs_2_), channel_id=1, source_target_pairs={{0,1},{1,0},{2,3},{3,2},{4,5},{5,4},{6,7},{7,6},{8,9},{9,8},{10,11... | collective-permute-start | bytes 196616 | tf_op jit(solution)/shard_map/ppermute | solution.py:27
  55.6 6.6 %collective-permute-start.10 = (bf16[128,256]{1,0:T(8,128)(2,1)S(1)}, bf16[128,256]{1,0:T(8,128)(2,1)S(1)}, u32[]{:S(2)}, u32[]{:S(2)}) collective-permute-start(bf16[128,256]{1,0:T(8,128)(2,1)S(1)} %collective-permute-done.9.refs_0_), channel_id=1, source_target_pairs={{0,1},{1,0},{2,3},{3,2},{4,5},{5,4},{6,7},{7,6},{8,9},{9,8},{10,11... | collective-permute-start | bytes 196616 | tf_op jit(solution)/shard_map/ppermute | solution.py:27
  57.9 6.8 %collective-permute-start.19 = (bf16[128,256]{1,0:T(8,128)(2,1)S(1)}, bf16[128,256]{1,0:T(8,128)(2,1)S(1)}, u32[]{:S(2)}, u32[]{:S(2)}) collective-permute-start(bf16[128,256]{1,0:T(8,128)(2,1)S(1)} %collective-permute-done.18.refs_0_.refs_6_), channel_id=1, source_target_pairs={{0,1},{1,0},{2,3},{3,2},{4,5},{5,4},{6,7},{7,6},{8,9},{9,8},{10,11... | collective-permute-start | bytes 196616 | tf_op jit(solution)/shard_map/ppermute | solution.py:27
  60.0 7.6 %collective-permute-start.17 = (bf16[128,256]{1,0:T(8,128)(2,1)S(1)}, bf16[128,256]{1,0:T(8,128)(2,1)S(1)}, u32[]{:S(2)}, u32[]{:S(2)}) collective-permute-start(bf16[128,256]{1,0:T(8,128)(2,1)S(1)} %collective-permute-done.16.refs_0_.refs_4_), channel_id=1, source_target_pairs={{0,1},{1,0},{2,3},{3,2},{4,5},{5,4},{6,7},{7,6},{8,9},{9,8},{10,11... | collective-permute-start | bytes 196616 | tf_op jit(solution)/shard_map/ppermute | solution.py:27
  62.2 15.1 %collective-permute-start.26 = (f32[128,256]{1,0:T(8,128)S(1)}, f32[128,256]{1,0:T(8,128)S(1)}, u32[]{:S(2)}, u32[]{:S(2)}) collective-permute-start(f32[128,256]{1,0:T(8,128)S(1)} %get-tuple-element.69), channel_id=1, source_target_pairs={{0,1},{1,0},{2,3},{3,2},{4,5},{5,4},{6,7},{7,6},{8,9},{9,8},{10,11... | collective-permute-start | bytes 393224 | tf_op jit(solution)/shard_map/ppermute | solution.py:27
  64.3 15.2 %collective-permute-start.21 = (f32[128,256]{1,0:T(8,128)S(1)}, f32[128,256]{1,0:T(8,128)S(1)}, u32[]{:S(2)}, u32[]{:S(2)}) collective-permute-start(f32[128,256]{1,0:T(8,128)S(1)} %get-tuple-element.63), channel_id=1, source_target_pairs={{0,1},{1,0},{2,3},{3,2},{4,5},{5,4},{6,7},{7,6},{8,9},{9,8},{10,11... | collective-permute-start | bytes 393224 | tf_op jit(solution)/shard_map/ppermute | solution.py:27
  64.8 14.8 %collective-permute-start.23 = (f32[128,256]{1,0:T(8,128)S(1)}, f32[128,256]{1,0:T(8,128)S(1)}, u32[]{:S(2)}, u32[]{:S(2)}) collective-permute-start(f32[128,256]{1,0:T(8,128)S(1)} %add.57), channel_id=1, source_target_pairs={{0,3},{1,2},{2,1},{3,0},{4,7},{5,6},{6,5},{7,4},{8,11},{9,10},{10,... | collective-permute-start | bytes 393224 | tf_op jit(solution)/shard_map/ppermute | solution.py:27
  67.6 11.9 %collective-permute-start.24 = (f32[128,256]{1,0:T(8,128)S(1)}, f32[128,256]{1,0:T(8,128)S(1)}, u32[]{:S(2)}, u32[]{:S(2)}) collective-permute-start(f32[128,256]{1,0:T(8,128)S(1)} %get-tuple-element.71), channel_id=1, source_target_pairs={{0,4},{1,5},{2,6},{3,7},{4,8},{5,9},{6,10},{7,11},{8,12},{9,13},{1... | collective-permute-start | bytes 393224 | tf_op jit(solution)/shard_map/ppermute | solution.py:27
  77.4 2.2 %collective-permute-start.25 = (f32[128,256]{1,0:T(8,128)S(1)}, f32[128,256]{1,0:T(8,128)S(1)}, u32[]{:S(2)}, u32[]{:S(2)}) collective-permute-start(f32[128,256]{1,0:T(8,128)S(1)} %get-tuple-element.67), channel_id=1, source_target_pairs={{0,1},{1,0},{2,3},{3,2},{4,5},{5,4},{6,7},{7,6},{8,9},{9,8},{10,11... | collective-permute-start | bytes 393224 | tf_op jit(solution)/shard_map/ppermute | solution.py:27
  78.0 5.3 %collective-permute-start.27 = (f32[128,256]{1,0:T(8,128)S(1)}, f32[128,256]{1,0:T(8,128)S(1)}, u32[]{:S(2)}, u32[]{:S(2)}) collective-permute-start(f32[128,256]{1,0:T(8,128)S(1)} %add.61), channel_id=1, source_target_pairs={{0,3},{1,2},{2,1},{3,0},{4,7},{5,6},{6,5},{7,4},{8,11},{9,10},{10,... | collective-permute-start | bytes 393224 | tf_op jit(solution)/shard_map/ppermute | solution.py:27
where the time goes:
time: 84.9 us; the launch traced here: 84.1 us
  Pallas kernels  47.2 us (56%)
  starting transfers between devices  24.5 us (29%)
  local copies, waits for them, and re-layouts  6.42 us (8%)
  waiting for transfers between devices  3.81 us (4%)
  between operations  1.09 us (1%)
  other arithmetic  1.05 us (1%)
    pallas_call x16, Pallas kernels, terms(): pl.pallas_call(functools.partial(terms_kernel, columns, min(512, user_row...  29.2 us
    ppermute x28, starting transfers between devices, route(): return lax.ppermute(block, ('strata', 'users'), pairs)  24.5 us
    pallas_call x2, Pallas kernels, dense_ratings(): pl.pallas_call(functools.partial(dense_kernel, step, tiles_per_shard), ou...  11 us
    pallas_call x2, Pallas kernels, update_users(): pl.pallas_call(functools.partial(users_kernel, number, low_out), grid=(us...  6.94 us
    unnamed x22, local copies, waits for them, and re-layouts  5.43 us
    ppermute x28, waiting for transfers between devices, route(): return lax.ppermute(block, ('strata', 'users'), pairs)  3.81 us
  transfers between devices with their start and end apart: 28, of which 1 were waited for; matrix products, arithmetic and copies ran while one was open for 0% of the time, Pallas kernels for 56%

commit v1 on v0

--- a/solution.py
+++ b/solution.py
@@ -27,73 +27,97 @@
     return lax.ppermute(block, ("strata", "users"), pairs)
 
 
-def dense_kernel(step, tiles_per_shard, rows_ref, columns_ref, counts_ref, ratings_ref, dense_ref, tiles, arrived):
-    count = counts_ref[0, 0, step]
+def dense_kernel(
+    step, tiles_per_shard, group, counts_hbm, rows_hbm, columns_hbm, ratings_hbm, dense_ref,
+    tiles, counts_ref, rows_ref, columns_ref, arrived, listed,
+):
     flip = lax.axis_index("users") * tiles_per_shard
-    tile = tiles.shape[1]
-
-    def copy(m):
-        return pltpu.make_async_copy(ratings_ref.at[0, 0, step, m], tiles.at[m], arrived.at[m])
-
-    @pl.loop(0, count)
-    def _(m):
-        copy(m).start()
+    lists = [
+        pltpu.make_async_copy(counts_hbm, counts_ref, listed.at[0]),
+        pltpu.make_async_copy(rows_hbm, rows_ref, listed.at[1]),
+        pltpu.make_async_copy(columns_hbm, columns_ref, listed.at[2]),
+    ]
+
+    def rating_copy(g):
+        some = pl.ds(g * group, group)
+        return pltpu.make_async_copy(
+            ratings_hbm.at[0, 0, step, some], tiles.at[some], arrived.at[g]
+        )
+
+    groups = tiles.shape[0] // group
+    for copy in lists:
+        copy.start()
+    for g in range(groups):
+        rating_copy(g).start()
 
     @pl.loop(0, dense_ref.shape[0])
     def _(j):
-        @pl.loop(0, dense_ref.shape[1] // tile)
-        def _(r):
-            dense_ref[j, pl.ds(r * tile, tile), :] = jnp.zeros((tile, tile), BF16)
-
-    @pl.loop(0, count)
-    def _(m):
-        j = columns_ref[0, 0, step, m] ^ flip
-        r = rows_ref[0, 0, step, m]
-        copy(m).wait()
-        dense_ref[j, pl.ds(pl.multiple_of(r * tile, tile), tile), :] = (
-            tiles[m].astype(F32).astype(BF16)
-        )
+        dense_ref[j] = jnp.zeros(dense_ref.shape[1:], BF16)
+
+    for copy in lists:
+        copy.wait()
+    count = counts_ref[0, 0, step]
+
+    @pl.loop(0, groups)
+    def _(g):
+        rating_copy(g).wait()
+
+        @pl.when(g * group < count)
+        def _():
+            for k in range(group):
+                m = g * group + k
+                j = columns_ref[0, 0, step, m] ^ flip
+                r = rows_ref[0, 0, step, m]
+                rating = jnp.where(m < count, tiles[m], 0)
+                dense_ref[j, r] = rating.astype(F32).astype(BF16).T
 
 
 def dense_ratings(step, tiles_per_shard, column_tiles, user_rows, tile_rows, tile_columns, tile_counts, ratings):
     slots, tile = ratings.shape[3], ratings.shape[4]
+    group = 8 if slots % 8 == 0 else 1
+    operands = [
+        pltpu.with_memory_space_constraint(x, pltpu.HBM)
+        for x in (tile_counts, tile_rows, tile_columns, ratings)
+    ]
     return pl.pallas_call(
-        functools.partial(dense_kernel, step, tiles_per_shard),
-        out_shape=jax.ShapeDtypeStruct((column_tiles, user_rows, tile), BF16),
-        in_specs=[SMEM, SMEM, SMEM, ANY],
+        functools.partial(dense_kernel, step, tiles_per_shard, group),
+        out_shape=jax.ShapeDtypeStruct((column_tiles, user_rows // tile, tile, tile), BF16),
+        in_specs=[pl.BlockSpec(memory_space=pltpu.HBM)] * 4,
         out_specs=VMEM,
         scratch_shapes=[
             pltpu.VMEM((slots, tile, tile), jnp.int32),
-            pltpu.SemaphoreType.DMA((slots,)),
+            pltpu.SMEM(tile_counts.shape, jnp.int32),
+            pltpu.SMEM(tile_rows.shape, jnp.int32),
+            pltpu.SMEM(tile_columns.shape, jnp.int32),
+            pltpu.SemaphoreType.DMA((slots // group,)),
+            pltpu.SemaphoreType.DMA((3,)),
         ],
         compiler_params=pltpu.CompilerParams(vmem_limit_bytes=12 * MIB),
         cost_estimate=pl.CostEstimate(flops=2 * 10**9, bytes_accessed=8 * MIB, transcendentals=0),
         name=f"dense_{step}",
-    )(tile_rows, tile_columns, tile_counts, ratings)
-
-
-def terms_kernel(columns, chunk, users_ref, dense_ref, *refs):
+    )(*operands)
+
+
+def terms_kernel(columns, users_ref, dense_ref, *refs):
     number = len(columns)
     item_refs, residual_refs, grad_refs = refs[:number], refs[number : 2 * number], refs[2 * number :]
     tile = item_refs[0].shape[0]
-    items = jnp.concatenate([ref[...] for ref in item_refs], axis=0)
-    for ref in grad_refs:
-        ref[...] = jnp.zeros_like(ref)
-
-    @pl.loop(0, users_ref.shape[0] // chunk)
-    def _(i):
-        rows = pl.ds(pl.multiple_of(i * chunk, chunk), chunk)
-        users = users_ref[rows, :]
-        predicted = lax.dot_general(users, items, BOTH_COLUMNS, preferred_element_type=F32)
-        for k, j in enumerate(columns):
-            rating = dense_ref[j, rows, :].astype(F32)
+    users = users_ref[...]
+    for k, j in enumerate(columns):
+        predicted = lax.dot_general(
+            item_refs[k][...], users, BOTH_COLUMNS, preferred_element_type=F32
+        )
+        residuals = []
+        for r in range(dense_ref.shape[1]):
+            rating = dense_ref[j, r].astype(F32)
             residual = jnp.where(
-                rating > 0, rating - predicted[:, k * tile : (k + 1) * tile], 0.0
+                rating > 0, rating - predicted[:, r * tile : (r + 1) * tile], 0.0
             ).astype(BF16)
-            residual_refs[k][rows, :] = residual
-            grad_refs[k][...] += lax.dot_general(
-                residual, users, BOTH_ROWS, preferred_element_type=F32
-            )
+            residual_refs[k][r] = residual
+            residuals.append(residual)
+        grad_refs[k][...] = jnp.dot(
+            jnp.concatenate(residuals, axis=1), users, preferred_element_type=F32
+        )
 
 
 def terms(columns, users_low, dense, items):
@@ -101,8 +125,8 @@
     tile = items[0].shape[0]
     number = len(columns)
     return pl.pallas_call(
-        functools.partial(terms_kernel, columns, min(512, user_rows)),
-        out_shape=[jax.ShapeDtypeStruct((user_rows, tile), BF16)] * number
+        functools.partial(terms_kernel, columns),
+        out_shape=[jax.ShapeDtypeStruct((user_rows // tile, tile, tile), BF16)] * number
         + [jax.ShapeDtypeStruct((tile, width), F32)] * number,
         in_specs=[VMEM] * (2 + number),
         out_specs=[VMEM] * (2 * number),
@@ -116,36 +140,35 @@
 
 def users_kernel(number, low_out, users_ref, *refs):
     item_refs, residual_refs, outs = refs[:number], refs[number : 2 * number], refs[2 * number :]
-    total = None
-    for k in range(0, number, 2):
-        two = slice(k, k + 2)
-        residual = jnp.concatenate([ref[...] for ref in residual_refs[two]], axis=1)
-        items = jnp.concatenate([ref[...] for ref in item_refs[two]], axis=0)
-        part = jnp.dot(residual, items, preferred_element_type=F32)
-        total = part if total is None else total + part
-    users = users_ref[...]
-    updated = users + 0.01 * (total - 0.05 * users)
-    outs[0][...] = updated
-    if low_out:
-        outs[1][...] = updated.astype(BF16)
+    items = jnp.concatenate([ref[...] for ref in item_refs], axis=0)
+    tile = item_refs[0].shape[0]
+    for r in range(residual_refs[0].shape[0]):
+        residual = jnp.concatenate([ref[r] for ref in residual_refs], axis=0)
+        total = lax.dot_general(residual, items, BOTH_ROWS, preferred_element_type=F32)
+        rows = slice(r * tile, (r + 1) * tile)
+        users = users_ref[rows, :]
+        updated = users + 0.01 * (total - 0.05 * users)
+        outs[0][rows, :] = updated
+        if low_out:
+            outs[1][rows, :] = updated.astype(BF16)
 
 
 def update_users(users, items, residuals, low_out):
     user_rows, width = users.shape
     number = len(items)
     tile = items[0].shape[0]
-    chunk = min(256, user_rows)
-    block = pl.BlockSpec((chunk, width), lambda i: (i, 0))
+    group = 2
+    block = pl.BlockSpec((group * tile, width), lambda i: (i, 0))
     out_types = [jax.ShapeDtypeStruct(users.shape, F32)]
     if low_out:
         out_types.append(jax.ShapeDtypeStruct(users.shape, BF16))
     return pl.pallas_call(
         functools.partial(users_kernel, number, low_out),
-        grid=(user_rows // chunk,),
+        grid=(user_rows // (group * tile),),
         out_shape=out_types,
         in_specs=[block]
         + [pl.BlockSpec((tile, width), lambda i: (0, 0))] * number
-        + [pl.BlockSpec((chunk, tile), lambda i: (i, 0))] * number,
+        + [pl.BlockSpec((group, tile, tile), lambda i: (i, 0, 0))] * number,
         out_specs=[block] * len(out_types),
         compiler_params=pltpu.CompilerParams(vmem_limit_bytes=12 * MIB),
         cost_estimate=pl.CostEstimate(

time: 84.9 us -> 57.9 us (0.68)
  the two profiles are of different devices: /device:TPU:17 before, /device:TPU:0 now
where the time goes in v1:
time: 57.9 us; the launch traced here: 57.8 us
  Pallas kernels  24 us (41%)
  starting transfers between devices  20.9 us (36%)
  waiting for transfers between devices  9.92 us (17%)
  other arithmetic  1.05 us (2%)
  local copies, waits for them, and re-layouts  1 us (2%)
  between operations  0.91 us (2%)
    ppermute x28, starting transfers between devices, route(): return lax.ppermute(block, ('strata', 'users'), pairs)  20.9 us
    pallas_call x16, Pallas kernels, terms(): pl.pallas_call(functools.partial(terms_kernel, columns), out_shape=[jax.S...  11.7 us
    ppermute x28, waiting for transfers between devices, route(): return lax.ppermute(block, ('strata', 'users'), pairs)  9.92 us
    pallas_call x2, Pallas kernels, update_users(): pl.pallas_call(functools.partial(users_kernel, number, low_out), grid=(us...  7.64 us
    pallas_call x2, Pallas kernels, dense_ratings(): pl.pallas_call(functools.partial(dense_kernel, step, tiles_per_shard, gro...  4.6 us
  transfers between devices with their start and end apart: 28, of which 6 were waited for; matrix products, arithmetic and copies ran while one was open for 0% of the time, Pallas kernels for 41%

profile of v1, /device:TPU:0, one launch (start us, length us, event | category | flops | bytes accessed | tf_op | source)
XLA Modules:
  0.0 57.8 jit_solution(8782946135758852971)
XLA Ops:
  0.6 1.0 %fusion.2 = (bf16[128,256]{1,0:T(8,128)(2,1)S(1)}, bf16[128,256]{1,0:T(8,128)(2,1)S(1)}) fusion(f32[256,256]{1,0:T(8,128)} %param.7), kind=kLoop, calls=%fused_computation.9 | loop fusion | bytes 262144 | tf_op jit(solution)/shard_map/slice | solution.py:190
  1.6 3.1 %collective-permute-start.4 = (bf16[128,256]{1,0:T(8,128)(2,1)S(1)}, bf16[128,256]{1,0:T(8,128)(2,1)S(1)}, u32[]{:S(2)}, u32[]{:S(2)}) collective-permute-start(bf16[128,256]{1,0:T(8,128)(2,1)S(1)} %get-tuple-element.76.refs_0_.refs_4_), channel_id=1, source_target_pairs={{0,2},{1,3},{2,0},{3,1},{4,6},{5,7},{6,4},{7,5},{8,10},{9,11},{10,... | collective-permute-start | bytes 196616 | tf_op jit(solution)/shard_map/ppermute | solution.py:27
  4.7 0.2 collective-permute-start.1
  4.8 0.3 collective-permute-start
  5.2 2.4 %dense_0.1.dense_ref = bf16[8,16,128,128]{3,2,1,0:T(8,128)(2,1)S(1)} custom-call(s32[1,1,2]{2,1,0:T(1,128)} %counts_hbm.3, s32[1,1,2,64]{3,2,1,0:T(2,128)} %rows_hbm.3, s32[1,1,2,64]{3,2,1,0:T(2,128)} %columns_hbm.3, s32[1,1,2,64,128,128]{5,4,3,2,1,0:T(8,128)} %ratings_hbm.3), custom_call_target="tpu_custom_call" | custom-call | flops 2000000000 | bytes 8388608 | tf_op jit(solution)/shard_map/dense_0/pallas_call | solution.py:82
  7.6 0.1 convert_element_type.17.users_ref
  7.7 0.7 %terms_5.2 = (bf16[16,128,128]{2,1,0:T(8,128)(2,1)S(1)}, f32[128,256]{1,0:T(8,128)S(1)}) custom-call(bf16[2048,256]{1,0:T(8,128)(2,1)S(1)} %convert_element_type.17.users_ref, bf16[8,16,128,128]{3,2,1,0:T(8,128)(2,1)S(1)} %dense_0.1.dense_ref, bf16[128,256]{1,0:T(8,128)(2,1)S(1)} %collective-permute-done.4.refs_0_.refs_6_), custom_call_target="tpu_custom_call" | custom-call | flops 268435456 | bytes 1048576 | tf_op jit(solution)/shard_map/terms_5/pallas_call | solution.py:127
  8.4 0.5 collective-permute-start.14
  9.0 0.2 collective-permute-done.1.refs_0_.refs_2_
  9.2 0.7 %terms_4.2 = (bf16[16,128,128]{2,1,0:T(8,128)(2,1)S(1)}, f32[128,256]{1,0:T(8,128)S(1)}) custom-call(bf16[2048,256]{1,0:T(8,128)(2,1)S(1)} %convert_element_type.17.users_ref, bf16[8,16,128,128]{3,2,1,0:T(8,128)(2,1)S(1)} %dense_0.1.dense_ref, bf16[128,256]{1,0:T(8,128)(2,1)S(1)} %collective-permute-done.1.refs_0_.refs_2_), custom_call_target="tpu_custom_call" | custom-call | flops 268435456 | bytes 1048576 | tf_op jit(solution)/shard_map/terms_4/pallas_call | solution.py:127
  9.9 0.1 collective-permute-start.7
  10.0 0.7 %terms_0.2 = (bf16[16,128,128]{2,1,0:T(8,128)(2,1)S(1)}, f32[128,256]{1,0:T(8,128)S(1)}) custom-call(bf16[2048,256]{1,0:T(8,128)(2,1)S(1)} %convert_element_type.17.users_ref, bf16[8,16,128,128]{3,2,1,0:T(8,128)(2,1)S(1)} %dense_0.1.dense_ref, bf16[128,256]{1,0:T(8,128)(2,1)S(1)} %get-tuple-element.77.refs_0_), custom_call_target="tpu_custom_call" | custom-call | flops 268435456 | bytes 1048576 | tf_op jit(solution)/shard_map/terms_0/pallas_call | solution.py:127
  10.8 0.6 collective-permute-start.5
  11.3 0.7 %terms_1.2 = (bf16[16,128,128]{2,1,0:T(8,128)(2,1)S(1)}, f32[128,256]{1,0:T(8,128)S(1)}) custom-call(bf16[2048,256]{1,0:T(8,128)(2,1)S(1)} %convert_element_type.17.users_ref, bf16[8,16,128,128]{3,2,1,0:T(8,128)(2,1)S(1)} %dense_0.1.dense_ref, bf16[128,256]{1,0:T(8,128)(2,1)S(1)} %get-tuple-element.76.refs_0_.refs_4_), custom_call_target="tpu_custom_call" | custom-call | flops 268435456 | bytes 1048576 | tf_op jit(solution)/shard_map/terms_1/pallas_call | solution.py:127
  12.1 0.1 collective-permute-start.2
  12.1 0.7 %terms_3.2 = (bf16[16,128,128]{2,1,0:T(8,128)(2,1)S(1)}, f32[128,256]{1,0:T(8,128)S(1)}) custom-call(bf16[2048,256]{1,0:T(8,128)(2,1)S(1)} %convert_element_type.17.users_ref, bf16[8,16,128,128]{3,2,1,0:T(8,128)(2,1)S(1)} %dense_0.1.dense_ref, bf16[128,256]{1,0:T(8,128)(2,1)S(1)} %collective-permute-done.3.refs_0_.refs_5_), custom_call_target="tpu_custom_call" | custom-call | flops 268435456 | bytes 1048576 | tf_op jit(solution)/shard_map/terms_3/pallas_call | solution.py:127
  12.9 0.0 collective-permute-done.refs_0_.refs_1_
  12.9 0.6 collective-permute-start.13
  13.5 0.7 %terms_2.2 = (bf16[16,128,128]{2,1,0:T(8,128)(2,1)S(1)}, f32[128,256]{1,0:T(8,128)S(1)}) custom-call(bf16[2048,256]{1,0:T(8,128)(2,1)S(1)} %convert_element_type.17.users_ref, bf16[8,16,128,128]{3,2,1,0:T(8,128)(2,1)S(1)} %dense_0.1.dense_ref, bf16[128,256]{1,0:T(8,128)(2,1)S(1)} %collective-permute-done.refs_0_.refs_1_), custom_call_target="tpu_custom_call" | custom-call | flops 268435456 | bytes 1048576 | tf_op jit(solution)/shard_map/terms_2/pallas_call | solution.py:127
  14.2 0.0 collective-permute-done.5.refs_0_.refs_7_
  14.2 0.1 collective-permute-start.6
  14.3 0.7 %terms_7.2 = (bf16[16,128,128]{2,1,0:T(8,128)(2,1)S(1)}, f32[128,256]{1,0:T(8,128)S(1)}) custom-call(bf16[2048,256]{1,0:T(8,128)(2,1)S(1)} %convert_element_type.17.users_ref, bf16[8,16,128,128]{3,2,1,0:T(8,128)(2,1)S(1)} %dense_0.1.dense_ref, bf16[128,256]{1,0:T(8,128)(2,1)S(1)} %collective-permute-done.5.refs_0_.refs_7_), custom_call_target="tpu_custom_call" | custom-call | flops 268435456 | bytes 1048576 | tf_op jit(solution)/shard_map/terms_7/pallas_call | solution.py:127
  15.0 0.7 %terms_6.2 = (bf16[16,128,128]{2,1,0:T(8,128)(2,1)S(1)}, f32[128,256]{1,0:T(8,128)S(1)}) custom-call(bf16[2048,256]{1,0:T(8,128)(2,1)S(1)} %convert_element_type.17.users_ref, bf16[8,16,128,128]{3,2,1,0:T(8,128)(2,1)S(1)} %dense_0.1.dense_ref, bf16[128,256]{1,0:T(8,128)(2,1)S(1)} %collective-permute-done.2.refs_0_.refs_3_), custom_call_target="tpu_custom_call" | custom-call | flops 268435456 | bytes 1048576 | tf_op jit(solution)/shard_map/terms_6/pallas_call | solution.py:127
  15.8 0.0 collective-permute-done.14
  15.8 1.4 %collective-permute-start.15 = (f32[128,256]{1,0:T(8,128)S(1)}, f32[128,256]{1,0:T(8,128)S(1)}, u32[]{:S(2)}, u32[]{:S(2)}) collective-permute-start(f32[128,256]{1,0:T(8,128)S(1)} %add.53), channel_id=1, source_target_pairs={{0,3},{1,2},{2,1},{3,0},{4,7},{5,6},{6,5},{7,4},{8,11},{9,10},{10,... | collective-permute-start | bytes 393224 | tf_op jit(solution)/shard_map/ppermute | solution.py:27
  17.2 0.0 copy-start.1
  17.2 0.5 collective-permute-start.8
  17.7 2.2 %dense_1.1.dense_ref = bf16[8,16,128,128]{3,2,1,0:T(8,128)(2,1)S(1)} custom-call(s32[1,1,2]{2,1,0:T(1,128)} %counts_hbm.3, s32[1,1,2,64]{3,2,1,0:T(2,128)} %rows_hbm.3, s32[1,1,2,64]{3,2,1,0:T(2,128)} %columns_hbm.3, s32[1,1,2,64,128,128]{5,4,3,2,1,0:T(8,128)} %ratings_hbm.3), custom_call_target="tpu_custom_call" | custom-call | flops 2000000000 | bytes 8388608 | tf_op jit(solution)/shard_map/dense_1/pallas_call | solution.py:82
  20.0 0.0 collective-permute-done.13
  20.0 1.1 %collective-permute-done.15 = f32[128,256]{1,0:T(8,128)S(1)} collective-permute-done((f32[128,256]{1,0:T(8,128)S(1)}, f32[128,256]{1,0:T(8,128)S(1)}, u32[]{:S(2)}, u32[]{:S(2)}) %collective-permute-start.15) | collective-permute-done | bytes 131104 | tf_op jit(solution)/shard_map/ppermute | solution.py:27
  21.1 2.7 %collective-permute-done.8 = f32[128,256]{1,0:T(8,128)S(1)} collective-permute-done((f32[128,256]{1,0:T(8,128)S(1)}, f32[128,256]{1,0:T(8,128)S(1)}, u32[]{:S(2)}, u32[]{:S(2)}) %collective-permute-start.8) | collective-permute-done | bytes 131104 | tf_op jit(solution)/shard_map/ppermute | solution.py:27
  23.8 0.1 fusion
  23.9 3.1 %collective-permute-start.11 = (bf16[128,256]{1,0:T(8,128)(2,1)S(1)}, bf16[128,256]{1,0:T(8,128)(2,1)S(1)}, u32[]{:S(2)}, u32[]{:S(2)}) collective-permute-start(bf16[128,256]{1,0:T(8,128)(2,1)S(1)} %get-tuple-element.74), channel_id=1, source_target_pairs={{0,6},{1,7},{2,4},{3,5},{4,10},{5,11},{6,8},{7,9},{8,14},{9,15},{1... | collective-permute-start | bytes 196616 | tf_op jit(solution)/shard_map/ppermute | solution.py:27
  27.0 1.6 %collective-permute-start.9 = (bf16[128,256]{1,0:T(8,128)(2,1)S(1)}, bf16[128,256]{1,0:T(8,128)(2,1)S(1)}, u32[]{:S(2)}, u32[]{:S(2)}) collective-permute-start(bf16[128,256]{1,0:T(8,128)(2,1)S(1)} %get-tuple-element.74), channel_id=1, source_target_pairs={{0,4},{1,5},{2,6},{3,7},{4,8},{5,9},{6,10},{7,11},{8,12},{9,13},{1... | collective-permute-start | bytes 196616 | tf_op jit(solution)/shard_map/ppermute | solution.py:27
  28.6 0.8 %collective-permute-start.18 = (bf16[128,256]{1,0:T(8,128)(2,1)S(1)}, bf16[128,256]{1,0:T(8,128)(2,1)S(1)}, u32[]{:S(2)}, u32[]{:S(2)}) collective-permute-start(bf16[128,256]{1,0:T(8,128)(2,1)S(1)} %get-tuple-element.70), channel_id=1, source_target_pairs={{0,6},{1,7},{2,4},{3,5},{4,10},{5,11},{6,8},{7,9},{8,14},{9,15},{1... | collective-permute-start | bytes 196616 | tf_op jit(solution)/shard_map/ppermute | solution.py:27
  29.4 3.0 %users.2 = (f32[2048,256]{1,0:T(8,128)S(1)}, bf16[2048,256]{1,0:T(8,128)(2,1)S(1)}) custom-call(f32[2048,256]{1,0:T(8,128)S(1)} %copy-done, bf16[128,256]{1,0:T(8,128)(2,1)S(1)} %get-tuple-element.77.refs_0_, bf16[128,256]{1,0:T(8,128)(2,1)S(1)} %collective-permute-done.refs_0_.refs_1_, bf16[128,256]{1,0:T(8,128)(2,1)S(1)} %collective-permute-done.1.refs_0_.refs_2_, ...), custom_call_target="tpu_custom_call" | custom-call | flops 1073741824 | bytes 4194304 | tf_op jit(solution)/shard_map/users/pallas_call | solution.py:165
  32.4 1.6 %collective-permute-start.16 = (bf16[128,256]{1,0:T(8,128)(2,1)S(1)}, bf16[128,256]{1,0:T(8,128)(2,1)S(1)}, u32[]{:S(2)}, u32[]{:S(2)}) collective-permute-start(bf16[128,256]{1,0:T(8,128)(2,1)S(1)} %get-tuple-element.70), channel_id=1, source_target_pairs={{0,4},{1,5},{2,6},{3,7},{4,8},{5,9},{6,10},{7,11},{8,12},{9,13},{1... | collective-permute-start | bytes 196616 | tf_op jit(solution)/shard_map/ppermute | solution.py:27
  34.0 0.0 collective-permute-done.11.refs_0_.refs_2_
  34.0 0.7 %terms_4.3 = (bf16[16,128,128]{2,1,0:T(8,128)(2,1)S(1)}, f32[128,256]{1,0:T(8,128)S(1)}) custom-call(bf16[2048,256]{1,0:T(8,128)(2,1)S(1)} %get-tuple-element.53.users_ref, bf16[8,16,128,128]{3,2,1,0:T(8,128)(2,1)S(1)} %dense_1.1.dense_ref, bf16[128,256]{1,0:T(8,128)(2,1)S(1)} %collective-permute-done.11.refs_0_.refs_2_), custom_call_target="tpu_custom_call" | custom-call | flops 268435456 | bytes 1048576 | tf_op jit(solution)/shard_map/terms_4/pallas_call | solution.py:127
  34.7 0.1 collective-permute-start.22
  34.8 1.6 %collective-permute-start.20 = (f32[128,256]{1,0:T(8,128)S(1)}, f32[128,256]{1,0:T(8,128)S(1)}, u32[]{:S(2)}, u32[]{:S(2)}) collective-permute-start(f32[128,256]{1,0:T(8,128)S(1)} %get-tuple-element.75), channel_id=1, source_target_pairs={{0,4},{1,5},{2,6},{3,7},{4,8},{5,9},{6,10},{7,11},{8,12},{9,13},{1... | collective-permute-start | bytes 393224 | tf_op jit(solution)/shard_map/ppermute | solution.py:27
  36.3 0.2 collective-permute-start.12
  36.5 0.7 %terms_0.3 = (bf16[16,128,128]{2,1,0:T(8,128)(2,1)S(1)}, f32[128,256]{1,0:T(8,128)S(1)}) custom-call(bf16[2048,256]{1,0:T(8,128)(2,1)S(1)} %get-tuple-element.53.users_ref, bf16[8,16,128,128]{3,2,1,0:T(8,128)(2,1)S(1)} %dense_1.1.dense_ref, bf16[128,256]{1,0:T(8,128)(2,1)S(1)} %collective-permute-done.9.refs_0_), custom_call_target="tpu_custom_call" | custom-call | flops 268435456 | bytes 1048576 | tf_op jit(solution)/shard_map/terms_0/pallas_call | solution.py:127
  37.2 0.4 collective-permute-start.10
  37.6 0.7 %terms_5.3 = (bf16[16,128,128]{2,1,0:T(8,128)(2,1)S(1)}, f32[128,256]{1,0:T(8,128)S(1)}) custom-call(bf16[2048,256]{1,0:T(8,128)(2,1)S(1)} %get-tuple-element.53.users_ref, bf16[8,16,128,128]{3,2,1,0:T(8,128)(2,1)S(1)} %dense_1.1.dense_ref, bf16[128,256]{1,0:T(8,128)(2,1)S(1)} %collective-permute-done.18.refs_0_.refs_6_), custom_call_target="tpu_custom_call" | custom-call | flops 268435456 | bytes 1048576 | tf_op jit(solution)/shard_map/terms_5/pallas_call | solution.py:127
  38.4 1.0 %collective-permute-done.16.refs_0_.refs_4_ = bf16[128,256]{1,0:T(8,128)(2,1)S(1)} collective-permute-done((bf16[128,256]{1,0:T(8,128)(2,1)S(1)}, bf16[128,256]{1,0:T(8,128)(2,1)S(1)}, u32[]{:S(2)}, u32[]{:S(2)}) %collective-permute-start.16) | collective-permute-done | bytes 65568 | tf_op jit(solution)/shard_map/ppermute | solution.py:27
  39.4 0.0 collective-permute-start.19
  39.4 0.7 %terms_1.3 = (bf16[16,128,128]{2,1,0:T(8,128)(2,1)S(1)}, f32[128,256]{1,0:T(8,128)S(1)}) custom-call(bf16[2048,256]{1,0:T(8,128)(2,1)S(1)} %get-tuple-element.53.users_ref, bf16[8,16,128,128]{3,2,1,0:T(8,128)(2,1)S(1)} %dense_1.1.dense_ref, bf16[128,256]{1,0:T(8,128)(2,1)S(1)} %collective-permute-done.16.refs_0_.refs_4_), custom_call_target="tpu_custom_call" | custom-call | flops 268435456 | bytes 1048576 | tf_op jit(solution)/shard_map/terms_1/pallas_call | solution.py:127
  40.1 0.6 collective-permute-start.17
  40.7 0.7 %terms_6.3 = (bf16[16,128,128]{2,1,0:T(8,128)(2,1)S(1)}, f32[128,256]{1,0:T(8,128)S(1)}) custom-call(bf16[2048,256]{1,0:T(8,128)(2,1)S(1)} %get-tuple-element.53.users_ref, bf16[8,16,128,128]{3,2,1,0:T(8,128)(2,1)S(1)} %dense_1.1.dense_ref, bf16[128,256]{1,0:T(8,128)(2,1)S(1)} %collective-permute-done.12.refs_0_.refs_3_), custom_call_target="tpu_custom_call" | custom-call | flops 268435456 | bytes 1048576 | tf_op jit(solution)/shard_map/terms_6/pallas_call | solution.py:127
  41.4 0.0 collective-permute-done.10.refs_0_.refs_1_
  41.4 0.1 collective-permute-start.26
  41.5 0.7 %terms_2.3 = (bf16[16,128,128]{2,1,0:T(8,128)(2,1)S(1)}, f32[128,256]{1,0:T(8,128)S(1)}) custom-call(bf16[2048,256]{1,0:T(8,128)(2,1)S(1)} %get-tuple-element.53.users_ref, bf16[8,16,128,128]{3,2,1,0:T(8,128)(2,1)S(1)} %dense_1.1.dense_ref, bf16[128,256]{1,0:T(8,128)(2,1)S(1)} %collective-permute-done.10.refs_0_.refs_1_), custom_call_target="tpu_custom_call" | custom-call | flops 268435456 | bytes 1048576 | tf_op jit(solution)/shard_map/terms_2/pallas_call | solution.py:127
  42.3 0.6 collective-permute-start.21
  42.9 1.7 %collective-permute-start.23 = (f32[128,256]{1,0:T(8,128)S(1)}, f32[128,256]{1,0:T(8,128)S(1)}, u32[]{:S(2)}, u32[]{:S(2)}) collective-permute-start(f32[128,256]{1,0:T(8,128)S(1)} %add.57), channel_id=1, source_target_pairs={{0,3},{1,2},{2,1},{3,0},{4,7},{5,6},{6,5},{7,4},{8,11},{9,10},{10,... | collective-permute-start | bytes 393224 | tf_op jit(solution)/shard_map/ppermute | solution.py:27
  44.6 0.7 %terms_7.3 = (bf16[16,128,128]{2,1,0:T(8,128)(2,1)S(1)}, f32[128,256]{1,0:T(8,128)S(1)}) custom-call(bf16[2048,256]{1,0:T(8,128)(2,1)S(1)} %get-tuple-element.53.users_ref, bf16[8,16,128,128]{3,2,1,0:T(8,128)(2,1)S(1)} %dense_1.1.dense_ref, bf16[128,256]{1,0:T(8,128)(2,1)S(1)} %collective-permute-done.19.refs_0_.refs_7_), custom_call_target="tpu_custom_call" | custom-call | flops 268435456 | bytes 1048576 | tf_op jit(solution)/shard_map/terms_7/pallas_call | solution.py:127
  45.3 0.9 %collective-permute-start.24 = (f32[128,256]{1,0:T(8,128)S(1)}, f32[128,256]{1,0:T(8,128)S(1)}, u32[]{:S(2)}, u32[]{:S(2)}) collective-permute-start(f32[128,256]{1,0:T(8,128)S(1)} %get-tuple-element.71), channel_id=1, source_target_pairs={{0,4},{1,5},{2,6},{3,7},{4,8},{5,9},{6,10},{7,11},{8,12},{9,13},{1... | collective-permute-start | bytes 393224 | tf_op jit(solution)/shard_map/ppermute | solution.py:27
  46.3 0.7 %terms_3.3 = (bf16[16,128,128]{2,1,0:T(8,128)(2,1)S(1)}, f32[128,256]{1,0:T(8,128)S(1)}) custom-call(bf16[2048,256]{1,0:T(8,128)(2,1)S(1)} %get-tuple-element.53.users_ref, bf16[8,16,128,128]{3,2,1,0:T(8,128)(2,1)S(1)} %dense_1.1.dense_ref, bf16[128,256]{1,0:T(8,128)(2,1)S(1)} %collective-permute-done.17.refs_0_.refs_5_), custom_call_target="tpu_custom_call" | custom-call | flops 268435456 | bytes 1048576 | tf_op jit(solution)/shard_map/terms_3/pallas_call | solution.py:127
  47.0 4.7 %users.3 = f32[2048,256]{1,0:T(8,128)} custom-call(f32[2048,256]{1,0:T(8,128)S(1)} %get-tuple-element.44.users_ref, bf16[128,256]{1,0:T(8,128)(2,1)S(1)} %collective-permute-done.9.refs_0_, bf16[128,256]{1,0:T(8,128)(2,1)S(1)} %collective-permute-done.10.refs_0_.refs_1_, bf16[128,256]{1,0:T(8,128)(2,1)S(1)} %collective-permute-done.11.refs_0_.refs_2_, ...), custom_call_target="tpu_custom_call" | custom-call | flops 1073741824 | bytes 4194304 | tf_op jit(solution)/shard_map/users/pallas_call | solution.py:165
  51.7 0.1 collective-permute-start.25
  51.8 0.4 collective-permute-start.27
  52.2 1.8 %collective-permute-done.24 = f32[128,256]{1,0:T(8,128)S(1)} collective-permute-done((f32[128,256]{1,0:T(8,128)S(1)}, f32[128,256]{1,0:T(8,128)S(1)}, u32[]{:S(2)}, u32[]{:S(2)}) %collective-permute-start.24) | collective-permute-done | bytes 131104 | tf_op jit(solution)/shard_map/ppermute | solution.py:27
  54.0 3.0 %collective-permute-done.27 = f32[128,256]{1,0:T(8,128)S(1)} collective-permute-done((f32[128,256]{1,0:T(8,128)S(1)}, f32[128,256]{1,0:T(8,128)S(1)}, u32[]{:S(2)}, u32[]{:S(2)}) %collective-permute-start.27) | collective-permute-done | bytes 131104 | tf_op jit(solution)/shard_map/ppermute | solution.py:27
  57.1 0.7 %pad_maximum_fusion = f32[256,256]{1,0:T(8,128)} fusion(f32[128,256]{1,0:T(8,128)S(1)} %multiply_add_fusion, f32[128,256]{1,0:T(8,128)S(1)} %multiply_add_fusion.1), kind=kLoop, calls=%fused_computation | loop fusion | flops 65536 | bytes 524288 | tf_op jit(solution)/shard_map/concatenate | solution.py:227
  (26 shorter events, 0.2 us)
Async XLA Ops:
  1.6 6.1 %collective-permute-start.4 = (bf16[128,256]{1,0:T(8,128)(2,1)S(1)}, bf16[128,256]{1,0:T(8,128)(2,1)S(1)}, u32[]{:S(2)}, u32[]{:S(2)}) collective-permute-start(bf16[128,256]{1,0:T(8,128)(2,1)S(1)} %get-tuple-element.76.refs_0_.refs_4_), channel_id=1, source_target_pairs={{0,2},{1,3},{2,0},{3,1},{4,6},{5,7},{6,4},{7,5},{8,10},{9,11},{10,... | collective-permute-start | bytes 196616 | tf_op jit(solution)/shard_map/ppermute | solution.py:27
  4.7 7.4 %collective-permute-start.3 = (bf16[128,256]{1,0:T(8,128)(2,1)S(1)}, bf16[128,256]{1,0:T(8,128)(2,1)S(1)}, u32[]{:S(2)}, u32[]{:S(2)}) collective-permute-start(bf16[128,256]{1,0:T(8,128)(2,1)S(1)} %get-tuple-element.76.refs_0_.refs_4_), channel_id=1, source_target_pairs={{0,1},{1,0},{2,3},{3,2},{4,5},{5,4},{6,7},{7,6},{8,9},{9,8},{10,11... | collective-permute-start | bytes 196616 | tf_op jit(solution)/shard_map/ppermute | solution.py:27
  4.7 2.9 %copy-start = (f32[2048,256]{1,0:T(8,128)S(1)}, f32[2048,256]{1,0:T(8,128)}, u32[]{:S(2)}) copy-start(f32[2048,256]{1,0:T(8,128)} %users_ref.1) | copy-start | bytes 6291460
  4.7 4.5 %collective-permute-start.1 = (bf16[128,256]{1,0:T(8,128)(2,1)S(1)}, bf16[128,256]{1,0:T(8,128)(2,1)S(1)}, u32[]{:S(2)}, u32[]{:S(2)}) collective-permute-start(bf16[128,256]{1,0:T(8,128)(2,1)S(1)} %get-tuple-element.77.refs_0_), channel_id=1, source_target_pairs={{0,2},{1,3},{2,0},{3,1},{4,6},{5,7},{6,4},{7,5},{8,10},{9,11},{10,... | collective-permute-start | bytes 196616 | tf_op jit(solution)/shard_map/ppermute | solution.py:27
  4.8 8.0 %collective-permute-start = (bf16[128,256]{1,0:T(8,128)(2,1)S(1)}, bf16[128,256]{1,0:T(8,128)(2,1)S(1)}, u32[]{:S(2)}, u32[]{:S(2)}) collective-permute-start(bf16[128,256]{1,0:T(8,128)(2,1)S(1)} %get-tuple-element.77.refs_0_), channel_id=1, source_target_pairs={{0,1},{1,0},{2,3},{3,2},{4,5},{5,4},{6,7},{7,6},{8,9},{9,8},{10,11... | collective-permute-start | bytes 196616 | tf_op jit(solution)/shard_map/ppermute | solution.py:27
  8.4 7.4 %collective-permute-start.14 = (f32[128,256]{1,0:T(8,128)S(1)}, f32[128,256]{1,0:T(8,128)S(1)}, u32[]{:S(2)}, u32[]{:S(2)}) collective-permute-start(f32[128,256]{1,0:T(8,128)S(1)} %get-tuple-element.52), channel_id=1, source_target_pairs={{0,1},{1,0},{2,3},{3,2},{4,5},{5,4},{6,7},{7,6},{8,9},{9,8},{10,11... | collective-permute-start | bytes 393224 | tf_op jit(solution)/shard_map/ppermute | solution.py:27
  9.9 7.3 %collective-permute-start.7 = (f32[128,256]{1,0:T(8,128)S(1)}, f32[128,256]{1,0:T(8,128)S(1)}, u32[]{:S(2)}, u32[]{:S(2)}) collective-permute-start(f32[128,256]{1,0:T(8,128)S(1)} %get-tuple-element.48), channel_id=1, source_target_pairs={{0,1},{1,0},{2,3},{3,2},{4,5},{5,4},{6,7},{7,6},{8,9},{9,8},{10,11... | collective-permute-start | bytes 393224 | tf_op jit(solution)/shard_map/ppermute | solution.py:27
  10.8 3.4 %collective-permute-start.5 = (bf16[128,256]{1,0:T(8,128)(2,1)S(1)}, bf16[128,256]{1,0:T(8,128)(2,1)S(1)}, u32[]{:S(2)}, u32[]{:S(2)}) collective-permute-start(bf16[128,256]{1,0:T(8,128)(2,1)S(1)} %collective-permute-done.4.refs_0_.refs_6_), channel_id=1, source_target_pairs={{0,1},{1,0},{2,3},{3,2},{4,5},{5,4},{6,7},{7,6},{8,9},{9,8},{10,11... | collective-permute-start | bytes 196616 | tf_op jit(solution)/shard_map/ppermute | solution.py:27
  12.1 3.0 %collective-permute-start.2 = (bf16[128,256]{1,0:T(8,128)(2,1)S(1)}, bf16[128,256]{1,0:T(8,128)(2,1)S(1)}, u32[]{:S(2)}, u32[]{:S(2)}) collective-permute-start(bf16[128,256]{1,0:T(8,128)(2,1)S(1)} %collective-permute-done.1.refs_0_.refs_2_), channel_id=1, source_target_pairs={{0,1},{1,0},{2,3},{3,2},{4,5},{5,4},{6,7},{7,6},{8,9},{9,8},{10,11... | collective-permute-start | bytes 196616 | tf_op jit(solution)/shard_map/ppermute | solution.py:27
  12.9 7.1 %collective-permute-start.13 = (f32[128,256]{1,0:T(8,128)S(1)}, f32[128,256]{1,0:T(8,128)S(1)}, u32[]{:S(2)}, u32[]{:S(2)}) collective-permute-start(f32[128,256]{1,0:T(8,128)S(1)} %get-tuple-element.50), channel_id=1, source_target_pairs={{0,1},{1,0},{2,3},{3,2},{4,5},{5,4},{6,7},{7,6},{8,9},{9,8},{10,11... | collective-permute-start | bytes 393224 | tf_op jit(solution)/shard_map/ppermute | solution.py:27
  14.2 5.8 %collective-permute-start.6 = (f32[128,256]{1,0:T(8,128)S(1)}, f32[128,256]{1,0:T(8,128)S(1)}, u32[]{:S(2)}, u32[]{:S(2)}) collective-permute-start(f32[128,256]{1,0:T(8,128)S(1)} %get-tuple-element.46), channel_id=1, source_target_pairs={{0,1},{1,0},{2,3},{3,2},{4,5},{5,4},{6,7},{7,6},{8,9},{9,8},{10,11... | collective-permute-start | bytes 393224 | tf_op jit(solution)/shard_map/ppermute | solution.py:27
  15.8 5.3 %collective-permute-start.15 = (f32[128,256]{1,0:T(8,128)S(1)}, f32[128,256]{1,0:T(8,128)S(1)}, u32[]{:S(2)}, u32[]{:S(2)}) collective-permute-start(f32[128,256]{1,0:T(8,128)S(1)} %add.53), channel_id=1, source_target_pairs={{0,3},{1,2},{2,1},{3,0},{4,7},{5,6},{6,5},{7,4},{8,11},{9,10},{10,... | collective-permute-start | bytes 393224 | tf_op jit(solution)/shard_map/ppermute | solution.py:27
  17.2 6.6 %copy-start.1 = (f32[256,256]{1,0:T(8,128)S(1)}, f32[256,256]{1,0:T(8,128)}, u32[]{:S(2)}) copy-start(f32[256,256]{1,0:T(8,128)} %param.7) | copy-start | bytes 786436
  17.2 6.6 %collective-permute-start.8 = (f32[128,256]{1,0:T(8,128)S(1)}, f32[128,256]{1,0:T(8,128)S(1)}, u32[]{:S(2)}, u32[]{:S(2)}) collective-permute-start(f32[128,256]{1,0:T(8,128)S(1)} %add.49), channel_id=1, source_target_pairs={{0,3},{1,2},{2,1},{3,0},{4,7},{5,6},{6,5},{7,4},{8,11},{9,10},{10,... | collective-permute-start | bytes 393224 | tf_op jit(solution)/shard_map/ppermute | solution.py:27
  23.9 10.1 %collective-permute-start.11 = (bf16[128,256]{1,0:T(8,128)(2,1)S(1)}, bf16[128,256]{1,0:T(8,128)(2,1)S(1)}, u32[]{:S(2)}, u32[]{:S(2)}) collective-permute-start(bf16[128,256]{1,0:T(8,128)(2,1)S(1)} %get-tuple-element.74), channel_id=1, source_target_pairs={{0,6},{1,7},{2,4},{3,5},{4,10},{5,11},{6,8},{7,9},{8,14},{9,15},{1... | collective-permute-start | bytes 196616 | tf_op jit(solution)/shard_map/ppermute | solution.py:27
  27.0 9.3 %collective-permute-start.9 = (bf16[128,256]{1,0:T(8,128)(2,1)S(1)}, bf16[128,256]{1,0:T(8,128)(2,1)S(1)}, u32[]{:S(2)}, u32[]{:S(2)}) collective-permute-start(bf16[128,256]{1,0:T(8,128)(2,1)S(1)} %get-tuple-element.74), channel_id=1, source_target_pairs={{0,4},{1,5},{2,6},{3,7},{4,8},{5,9},{6,10},{7,11},{8,12},{9,13},{1... | collective-permute-start | bytes 196616 | tf_op jit(solution)/shard_map/ppermute | solution.py:27
  28.6 8.6 %collective-permute-start.18 = (bf16[128,256]{1,0:T(8,128)(2,1)S(1)}, bf16[128,256]{1,0:T(8,128)(2,1)S(1)}, u32[]{:S(2)}, u32[]{:S(2)}) collective-permute-start(bf16[128,256]{1,0:T(8,128)(2,1)S(1)} %get-tuple-element.70), channel_id=1, source_target_pairs={{0,6},{1,7},{2,4},{3,5},{4,10},{5,11},{6,8},{7,9},{8,14},{9,15},{1... | collective-permute-start | bytes 196616 | tf_op jit(solution)/shard_map/ppermute | solution.py:27
  32.4 7.0 %collective-permute-start.16 = (bf16[128,256]{1,0:T(8,128)(2,1)S(1)}, bf16[128,256]{1,0:T(8,128)(2,1)S(1)}, u32[]{:S(2)}, u32[]{:S(2)}) collective-permute-start(bf16[128,256]{1,0:T(8,128)(2,1)S(1)} %get-tuple-element.70), channel_id=1, source_target_pairs={{0,4},{1,5},{2,6},{3,7},{4,8},{5,9},{6,10},{7,11},{8,12},{9,13},{1... | collective-permute-start | bytes 196616 | tf_op jit(solution)/shard_map/ppermute | solution.py:27
  34.7 7.6 %collective-permute-start.22 = (f32[128,256]{1,0:T(8,128)S(1)}, f32[128,256]{1,0:T(8,128)S(1)}, u32[]{:S(2)}, u32[]{:S(2)}) collective-permute-start(f32[128,256]{1,0:T(8,128)S(1)} %get-tuple-element.65), channel_id=1, source_target_pairs={{0,1},{1,0},{2,3},{3,2},{4,5},{5,4},{6,7},{7,6},{8,9},{9,8},{10,11... | collective-permute-start | bytes 393224 | tf_op jit(solution)/shard_map/ppermute | solution.py:27
  34.8 17.0 %collective-permute-start.20 = (f32[128,256]{1,0:T(8,128)S(1)}, f32[128,256]{1,0:T(8,128)S(1)}, u32[]{:S(2)}, u32[]{:S(2)}) collective-permute-start(f32[128,256]{1,0:T(8,128)S(1)} %get-tuple-element.75), channel_id=1, source_target_pairs={{0,4},{1,5},{2,6},{3,7},{4,8},{5,9},{6,10},{7,11},{8,12},{9,13},{1... | collective-permute-start | bytes 393224 | tf_op jit(solution)/shard_map/ppermute | solution.py:27
  36.3 3.8 %collective-permute-start.12 = (bf16[128,256]{1,0:T(8,128)(2,1)S(1)}, bf16[128,256]{1,0:T(8,128)(2,1)S(1)}, u32[]{:S(2)}, u32[]{:S(2)}) collective-permute-start(bf16[128,256]{1,0:T(8,128)(2,1)S(1)} %collective-permute-done.11.refs_0_.refs_2_), channel_id=1, source_target_pairs={{0,1},{1,0},{2,3},{3,2},{4,5},{5,4},{6,7},{7,6},{8,9},{9,8},{10,11... | collective-permute-start | bytes 196616 | tf_op jit(solution)/shard_map/ppermute | solution.py:27
  37.2 4.2 %collective-permute-start.10 = (bf16[128,256]{1,0:T(8,128)(2,1)S(1)}, bf16[128,256]{1,0:T(8,128)(2,1)S(1)}, u32[]{:S(2)}, u32[]{:S(2)}) collective-permute-start(bf16[128,256]{1,0:T(8,128)(2,1)S(1)} %collective-permute-done.9.refs_0_), channel_id=1, source_target_pairs={{0,1},{1,0},{2,3},{3,2},{4,5},{5,4},{6,7},{7,6},{8,9},{9,8},{10,11... | collective-permute-start | bytes 196616 | tf_op jit(solution)/shard_map/ppermute | solution.py:27
  39.4 3.5 %collective-permute-start.19 = (bf16[128,256]{1,0:T(8,128)(2,1)S(1)}, bf16[128,256]{1,0:T(8,128)(2,1)S(1)}, u32[]{:S(2)}, u32[]{:S(2)}) collective-permute-start(bf16[128,256]{1,0:T(8,128)(2,1)S(1)} %collective-permute-done.18.refs_0_.refs_6_), channel_id=1, source_target_pairs={{0,1},{1,0},{2,3},{3,2},{4,5},{5,4},{6,7},{7,6},{8,9},{9,8},{10,11... | collective-permute-start | bytes 196616 | tf_op jit(solution)/shard_map/ppermute | solution.py:27
  40.1 5.2 %collective-permute-start.17 = (bf16[128,256]{1,0:T(8,128)(2,1)S(1)}, bf16[128,256]{1,0:T(8,128)(2,1)S(1)}, u32[]{:S(2)}, u32[]{:S(2)}) collective-permute-start(bf16[128,256]{1,0:T(8,128)(2,1)S(1)} %collective-permute-done.16.refs_0_.refs_4_), channel_id=1, source_target_pairs={{0,1},{1,0},{2,3},{3,2},{4,5},{5,4},{6,7},{7,6},{8,9},{9,8},{10,11... | collective-permute-start | bytes 196616 | tf_op jit(solution)/shard_map/ppermute | solution.py:27
  41.4 10.2 %collective-permute-start.26 = (f32[128,256]{1,0:T(8,128)S(1)}, f32[128,256]{1,0:T(8,128)S(1)}, u32[]{:S(2)}, u32[]{:S(2)}) collective-permute-start(f32[128,256]{1,0:T(8,128)S(1)} %get-tuple-element.69), channel_id=1, source_target_pairs={{0,1},{1,0},{2,3},{3,2},{4,5},{5,4},{6,7},{7,6},{8,9},{9,8},{10,11... | collective-permute-start | bytes 393224 | tf_op jit(solution)/shard_map/ppermute | solution.py:27
  42.3 9.9 %collective-permute-start.21 = (f32[128,256]{1,0:T(8,128)S(1)}, f32[128,256]{1,0:T(8,128)S(1)}, u32[]{:S(2)}, u32[]{:S(2)}) collective-permute-start(f32[128,256]{1,0:T(8,128)S(1)} %get-tuple-element.63), channel_id=1, source_target_pairs={{0,1},{1,0},{2,3},{3,2},{4,5},{5,4},{6,7},{7,6},{8,9},{9,8},{10,11... | collective-permute-start | bytes 393224 | tf_op jit(solution)/shard_map/ppermute | solution.py:27
  42.9 9.3 %collective-permute-start.23 = (f32[128,256]{1,0:T(8,128)S(1)}, f32[128,256]{1,0:T(8,128)S(1)}, u32[]{:S(2)}, u32[]{:S(2)}) collective-permute-start(f32[128,256]{1,0:T(8,128)S(1)} %add.57), channel_id=1, source_target_pairs={{0,3},{1,2},{2,1},{3,0},{4,7},{5,6},{6,5},{7,4},{8,11},{9,10},{10,... | collective-permute-start | bytes 393224 | tf_op jit(solution)/shard_map/ppermute | solution.py:27
  45.3 8.6 %collective-permute-start.24 = (f32[128,256]{1,0:T(8,128)S(1)}, f32[128,256]{1,0:T(8,128)S(1)}, u32[]{:S(2)}, u32[]{:S(2)}) collective-permute-start(f32[128,256]{1,0:T(8,128)S(1)} %get-tuple-element.71), channel_id=1, source_target_pairs={{0,4},{1,5},{2,6},{3,7},{4,8},{5,9},{6,10},{7,11},{8,12},{9,13},{1... | collective-permute-start | bytes 393224 | tf_op jit(solution)/shard_map/ppermute | solution.py:27
  51.7 2.3 %collective-permute-start.25 = (f32[128,256]{1,0:T(8,128)S(1)}, f32[128,256]{1,0:T(8,128)S(1)}, u32[]{:S(2)}, u32[]{:S(2)}) collective-permute-start(f32[128,256]{1,0:T(8,128)S(1)} %get-tuple-element.67), channel_id=1, source_target_pairs={{0,1},{1,0},{2,3},{3,2},{4,5},{5,4},{6,7},{7,6},{8,9},{9,8},{10,11... | collective-permute-start | bytes 393224 | tf_op jit(solution)/shard_map/ppermute | solution.py:27
  51.8 5.2 %collective-permute-start.27 = (f32[128,256]{1,0:T(8,128)S(1)}, f32[128,256]{1,0:T(8,128)S(1)}, u32[]{:S(2)}, u32[]{:S(2)}) collective-permute-start(f32[128,256]{1,0:T(8,128)S(1)} %add.61), channel_id=1, source_target_pairs={{0,3},{1,2},{2,1},{3,0},{4,7},{5,6},{6,5},{7,4},{8,11},{9,10},{10,... | collective-permute-start | bytes 393224 | tf_op jit(solution)/shard_map/ppermute | solution.py:27

commit v2 on v1

v2 whole, which is shorter than its diff:
```python
import functools

import jax
import jax.numpy as jnp
from jax import lax
from jax.experimental import pallas as pl
from jax.experimental.pallas import tpu as pltpu
from jax.sharding import PartitionSpec as P


F32 = jnp.float32
BF16 = jnp.bfloat16
VMEM = pl.BlockSpec(memory_space=pltpu.VMEM)
SMEM = pl.BlockSpec(memory_space=pltpu.SMEM)
ANY = pl.BlockSpec(memory_space=pl.ANY)
BOTH_ROWS = (((0,), (0,)), ((), ()))
BOTH_COLUMNS = (((1,), (1,)), ((), ()))
MIB = 1 << 20


def route(block, strata_shift, users_flip):
    strata, users = lax.axis_size("strata"), lax.axis_size("users")
    pairs = [
        (s * users + u, ((s + strata_shift) % strata) * users + (u ^ users_flip))
        for s in range(strata)
        for u in range(users)
    ]
    return lax.ppermute(block, ("strata", "users"), pairs)


def dense_kernel(
    step, tiles_per_shard, group, counts_hbm, rows_hbm, columns_hbm, ratings_hbm, dense_ref,
    tiles, counts_ref, rows_ref, columns_ref, arrived, listed,
):
    flip = lax.axis_index("users") * tiles_per_shard
    lists = [
        pltpu.make_async_copy(counts_hbm, counts_ref, listed.at[0]),
        pltpu.make_async_copy(rows_hbm, rows_ref, listed.at[1]),
        pltpu.make_async_copy(columns_hbm, columns_ref, listed.at[2]),
    ]

    def rating_copy(g):
        some = pl.ds(g * group, group)
        return pltpu.make_async_copy(
            ratings_hbm.at[0, 0, step, some], tiles.at[some], arrived.at[g]
        )

    groups = tiles.shape[0] // group
    for copy in lists:
        copy.start()
    for g in range(groups):
        rating_copy(g).start()

    @pl.loop(0, dense_ref.shape[0])
    def _(j):
        dense_ref[j] = jnp.zeros(dense_ref.shape[1:], BF16)

    for copy in lists:
        copy.wait()
    count = counts_ref[0, 0, step]

    @pl.loop(0, groups)
    def _(g):
        rating_copy(g).wait()

        @pl.when(g * group < count)
        def _():
            for k in range(group):
                m = g * group + k
                j = columns_ref[0, 0, step, m] ^ flip
                r = rows_ref[0, 0, step, m]
                rating = jnp.where(m < count, tiles[m], 0)
                dense_ref[j, r] = rating.astype(F32).astype(BF16).T


def dense_ratings(step, tiles_per_shard, column_tiles, user_rows, tile_rows, tile_columns, tile_counts, ratings):
    slots, tile = ratings.shape[3], ratings.shape[4]
    group = 8 if slots % 8 == 0 else 1
    operands = [
        pltpu.with_memory_space_constraint(x, pltpu.HBM)
        for x in (tile_counts, tile_rows, tile_columns, ratings)
    ]
    return pl.pallas_call(
        functools.partial(dense_kernel, step, tiles_per_shard, group),
        out_shape=jax.ShapeDtypeStruct((column_tiles, user_rows // tile, tile, tile), BF16),
        in_specs=[pl.BlockSpec(memory_space=pltpu.HBM)] * 4,
        out_specs=VMEM,
        scratch_shapes=[
            pltpu.VMEM((slots, tile, tile), jnp.int32),
            pltpu.SMEM(tile_counts.shape, jnp.int32),
            pltpu.SMEM(tile_rows.shape, jnp.int32),
            pltpu.SMEM(tile_columns.shape, jnp.int32),
            pltpu.SemaphoreType.DMA((slots // group,)),
            pltpu.SemaphoreType.DMA((3,)),
        ],
        compiler_params=pltpu.CompilerParams(vmem_limit_bytes=12 * MIB),
        cost_estimate=pl.CostEstimate(flops=2 * 10**9, bytes_accessed=8 * MIB, transcendentals=0),
    )(*operands)


def terms_kernel(columns, sizes, chunk, users_ref, dense_ref, *refs):
    item_refs, (residual_ref, *grad_refs) = refs[: len(refs) - 1 - len(sizes)], refs[-1 - len(sizes) :]
    tile = dense_ref.shape[-1]
    per_chunk = chunk // tile
    items = jnp.concatenate([ref[...] for ref in item_refs], axis=0)
    chunks = users_ref.shape[0] // chunk

    def users(i):
        return users_ref[i * chunk : (i + 1) * chunk, :]

    def predict(i):
        return lax.dot_general(items, users(i), BOTH_COLUMNS, preferred_element_type=F32)

    grad = None
    ahead = predict(0)
    for i in range(chunks):
        predicted = ahead
        if i + 1 < chunks:
            ahead = predict(i + 1)
        residuals = []
        for q in range(per_chunk):
            r = i * per_chunk + q
            rating = jnp.concatenate([dense_ref[j, r] for j in columns], axis=0).astype(F32)
            residual = jnp.where(
                rating > 0, rating - predicted[:, q * tile : (q + 1) * tile], 0.0
            ).astype(BF16)
            residual_ref[r] = residual
            residuals.append(residual)
        part = jnp.dot(jnp.concatenate(residuals, axis=1), users(i), preferred_element_type=F32)
        grad = part if grad is None else grad + part
    start = 0
    for ref in grad_refs:
        ref[...] = grad[start : start + ref.shape[0]]
        start += ref.shape[0]


def terms(columns, sizes, users_low, dense, items):
    user_rows, width = users_low.shape
    tile = dense.shape[-1]
    rows = tile * len(columns)
    return pl.pallas_call(
        functools.partial(terms_kernel, columns, sizes, min(4 * tile, user_rows)),
        out_shape=[jax.ShapeDtypeStruct((user_rows // tile, rows, tile), BF16)]
        + [jax.ShapeDtypeStruct((size, width), F32) for size in sizes],
        in_specs=[VMEM] * (2 + len(items)),
        out_specs=[VMEM] * (1 + len(sizes)),
        compiler_params=pltpu.CompilerParams(vmem_limit_bytes=16 * MIB),
        cost_estimate=pl.CostEstimate(
            flops=4 * user_rows * rows * width, bytes_accessed=MIB, transcendentals=0
        ),
    )(users_low, dense, *items)


def users_kernel(number, chunk, low_out, users_ref, *refs):
    item_refs, refs = refs[:number], refs[number:]
    items = jnp.concatenate([ref[...] for ref in item_refs], axis=0)
    tile = refs[0].shape[-1]
    if low_out:
        *residual_refs, out_ref, low_ref = refs
    else:
        *residual_refs, out_hbm, out_ref, sent = refs
    copies = []
    for i in range(users_ref.shape[0] // chunk):
        rows = slice(i * chunk, (i + 1) * chunk)
        residual = jnp.concatenate(
            [
                jnp.concatenate([ref[r] for ref in residual_refs], axis=0)
                for r in range(i * chunk // tile, (i + 1) * chunk // tile)
            ],
            axis=1,
        )
        total = lax.dot_general(residual, items, BOTH_ROWS, preferred_element_type=F32)
        users = users_ref[rows, :]
        updated = users + 0.01 * (total - 0.05 * users)
        out_ref[rows, :] = updated
        if low_out:
            low_ref[rows, :] = updated.astype(BF16)
        else:
            copies.append(pltpu.make_async_copy(out_ref.at[rows], out_hbm.at[rows], sent.at[i]))
            copies[-1].start()
    for copy in copies:
        copy.wait()


def update_users(users, items, residuals, low_out):
    user_rows, width = users.shape
    tile = residuals[0].shape[-1]
    chunk = min(2 * tile, user_rows)
    item_rows = sum(block.shape[0] for block in items)
    full = jax.ShapeDtypeStruct(users.shape, F32)
    if low_out:
        out_shape, out_specs, scratch = [full, jax.ShapeDtypeStruct(users.shape, BF16)], [VMEM] * 2, []
    else:
        out_shape, out_specs = [full], [pl.BlockSpec(memory_space=pltpu.HBM)]
        scratch = [pltpu.VMEM(users.shape, F32), pltpu.SemaphoreType.DMA((user_rows // chunk,))]
    return pl.pallas_call(
        functools.partial(users_kernel, len(items), chunk, low_out),
        out_shape=out_shape,
        in_specs=[VMEM] * (1 + len(items) + len(residuals)),
        out_specs=out_specs,
        scratch_shapes=scratch,
        compiler_params=pltpu.CompilerParams(vmem_limit_bytes=12 * MIB),
        cost_estimate=pl.CostEstimate(
            flops=2 * user_rows * item_rows * width, bytes_accessed=4 * MIB, transcendentals=0
        ),
        name="users",
    )(users, *items, *residuals)


def updated_items(items, grad):
    return items + 0.003 * (grad - 0.05 * items)


def after(value, *earlier):
    return lax.optimization_barrier((value, *earlier))[0]


def paired_shards(user_factors, item_factors, tile_rows, tile_columns, tile_counts, ratings):
    step_total, tile = ratings.shape[2], ratings.shape[-1]
    per_shard = item_factors.shape[0] // tile
    column_tiles = per_shard * lax.axis_size("users")
    halves = range(per_shard)
    low = item_factors.astype(BF16)
    users_now, items_now = user_factors, item_factors
    held = {0: [low], 1: [route(low, 0, 1)], 2: [route(low, 0, 2)]}
    mark = []

    def ratings_of(step):
        return dense_ratings(
            step, per_shard, column_tiles, user_factors.shape[0],
            after(tile_rows, *mark), tile_columns, tile_counts, ratings,
        )

    dense = ratings_of(0)
    users_low = after(user_factors, dense).astype(BF16)
    for step in range(step_total):
        pieces = len(held[2])
        items_in, residuals, sums = [], [], []

        def run(*which):
            items = [held[d][p] for d, p in which]
            sizes = tuple(block.shape[0] for block in items)
            columns = tuple(
                d * per_shard + p * size // tile + k
                for (d, p), size in zip(which, sizes)
                for k in range(size // tile)
            )
            items[0] = after(items[0], *mark)
            residual, *grads = terms(columns, sizes, users_low, dense, items)
            mark[:] = grads[-1:]
            items_in.extend(held[d][p] for d, p in which)
            residuals.append(residual)
            return grads

        def near():
            own, passed = run((0, 0), (1, 0))
            return own + route(passed, 0, 1)

        def far(p):
            (passed,) = run((2, p))
            passed = route(passed, 0, 1)
            (own,) = run((3, p))
            for k in range(per_shard // pieces):
                rows = slice(k * tile, (k + 1) * tile)
                sums.append(route(own[rows] + passed[rows], 0, 3))

        def update(low_out):
            blocks = list(items_in)
            blocks[0] = after(blocks[0], *mark)
            results = update_users(users_now, blocks, residuals, low_out)
            mark[:] = results[-1:]
            return results

        last = step == step_total - 1
        held[3] = []
        if step == 0:
            near_sum = near()
        for p in range(pieces):
            block = after(held[2][p], *mark) if p else held[2][p]
            held[3].append(route(block, 0, 1))
            far(p)
        if step > 0:
            held[0] = [after(held[0][0], *mark)]
            held[1] = [route(held[0][0], 0, 1)]
            near_sum = near()
        if not last:
            dense = ratings_of(step + 1)
        low_parts, held = [], {2: []}
        users_now, *rest = update(not last)
        parts = []
        for h in halves:
            rows = slice(h * tile, (h + 1) * tile)
            base = updated_items(items_now[rows], after(near_sum, *parts)[rows])
            base = lax.optimization_barrier(base)
            parts.append(base + 0.003 * sums[h])
            if not last:
                low_parts.append(parts[h].astype(BF16))
                held[2].append(route(low_parts[h], 1, 2))
        items_now = jnp.concatenate(parts, axis=0)
        if not last:
            users_low = rest[0]
            held[0] = [route(jnp.concatenate(low_parts, axis=0), 1, 0)]
            items_now = route(after(items_now, *mark), 1, 0)
    return users_now, items_now


def gathered_shards(user_factors, item_factors, tile_rows, tile_columns, tile_counts, ratings):
    step_total, tile = ratings.shape[2], ratings.shape[-1]
    users_now, item_part = user_factors, item_factors
    for step in range(step_total):
        block = lax.all_gather(item_part.astype(BF16), "users", axis=0, tiled=True)
        column_tiles = block.shape[0] // tile
        dense = dense_ratings(
            step, 0, column_tiles, users_now.shape[0], tile_rows, tile_columns, tile_counts, ratings
        )
        residual, grad = terms(
            tuple(range(column_tiles)), block.shape[:1], users_now.astype(BF16), dense, [block]
        )
        grad_part = lax.psum_scatter(grad, "users", scatter_dimension=0, tiled=True)
        users_now = update_users(users_now, [block], [residual], False)[0]
        item_part = updated_items(item_part, grad_part)
        if step < step_total - 1:
            item_part = route(item_part, 1, 0)
    return users_now, item_part


def solution(mesh):
    placed = (
        P(("strata", "users"), None),
        P(("strata", "users"), None),
        P("strata", "users", None, None),
        P("strata", "users", None, None),
        P("strata", "users", None),
        P("strata", "users", None, None, None, None),
    )

    def shards(user_factors, item_factors, *lists):
        tile = lists[-1].shape[-1]
        paired = mesh.shape["users"] == 4 and item_factors.shape[0] % tile == 0
        body = paired_shards if paired else gathered_shards
        return body(user_factors, item_factors, *lists)

    return jax.shard_map(
        shards,
        mesh=mesh,
        in_specs=placed,
        out_specs=(P(("strata", "users"), None), P(("strata", "users"), None)),
        check_vma=False,
    )
```

time: 57.9 us -> 55.6 us (0.960)
  waiting for transfers between devices: 9.92 us -> 22.5 us
  starting transfers between devices: 20.9 us -> 13.3 us
  Pallas kernels: 24 us -> 16.6 us
  other arithmetic: 1.05 us -> 2.14 us
  local copies, waits for them, and re-layouts: 1 us -> 0.01 us
    ppermute x28 -> x19, waiting for transfers between devices: 9.92 us -> 22.5 us  [route(): return lax.ppermute(block, ('strata', 'users'), pairs)]
    ppermute x28 -> x19, starting transfers between devices: 20.9 us -> 13.3 us  [route(): return lax.ppermute(block, ('strata', 'users'), pairs)]
    pallas_call x18 -> x10, Pallas kernels: 19.4 us -> 12.1 us  [the longest x8 8.26 us: terms(): pl.pallas_call(functools.partial(terms_kernel, columns, sizes, min(4 * ti...]
    slice x1 -> x0, local copies, waits for them, and re-layouts: 0.99 us -> none  [paired_shards(): parts = [item_factors[h * tile:(h + 1) * tile] for h in halves]]
    convert_element_type x2 -> x4, other arithmetic: 0.18 us -> 1.11 us  [the longest x1 0.97 us: paired_shards(): low = item_factors.astype(BF16)]
  transfers between devices with their start and end apart: 28 -> 19, of which waited for: 6 -> 11; matrix products, arithmetic and copies ran while one was open for 0% -> 1% of each run, Pallas kernels for 41% -> 27%
where the time goes in v2:
time: 55.6 us; the launch traced here: 55.4 us
  waiting for transfers between devices  22.5 us (40%)
  Pallas kernels  16.6 us (30%)
  starting transfers between devices  13.3 us (24%)
  other arithmetic  2.14 us (4%)
  between operations  0.87 us (2%)
    ppermute x19, waiting for transfers between devices, route(): return lax.ppermute(block, ('strata', 'users'), pairs)  22.5 us
    ppermute x19, starting transfers between devices, route(): return lax.ppermute(block, ('strata', 'users'), pairs)  13.3 us
    pallas_call x8, Pallas kernels, terms(): pl.pallas_call(functools.partial(terms_kernel, columns, sizes, min(4 * ti...  8.26 us
    pallas_call x2, Pallas kernels, dense_ratings(): pl.pallas_call(functools.partial(dense_kernel, step, tiles_per_shard, gro...  4.53 us
    pallas_call x2, Pallas kernels, update_users(): pl.pallas_call(functools.partial(users_kernel, len(items), chunk, low_out...  3.79 us
  transfers between devices with their start and end apart: 19, of which 11 were waited for; matrix products, arithmetic and copies ran while one was open for 1% of the time, Pallas kernels for 27%

profile of v2, /device:TPU:0, one launch (start us, length us, event | category | flops | bytes accessed | tf_op | source)
XLA Modules:
  0.0 55.4 jit_solution(13147849676583720511)
XLA Ops:
  0.6 1.0 %convert_element_type.12.refs_0_ = bf16[256,256]{1,0:T(8,128)(2,1)S(1)} convert(f32[256,256]{1,0:T(8,128)} %param.7) | non-fusion elementwise | flops 65536 | bytes 393216 | tf_op jit(solution)/shard_map/convert_element_type | solution.py:223
  1.6 0.0 copy-start
  1.6 0.6 %collective-permute-start.2 = (bf16[256,256]{1,0:T(8,128)(2,1)S(1)}, bf16[256,256]{1,0:T(8,128)(2,1)S(1)}, u32[]{:S(2)}, u32[]{:S(2)}) collective-permute-start(bf16[256,256]{1,0:T(8,128)(2,1)S(1)} %convert_element_type.12.refs_0_), channel_id=1, source_target_pairs={{0,1},{1,0},{2,3},{3,2},{4,5},{5,4},{6,7},{7,6},{8,9},{9,8},{10,11... | collective-permute-start | bytes 393224 | tf_op jit(solution)/shard_map/ppermute | solution.py:28
  2.2 2.6 %collective-permute-start = (bf16[256,256]{1,0:T(8,128)(2,1)S(1)}, bf16[256,256]{1,0:T(8,128)(2,1)S(1)}, u32[]{:S(2)}, u32[]{:S(2)}) collective-permute-start(bf16[256,256]{1,0:T(8,128)(2,1)S(1)} %convert_element_type.12.refs_0_), channel_id=1, source_target_pairs={{0,2},{1,3},{2,0},{3,1},{4,6},{5,7},{6,4},{7,5},{8,10},{9,11},{10,... | collective-permute-start | bytes 393224 | tf_op jit(solution)/shard_map/ppermute | solution.py:28
  4.8 2.2 %shard_map.77.dense_ref = bf16[8,16,128,128]{3,2,1,0:T(8,128)(2,1)S(1)} custom-call(s32[1,1,2]{2,1,0:T(1,128)} %counts_hbm.3, s32[1,1,2,64]{3,2,1,0:T(2,128)} %rows_hbm.1, s32[1,1,2,64]{3,2,1,0:T(2,128)} %columns_hbm.3, s32[1,1,2,64,128,128]{5,4,3,2,1,0:T(8,128)} %ratings_hbm.3), custom_call_target="tpu_custom_call" | custom-call | flops 2000000000 | bytes 8388608 | tf_op jit(solution)/shard_map/pallas_call | solution.py:83
  7.0 0.0 copy-done
  7.0 0.1 convert_element_type.13.users_ref
  7.1 1.7 %collective-permute-done.refs_0_.refs_2_ = bf16[256,256]{1,0:T(8,128)(2,1)S(1)} collective-permute-done((bf16[256,256]{1,0:T(8,128)(2,1)S(1)}, bf16[256,256]{1,0:T(8,128)(2,1)S(1)}, u32[]{:S(2)}, u32[]{:S(2)}) %collective-permute-start) | collective-permute-done | bytes 131104 | tf_op jit(solution)/shard_map/ppermute | solution.py:28
  8.8 0.0 collective-permute-start.1
  8.8 0.0 collective-permute-done.2.refs_1_
  8.8 1.7 %shard_map.78 = (bf16[16,512,128]{2,1,0:T(8,128)(2,1)S(1)}, f32[256,256]{1,0:T(8,128)S(1)}, f32[256,256]{1,0:T(8,128)S(1)}) custom-call(bf16[2048,256]{1,0:T(8,128)(2,1)S(1)} %convert_element_type.13.users_ref, bf16[8,16,128,128]{3,2,1,0:T(8,128)(2,1)S(1)} %shard_map.77.dense_ref, bf16[256,256]{1,0:T(8,128)(2,1)S(1)} %convert_element_type.12.refs_0_, ...), custom_call_target="tpu_custom_call" | custom-call | flops 1073741824 | bytes 1048576 | tf_op jit(solution)/shard_map/pallas_call | solution.py:141
  10.6 0.6 %collective-permute-start.3 = (f32[256,256]{1,0:T(8,128)S(1)}, f32[256,256]{1,0:T(8,128)S(1)}, u32[]{:S(2)}, u32[]{:S(2)}) collective-permute-start(f32[256,256]{1,0:T(8,128)S(1)} %get-tuple-element.38), channel_id=1, source_target_pairs={{0,1},{1,0},{2,3},{3,2},{4,5},{5,4},{6,7},{7,6},{8,9},{9,8},{10,11... | collective-permute-start | bytes 786440 | tf_op jit(solution)/shard_map/ppermute | solution.py:28
  11.1 1.0 %shard_map.79 = (bf16[16,256,128]{2,1,0:T(8,128)(2,1)S(1)}, f32[256,256]{1,0:T(8,128)S(1)}) custom-call(bf16[2048,256]{1,0:T(8,128)(2,1)S(1)} %convert_element_type.13.users_ref, bf16[8,16,128,128]{3,2,1,0:T(8,128)(2,1)S(1)} %shard_map.77.dense_ref, bf16[256,256]{1,0:T(8,128)(2,1)S(1)} %collective-permute-done.refs_0_.refs_2_), custom_call_target="tpu_custom_call" | custom-call | flops 536870912 | bytes 1048576 | tf_op jit(solution)/shard_map/pallas_call | solution.py:141
  12.1 0.1 collective-permute-start.4
  12.2 0.0 collective-permute-done.1.refs_0_.refs_3_
  12.2 1.0 %shard_map.80 = (bf16[16,256,128]{2,1,0:T(8,128)(2,1)S(1)}, f32[256,256]{1,0:T(8,128)S(1)}) custom-call(bf16[2048,256]{1,0:T(8,128)(2,1)S(1)} %convert_element_type.13.users_ref, bf16[8,16,128,128]{3,2,1,0:T(8,128)(2,1)S(1)} %shard_map.77.dense_ref, bf16[256,256]{1,0:T(8,128)(2,1)S(1)} %collective-permute-done.1.refs_0_.refs_3_), custom_call_target="tpu_custom_call" | custom-call | flops 536870912 | bytes 1048576 | tf_op jit(solution)/shard_map/pallas_call | solution.py:141
  13.3 1.5 %users.2 = (f32[2048,256]{1,0:T(8,128)S(1)}, bf16[2048,256]{1,0:T(8,128)(2,1)S(1)}) custom-call(f32[2048,256]{1,0:T(8,128)S(1)} %copy-done, bf16[256,256]{1,0:T(8,128)(2,1)S(1)} %convert_element_type.12.refs_0_, bf16[256,256]{1,0:T(8,128)(2,1)S(1)} %collective-permute-done.2.refs_1_, bf16[256,256]{1,0:T(8,128)(2,1)S(1)} %collective-permute-done.refs_0_.refs_2_, ...), custom_call_target="tpu_custom_call" | custom-call | flops 1073741824 | bytes 4194304 | tf_op jit(solution)/shard_map/users/pallas_call | solution.py:196
  14.8 0.0 copy-start.1
  14.8 2.3 %shard_map.81.dense_ref = bf16[8,16,128,128]{3,2,1,0:T(8,128)(2,1)S(1)} custom-call(s32[1,1,2]{2,1,0:T(1,128)} %counts_hbm.3, s32[1,1,2,64]{3,2,1,0:T(2,128)} %rows_hbm.1, s32[1,1,2,64]{3,2,1,0:T(2,128)} %columns_hbm.3, s32[1,1,2,64,128,128]{5,4,3,2,1,0:T(8,128)} %ratings_hbm.3), custom_call_target="tpu_custom_call" | custom-call | flops 2000000000 | bytes 8388608 | tf_op jit(solution)/shard_map/pallas_call | solution.py:83
  17.1 0.0 collective-permute-done.3
  17.1 0.0 collective-permute-done.4
  17.2 1.9 %collective-permute-start.5 = (f32[128,256]{1,0:T(8,128)S(1)}, f32[128,256]{1,0:T(8,128)S(1)}, u32[]{:S(2)}, u32[]{:S(2)}) collective-permute-start(f32[128,256]{1,0:T(8,128)S(1)} %get-tuple-element.77), channel_id=1, source_target_pairs={{0,3},{1,2},{2,1},{3,0},{4,7},{5,6},{6,5},{7,4},{8,11},{9,10},{10,... | collective-permute-start | bytes 393224 | tf_op jit(solution)/shard_map/ppermute | solution.py:28
  19.1 0.0 copy-done.1
  19.1 0.1 collective-permute-start.7
  19.2 3.8 %collective-permute-done.5 = f32[128,256]{1,0:T(8,128)S(1)} collective-permute-done((f32[128,256]{1,0:T(8,128)S(1)}, f32[128,256]{1,0:T(8,128)S(1)}, u32[]{:S(2)}, u32[]{:S(2)}) %collective-permute-start.5) | collective-permute-done | bytes 131104 | tf_op jit(solution)/shard_map/ppermute | solution.py:28
  23.0 2.1 %collective-permute-start.6 = (bf16[128,256]{1,0:T(8,128)(2,1)S(1)}, bf16[128,256]{1,0:T(8,128)(2,1)S(1)}, u32[]{:S(2)}, u32[]{:S(2)}) collective-permute-start(bf16[128,256]{1,0:T(8,128)(2,1)S(1)} %get-tuple-element.74), channel_id=1, source_target_pairs={{0,6},{1,7},{2,4},{3,5},{4,10},{5,11},{6,8},{7,9},{8,14},{9,15},{1... | collective-permute-start | bytes 196616 | tf_op jit(solution)/shard_map/ppermute | solution.py:28
  25.2 0.2 collective-permute-done.7
  25.4 2.5 %collective-permute-start.9 = (bf16[128,256]{1,0:T(8,128)(2,1)S(1)}, bf16[128,256]{1,0:T(8,128)(2,1)S(1)}, u32[]{:S(2)}, u32[]{:S(2)}) collective-permute-start(bf16[128,256]{1,0:T(8,128)(2,1)S(1)} %get-tuple-element.72), channel_id=1, source_target_pairs={{0,6},{1,7},{2,4},{3,5},{4,10},{5,11},{6,8},{7,9},{8,14},{9,15},{1... | collective-permute-start | bytes 196616 | tf_op jit(solution)/shard_map/ppermute | solution.py:28
  27.9 3.5 %collective-permute-done.6.refs_0_ = bf16[128,256]{1,0:T(8,128)(2,1)S(1)} collective-permute-done((bf16[128,256]{1,0:T(8,128)(2,1)S(1)}, bf16[128,256]{1,0:T(8,128)(2,1)S(1)}, u32[]{:S(2)}, u32[]{:S(2)}) %collective-permute-start.6) | collective-permute-done | bytes 65568 | tf_op jit(solution)/shard_map/ppermute | solution.py:28
  31.4 0.1 collective-permute-start.10
  31.5 0.1 collective-permute-start.8
  31.6 0.7 %shard_map.82 = (bf16[16,128,128]{2,1,0:T(8,128)(2,1)S(1)}, f32[128,256]{1,0:T(8,128)S(1)}) custom-call(bf16[2048,256]{1,0:T(8,128)(2,1)S(1)} %get-tuple-element.49.users_ref, bf16[8,16,128,128]{3,2,1,0:T(8,128)(2,1)S(1)} %shard_map.81.dense_ref, bf16[128,256]{1,0:T(8,128)(2,1)S(1)} %collective-permute-done.6.refs_0_), custom_call_target="tpu_custom_call" | custom-call | flops 268435456 | bytes 1048576 | tf_op jit(solution)/shard_map/pallas_call | solution.py:141
  32.3 0.3 collective-permute-done.10.refs_0_.refs_1_
  32.6 0.7 %shard_map.83 = (bf16[16,128,128]{2,1,0:T(8,128)(2,1)S(1)}, f32[128,256]{1,0:T(8,128)S(1)}) custom-call(bf16[2048,256]{1,0:T(8,128)(2,1)S(1)} %get-tuple-element.49.users_ref, bf16[8,16,128,128]{3,2,1,0:T(8,128)(2,1)S(1)} %shard_map.81.dense_ref, bf16[128,256]{1,0:T(8,128)(2,1)S(1)} %collective-permute-done.10.refs_0_.refs_1_), custom_call_target="tpu_custom_call" | custom-call | flops 268435456 | bytes 1048576 | tf_op jit(solution)/shard_map/pallas_call | solution.py:141
  33.4 0.6 %collective-permute-done.9.refs_0_.refs_2_ = bf16[128,256]{1,0:T(8,128)(2,1)S(1)} collective-permute-done((bf16[128,256]{1,0:T(8,128)(2,1)S(1)}, bf16[128,256]{1,0:T(8,128)(2,1)S(1)}, u32[]{:S(2)}, u32[]{:S(2)}) %collective-permute-start.9) | collective-permute-done | bytes 65568 | tf_op jit(solution)/shard_map/ppermute | solution.py:28
  34.0 0.1 collective-permute-start.11
  34.1 0.7 %shard_map.84 = (bf16[16,128,128]{2,1,0:T(8,128)(2,1)S(1)}, f32[128,256]{1,0:T(8,128)S(1)}) custom-call(bf16[2048,256]{1,0:T(8,128)(2,1)S(1)} %get-tuple-element.49.users_ref, bf16[8,16,128,128]{3,2,1,0:T(8,128)(2,1)S(1)} %shard_map.81.dense_ref, bf16[128,256]{1,0:T(8,128)(2,1)S(1)} %collective-permute-done.9.refs_0_.refs_2_), custom_call_target="tpu_custom_call" | custom-call | flops 268435456 | bytes 1048576 | tf_op jit(solution)/shard_map/pallas_call | solution.py:141
  34.8 0.4 collective-permute-done.11.refs_0_.refs_3_
  35.2 0.7 %shard_map.85 = (bf16[16,128,128]{2,1,0:T(8,128)(2,1)S(1)}, f32[128,256]{1,0:T(8,128)S(1)}) custom-call(bf16[2048,256]{1,0:T(8,128)(2,1)S(1)} %get-tuple-element.49.users_ref, bf16[8,16,128,128]{3,2,1,0:T(8,128)(2,1)S(1)} %shard_map.81.dense_ref, bf16[128,256]{1,0:T(8,128)(2,1)S(1)} %collective-permute-done.11.refs_0_.refs_3_), custom_call_target="tpu_custom_call" | custom-call | flops 268435456 | bytes 1048576 | tf_op jit(solution)/shard_map/pallas_call | solution.py:141
  36.0 4.1 %collective-permute-done.8.refs_0_.refs_4_ = bf16[256,256]{1,0:T(8,128)(2,1)S(1)} collective-permute-done((bf16[256,256]{1,0:T(8,128)(2,1)S(1)}, bf16[256,256]{1,0:T(8,128)(2,1)S(1)}, u32[]{:S(2)}, u32[]{:S(2)}) %collective-permute-start.8) | collective-permute-done | bytes 131104 | tf_op jit(solution)/shard_map/ppermute | solution.py:28
  40.1 0.0 collective-permute-start.12
  40.1 1.3 %collective-permute-done.12.refs_1_.refs_5_ = bf16[256,256]{1,0:T(8,128)(2,1)S(1)} collective-permute-done((bf16[256,256]{1,0:T(8,128)(2,1)S(1)}, bf16[256,256]{1,0:T(8,128)(2,1)S(1)}, u32[]{:S(2)}, u32[]{:S(2)}) %collective-permute-start.12) | collective-permute-done | bytes 131104 | tf_op jit(solution)/shard_map/ppermute | solution.py:28
  41.4 1.7 %shard_map.86 = (bf16[16,512,128]{2,1,0:T(8,128)(2,1)S(1)}, f32[256,256]{1,0:T(8,128)S(1)}, f32[256,256]{1,0:T(8,128)S(1)}) custom-call(bf16[2048,256]{1,0:T(8,128)(2,1)S(1)} %get-tuple-element.49.users_ref, bf16[8,16,128,128]{3,2,1,0:T(8,128)(2,1)S(1)} %shard_map.81.dense_ref, bf16[256,256]{1,0:T(8,128)(2,1)S(1)} %collective-permute-done.8.refs_0_.refs_4_, ...), custom_call_target="tpu_custom_call" | custom-call | flops 1073741824 | bytes 1048576 | tf_op jit(solution)/shard_map/pallas_call | solution.py:141
  43.1 0.2 collective-permute-start.14
  43.3 0.0 collective-permute-start.13
  43.3 0.4 collective-permute-start.15
  43.7 0.1 collective-permute-start.17
  43.8 1.1 %collective-permute-done.15 = f32[128,256]{1,0:T(8,128)S(1)} collective-permute-done((f32[128,256]{1,0:T(8,128)S(1)}, f32[128,256]{1,0:T(8,128)S(1)}, u32[]{:S(2)}, u32[]{:S(2)}) %collective-permute-start.15) | collective-permute-done | bytes 131104 | tf_op jit(solution)/shard_map/ppermute | solution.py:28
  44.9 0.8 %collective-permute-start.16 = (f32[128,256]{1,0:T(8,128)S(1)}, f32[128,256]{1,0:T(8,128)S(1)}, u32[]{:S(2)}, u32[]{:S(2)}) collective-permute-start(f32[128,256]{1,0:T(8,128)S(1)} %add.51), channel_id=1, source_target_pairs={{0,3},{1,2},{2,1},{3,0},{4,7},{5,6},{6,5},{7,4},{8,11},{9,10},{10,... | collective-permute-start | bytes 393224 | tf_op jit(solution)/shard_map/ppermute | solution.py:28
  45.7 0.0 collective-permute-done.17
  45.7 1.1 %collective-permute-start.18 = (f32[128,256]{1,0:T(8,128)S(1)}, f32[128,256]{1,0:T(8,128)S(1)}, u32[]{:S(2)}, u32[]{:S(2)}) collective-permute-start(f32[128,256]{1,0:T(8,128)S(1)} %add.54), channel_id=1, source_target_pairs={{0,3},{1,2},{2,1},{3,0},{4,7},{5,6},{6,5},{7,4},{8,11},{9,10},{10,... | collective-permute-start | bytes 393224 | tf_op jit(solution)/shard_map/ppermute | solution.py:28
  46.8 2.3 %users.3 = f32[2048,256]{1,0:T(8,128)} custom-call(f32[2048,256]{1,0:T(8,128)S(1)} %get-tuple-element.47.users_ref, bf16[128,256]{1,0:T(8,128)(2,1)S(1)} %collective-permute-done.6.refs_0_, bf16[128,256]{1,0:T(8,128)(2,1)S(1)} %collective-permute-done.10.refs_0_.refs_1_, bf16[128,256]{1,0:T(8,128)(2,1)S(1)} %collective-permute-done.9.refs_0_.refs_2_, ...), custom_call_target="tpu_custom_call" | custom-call | flops 1073741824 | bytes 4194304 | tf_op jit(solution)/shard_map/users/pallas_call | solution.py:196
  49.1 0.0 collective-permute-done.14
  49.2 5.4 %collective-permute-done.13 = f32[256,256]{1,0:T(8,128)S(1)} collective-permute-done((f32[256,256]{1,0:T(8,128)S(1)}, f32[256,256]{1,0:T(8,128)S(1)}, u32[]{:S(2)}, u32[]{:S(2)}) %collective-permute-start.13) | collective-permute-done | bytes 262176 | tf_op jit(solution)/shard_map/ppermute | solution.py:28
  54.6 0.0 collective-permute-done.16
  54.7 0.0 collective-permute-done.18
  54.7 0.7 %pad_maximum_fusion.1 = f32[256,256]{1,0:T(8,128)} fusion(f32[128,256]{1,0:T(8,128)S(1)} %multiply_add_fusion, f32[128,256]{1,0:T(8,128)S(1)} %multiply_add_fusion.2), kind=kLoop, calls=%fused_computation.1 | loop fusion | flops 65536 | bytes 524288 | tf_op jit(solution)/shard_map/concatenate | solution.py:299
  (15 shorter events, 0.4 us)
Async XLA Ops:
  1.6 5.4 %copy-start = (f32[2048,256]{1,0:T(8,128)S(1)}, f32[2048,256]{1,0:T(8,128)}, u32[]{:S(2)}) copy-start(f32[2048,256]{1,0:T(8,128)} %users_ref.1) | copy-start | bytes 6291460
  1.6 7.2 %collective-permute-start.2 = (bf16[256,256]{1,0:T(8,128)(2,1)S(1)}, bf16[256,256]{1,0:T(8,128)(2,1)S(1)}, u32[]{:S(2)}, u32[]{:S(2)}) collective-permute-start(bf16[256,256]{1,0:T(8,128)(2,1)S(1)} %convert_element_type.12.refs_0_), channel_id=1, source_target_pairs={{0,1},{1,0},{2,3},{3,2},{4,5},{5,4},{6,7},{7,6},{8,9},{9,8},{10,11... | collective-permute-start | bytes 393224 | tf_op jit(solution)/shard_map/ppermute | solution.py:28
  2.2 6.7 %collective-permute-start = (bf16[256,256]{1,0:T(8,128)(2,1)S(1)}, bf16[256,256]{1,0:T(8,128)(2,1)S(1)}, u32[]{:S(2)}, u32[]{:S(2)}) collective-permute-start(bf16[256,256]{1,0:T(8,128)(2,1)S(1)} %convert_element_type.12.refs_0_), channel_id=1, source_target_pairs={{0,2},{1,3},{2,0},{3,1},{4,6},{5,7},{6,4},{7,5},{8,10},{9,11},{10,... | collective-permute-start | bytes 393224 | tf_op jit(solution)/shard_map/ppermute | solution.py:28
  8.8 3.4 %collective-permute-start.1 = (bf16[256,256]{1,0:T(8,128)(2,1)S(1)}, bf16[256,256]{1,0:T(8,128)(2,1)S(1)}, u32[]{:S(2)}, u32[]{:S(2)}) collective-permute-start(bf16[256,256]{1,0:T(8,128)(2,1)S(1)} %collective-permute-done.refs_0_.refs_2_), channel_id=1, source_target_pairs={{0,1},{1,0},{2,3},{3,2},{4,5},{5,4},{6,7},{7,6},{8,9},{9,8},{10,11... | collective-permute-start | bytes 393224 | tf_op jit(solution)/shard_map/ppermute | solution.py:28
  10.6 6.5 %collective-permute-start.3 = (f32[256,256]{1,0:T(8,128)S(1)}, f32[256,256]{1,0:T(8,128)S(1)}, u32[]{:S(2)}, u32[]{:S(2)}) collective-permute-start(f32[256,256]{1,0:T(8,128)S(1)} %get-tuple-element.38), channel_id=1, source_target_pairs={{0,1},{1,0},{2,3},{3,2},{4,5},{5,4},{6,7},{7,6},{8,9},{9,8},{10,11... | collective-permute-start | bytes 786440 | tf_op jit(solution)/shard_map/ppermute | solution.py:28
  12.1 5.0 %collective-permute-start.4 = (f32[256,256]{1,0:T(8,128)S(1)}, f32[256,256]{1,0:T(8,128)S(1)}, u32[]{:S(2)}, u32[]{:S(2)}) collective-permute-start(f32[256,256]{1,0:T(8,128)S(1)} %get-tuple-element.40), channel_id=1, source_target_pairs={{0,1},{1,0},{2,3},{3,2},{4,5},{5,4},{6,7},{7,6},{8,9},{9,8},{10,11... | collective-permute-start | bytes 786440 | tf_op jit(solution)/shard_map/ppermute | solution.py:28
  14.8 4.3 %copy-start.1 = (f32[256,256]{1,0:T(8,128)S(1)}, f32[256,256]{1,0:T(8,128)}, u32[]{:S(2)}) copy-start(f32[256,256]{1,0:T(8,128)} %param.7) | copy-start | bytes 786436
  17.2 5.8 %collective-permute-start.5 = (f32[128,256]{1,0:T(8,128)S(1)}, f32[128,256]{1,0:T(8,128)S(1)}, u32[]{:S(2)}, u32[]{:S(2)}) collective-permute-start(f32[128,256]{1,0:T(8,128)S(1)} %get-tuple-element.77), channel_id=1, source_target_pairs={{0,3},{1,2},{2,1},{3,0},{4,7},{5,6},{6,5},{7,4},{8,11},{9,10},{10,... | collective-permute-start | bytes 393224 | tf_op jit(solution)/shard_map/ppermute | solution.py:28
  19.1 6.3 %collective-permute-start.7 = (f32[128,256]{1,0:T(8,128)S(1)}, f32[128,256]{1,0:T(8,128)S(1)}, u32[]{:S(2)}, u32[]{:S(2)}) collective-permute-start(f32[128,256]{1,0:T(8,128)S(1)} %get-tuple-element.76), channel_id=1, source_target_pairs={{0,3},{1,2},{2,1},{3,0},{4,7},{5,6},{6,5},{7,4},{8,11},{9,10},{10,... | collective-permute-start | bytes 393224 | tf_op jit(solution)/shard_map/ppermute | solution.py:28
  23.0 8.4 %collective-permute-start.6 = (bf16[128,256]{1,0:T(8,128)(2,1)S(1)}, bf16[128,256]{1,0:T(8,128)(2,1)S(1)}, u32[]{:S(2)}, u32[]{:S(2)}) collective-permute-start(bf16[128,256]{1,0:T(8,128)(2,1)S(1)} %get-tuple-element.74), channel_id=1, source_target_pairs={{0,6},{1,7},{2,4},{3,5},{4,10},{5,11},{6,8},{7,9},{8,14},{9,15},{1... | collective-permute-start | bytes 196616 | tf_op jit(solution)/shard_map/ppermute | solution.py:28
  25.4 8.6 %collective-permute-start.9 = (bf16[128,256]{1,0:T(8,128)(2,1)S(1)}, bf16[128,256]{1,0:T(8,128)(2,1)S(1)}, u32[]{:S(2)}, u32[]{:S(2)}) collective-permute-start(bf16[128,256]{1,0:T(8,128)(2,1)S(1)} %get-tuple-element.72), channel_id=1, source_target_pairs={{0,6},{1,7},{2,4},{3,5},{4,10},{5,11},{6,8},{7,9},{8,14},{9,15},{1... | collective-permute-start | bytes 196616 | tf_op jit(solution)/shard_map/ppermute | solution.py:28
  31.4 1.3 %collective-permute-start.10 = (bf16[128,256]{1,0:T(8,128)(2,1)S(1)}, bf16[128,256]{1,0:T(8,128)(2,1)S(1)}, u32[]{:S(2)}, u32[]{:S(2)}) collective-permute-start(bf16[128,256]{1,0:T(8,128)(2,1)S(1)} %collective-permute-done.6.refs_0_), channel_id=1, source_target_pairs={{0,1},{1,0},{2,3},{3,2},{4,5},{5,4},{6,7},{7,6},{8,9},{9,8},{10,11... | collective-permute-start | bytes 196616 | tf_op jit(solution)/shard_map/ppermute | solution.py:28
  31.5 8.5 %collective-permute-start.8 = (bf16[256,256]{1,0:T(8,128)(2,1)S(1)}, bf16[256,256]{1,0:T(8,128)(2,1)S(1)}, u32[]{:S(2)}, u32[]{:S(2)}) collective-permute-start(bf16[256,256]{1,0:T(8,128)(2,1)S(1)} %pad_maximum_fusion.2), channel_id=1, source_target_pairs={{0,4},{1,5},{2,6},{3,7},{4,8},{5,9},{6,10},{7,11},{8,12},{9,13},{1... | collective-permute-start | bytes 393224 | tf_op jit(solution)/shard_map/ppermute | solution.py:28
  34.0 1.3 %collective-permute-start.11 = (bf16[128,256]{1,0:T(8,128)(2,1)S(1)}, bf16[128,256]{1,0:T(8,128)(2,1)S(1)}, u32[]{:S(2)}, u32[]{:S(2)}) collective-permute-start(bf16[128,256]{1,0:T(8,128)(2,1)S(1)} %collective-permute-done.9.refs_0_.refs_2_), channel_id=1, source_target_pairs={{0,1},{1,0},{2,3},{3,2},{4,5},{5,4},{6,7},{7,6},{8,9},{9,8},{10,11... | collective-permute-start | bytes 196616 | tf_op jit(solution)/shard_map/ppermute | solution.py:28
  40.1 1.3 %collective-permute-start.12 = (bf16[256,256]{1,0:T(8,128)(2,1)S(1)}, bf16[256,256]{1,0:T(8,128)(2,1)S(1)}, u32[]{:S(2)}, u32[]{:S(2)}) collective-permute-start(bf16[256,256]{1,0:T(8,128)(2,1)S(1)} %collective-permute-done.8.refs_0_.refs_4_), channel_id=1, source_target_pairs={{0,1},{1,0},{2,3},{3,2},{4,5},{5,4},{6,7},{7,6},{8,9},{9,8},{10,11... | collective-permute-start | bytes 393224 | tf_op jit(solution)/shard_map/ppermute | solution.py:28
  43.1 6.0 %collective-permute-start.14 = (f32[256,256]{1,0:T(8,128)S(1)}, f32[256,256]{1,0:T(8,128)S(1)}, u32[]{:S(2)}, u32[]{:S(2)}) collective-permute-start(f32[256,256]{1,0:T(8,128)S(1)} %get-tuple-element.62), channel_id=1, source_target_pairs={{0,1},{1,0},{2,3},{3,2},{4,5},{5,4},{6,7},{7,6},{8,9},{9,8},{10,11... | collective-permute-start | bytes 786440 | tf_op jit(solution)/shard_map/ppermute | solution.py:28
  43.3 11.3 %collective-permute-start.13 = (f32[256,256]{1,0:T(8,128)S(1)}, f32[256,256]{1,0:T(8,128)S(1)}, u32[]{:S(2)}, u32[]{:S(2)}) collective-permute-start(f32[256,256]{1,0:T(8,128)S(1)} %pad_maximum_fusion), channel_id=1, source_target_pairs={{0,4},{1,5},{2,6},{3,7},{4,8},{5,9},{6,10},{7,11},{8,12},{9,13},{1... | collective-permute-start | bytes 786440 | tf_op jit(solution)/shard_map/ppermute | solution.py:28
  43.3 1.6 %collective-permute-start.15 = (f32[128,256]{1,0:T(8,128)S(1)}, f32[128,256]{1,0:T(8,128)S(1)}, u32[]{:S(2)}, u32[]{:S(2)}) collective-permute-start(f32[128,256]{1,0:T(8,128)S(1)} %get-tuple-element.53), channel_id=1, source_target_pairs={{0,1},{1,0},{2,3},{3,2},{4,5},{5,4},{6,7},{7,6},{8,9},{9,8},{10,11... | collective-permute-start | bytes 393224 | tf_op jit(solution)/shard_map/ppermute | solution.py:28
  43.7 2.0 %collective-permute-start.17 = (f32[128,256]{1,0:T(8,128)S(1)}, f32[128,256]{1,0:T(8,128)S(1)}, u32[]{:S(2)}, u32[]{:S(2)}) collective-permute-start(f32[128,256]{1,0:T(8,128)S(1)} %get-tuple-element.57), channel_id=1, source_target_pairs={{0,1},{1,0},{2,3},{3,2},{4,5},{5,4},{6,7},{7,6},{8,9},{9,8},{10,11... | collective-permute-start | bytes 393224 | tf_op jit(solution)/shard_map/ppermute | solution.py:28
  44.9 9.7 %collective-permute-start.16 = (f32[128,256]{1,0:T(8,128)S(1)}, f32[128,256]{1,0:T(8,128)S(1)}, u32[]{:S(2)}, u32[]{:S(2)}) collective-permute-start(f32[128,256]{1,0:T(8,128)S(1)} %add.51), channel_id=1, source_target_pairs={{0,3},{1,2},{2,1},{3,0},{4,7},{5,6},{6,5},{7,4},{8,11},{9,10},{10,... | collective-permute-start | bytes 393224 | tf_op jit(solution)/shard_map/ppermute | solution.py:28
  45.7 9.0 %collective-permute-start.18 = (f32[128,256]{1,0:T(8,128)S(1)}, f32[128,256]{1,0:T(8,128)S(1)}, u32[]{:S(2)}, u32[]{:S(2)}) collective-permute-start(f32[128,256]{1,0:T(8,128)S(1)} %add.54), channel_id=1, source_target_pairs={{0,3},{1,2},{2,1},{3,0},{4,7},{5,6},{6,5},{7,4},{8,11},{9,10},{10,... | collective-permute-start | bytes 393224 | tf_op jit(solution)/shard_map/ppermute | solution.py:28

commit v3 on v2

v3 whole, which is shorter than its diff:
```python
import functools

import jax
import jax.numpy as jnp
from jax import lax
from jax.experimental import pallas as pl
from jax.experimental.pallas import tpu as pltpu
from jax.sharding import PartitionSpec as P


F32 = jnp.float32
BF16 = jnp.bfloat16
VMEM = pl.BlockSpec(memory_space=pltpu.VMEM)
HBM = pl.BlockSpec(memory_space=pltpu.HBM)
BOTH_ROWS = (((0,), (0,)), ((), ()))
MIB = 1 << 20
CHUNK_TILES = 4
LATENCY_SCALE = 3


def route(block, strata_shift, users_flip):
    strata, users = lax.axis_size("strata"), lax.axis_size("users")
    pairs = [
        (s * users + u, ((s + strata_shift) % strata) * users + (u ^ users_flip))
        for s in range(strata)
        for u in range(users)
    ]
    return lax.ppermute(block, ("strata", "users"), pairs)


def lower_users(users, rows, low_ref, low_t_ref):
    low = users.astype(BF16)
    low_ref[rows, :] = low
    low_t_ref[:, rows] = low.T


def low_shapes(users):
    return [jax.ShapeDtypeStruct(users.shape, BF16), jax.ShapeDtypeStruct(users.shape[::-1], BF16)]


def lower_kernel(chunk, users_ref, low_ref, low_t_ref):
    for i in range(users_ref.shape[0] // chunk):
        rows = slice(i * chunk, (i + 1) * chunk)
        lower_users(users_ref[rows, :], rows, low_ref, low_t_ref)


def lower(users, tile):
    return pl.pallas_call(
        functools.partial(lower_kernel, tile),
        out_shape=low_shapes(users),
        in_specs=[VMEM],
        out_specs=[VMEM] * 2,
        compiler_params=pltpu.CompilerParams(vmem_limit_bytes=8 * MIB),
        cost_estimate=pl.CostEstimate(flops=10**8, bytes_accessed=MIB, transcendentals=0),
        name="lower",
    )(users)


def rating_copies(ratings_hbm, step, tiles, arrived):
    group = tiles.shape[0] // arrived.shape[0]
    return [
        pltpu.make_async_copy(
            ratings_hbm.at[0, 0, step, pl.ds(g * group, group)],
            tiles.at[pl.ds(g * group, group)],
            arrived.at[g],
        )
        for g in range(arrived.shape[0])
    ]


def dense_kernel(step, tiles_per_shard, group, fetched, counts_hbm, rows_hbm, columns_hbm, ratings, dense_ref, *scratch):
    *lists, listed = scratch if fetched else scratch[2:]
    tiles = ratings.at[0, 0, step] if fetched else scratch[0]
    counts_ref, rows_ref, columns_ref = lists
    flip = lax.axis_index("users") * tiles_per_shard
    copies = [
        pltpu.make_async_copy(source, target, listed.at[k])
        for k, (source, target) in enumerate(zip((counts_hbm, rows_hbm, columns_hbm), lists))
    ]
    for copy in copies:
        copy.start()
    if not fetched:
        for copy in rating_copies(ratings, step, tiles, scratch[1]):
            copy.start()

    @pl.loop(0, dense_ref.shape[0])
    def _(j):
        dense_ref[j] = jnp.zeros(dense_ref.shape[1:], BF16)

    for copy in copies:
        copy.wait()
    count = counts_ref[0, 0, step]

    def place(g):
        @pl.when(g * group < count)
        def _():
            for k in range(group):
                m = g * group + k
                j = columns_ref[0, 0, step, m] ^ flip
                r = rows_ref[0, 0, step, m]
                rating = jnp.where(m < count, tiles[m], 0)
                dense_ref[j, r] = rating.astype(F32).astype(BF16).T

    @pl.loop(0, tiles.shape[0] // group)
    def _(g):
        if not fetched:
            some = pl.ds(g * group, group)
            pltpu.make_async_copy(ratings.at[0, 0, step, some], tiles.at[some], scratch[1].at[g]).wait()
        place(g)


def slot_group(slots):
    return 8 if slots % 8 == 0 else 1


def in_hbm(*arrays):
    return [pltpu.with_memory_space_constraint(array, pltpu.HBM) for array in arrays]


def dense_ratings(
    step, tiles_per_shard, column_tiles, user_rows, tile_rows, tile_columns, tile_counts, ratings, fetched=False
):
    slots, tile = ratings.shape[3], ratings.shape[4]
    group = slot_group(slots)
    lists = (tile_counts, tile_rows, tile_columns)
    scratch = [pltpu.SMEM(some.shape, jnp.int32) for some in lists] + [pltpu.SemaphoreType.DMA((3,))]
    if not fetched:
        scratch = [
            pltpu.VMEM((slots, tile, tile), jnp.int32), pltpu.SemaphoreType.DMA((slots // group,)), *scratch
        ]
        operands, last_spec = in_hbm(*lists, ratings), HBM
    else:
        operands, last_spec = [*in_hbm(*lists), ratings], VMEM
    return pl.pallas_call(
        functools.partial(dense_kernel, step, tiles_per_shard, group, fetched),
        out_shape=jax.ShapeDtypeStruct((column_tiles, user_rows // tile, tile, tile), BF16),
        in_specs=[HBM] * 3 + [last_spec],
        out_specs=VMEM,
        scratch_shapes=scratch,
        compiler_params=pltpu.CompilerParams(vmem_limit_bytes=12 * MIB),
        cost_estimate=pl.CostEstimate(flops=2 * 10**9, bytes_accessed=8 * MIB, transcendentals=0),
    )(*operands)


def terms_kernel(columns, sizes, chunk, users_ref, users_t_ref, dense_ref, *refs):
    item_refs, (residual_ref, *grad_refs) = refs[: len(refs) - 1 - len(sizes)], refs[-1 - len(sizes) :]
    tile = dense_ref.shape[-1]
    per_chunk = chunk // tile
    items = jnp.concatenate([ref[...] for ref in item_refs], axis=0)
    chunks = users_ref.shape[0] // chunk

    def users(i):
        return users_ref[i * chunk : (i + 1) * chunk, :]

    def predict(i):
        users_t = users_t_ref[:, i * chunk : (i + 1) * chunk]
        return jnp.dot(items, users_t, preferred_element_type=F32)

    grad = None
    ahead = predict(0)
    for i in range(chunks):
        predicted = ahead
        if i + 1 < chunks:
            ahead = predict(i + 1)
        residuals = []
        for q in range(per_chunk):
            r = i * per_chunk + q
            rating = jnp.concatenate([dense_ref[j, r] for j in columns], axis=0).astype(F32)
            residual = jnp.where(
                rating > 0, rating - predicted[:, q * tile : (q + 1) * tile], 0.0
            ).astype(BF16)
            residual_ref[r] = residual
            residuals.append(residual)
        part = jnp.dot(jnp.concatenate(residuals, axis=1), users(i), preferred_element_type=F32)
        grad = part if grad is None else grad + part
    start = 0
    for ref in grad_refs:
        ref[...] = grad[start : start + ref.shape[0]]
        start += ref.shape[0]


def terms(columns, sizes, lowered, dense, items):
    user_rows, width = lowered[0].shape
    tile = dense.shape[-1]
    rows = tile * len(columns)
    return pl.pallas_call(
        functools.partial(terms_kernel, columns, sizes, min(CHUNK_TILES * tile, user_rows)),
        out_shape=[jax.ShapeDtypeStruct((user_rows // tile, rows, tile), BF16)]
        + [jax.ShapeDtypeStruct((size, width), F32) for size in sizes],
        in_specs=[VMEM] * (3 + len(items)),
        out_specs=[VMEM] * (1 + len(sizes)),
        compiler_params=pltpu.CompilerParams(vmem_limit_bytes=16 * MIB),
        cost_estimate=pl.CostEstimate(
            flops=LATENCY_SCALE * 4 * user_rows * rows * width, bytes_accessed=MIB, transcendentals=0
        ),
    )(*lowered, dense, *items)


def users_kernel(number, chunk, last, users_ref, *refs):
    item_refs, refs = refs[:number], refs[number:]
    items = jnp.concatenate([ref[...] for ref in item_refs], axis=0)
    tile = refs[0].shape[-1]
    copies = []
    if last:
        *residual_refs, out_hbm, out_ref, sent = refs
    else:
        *residual_refs, out_ref, low_ref, low_t_ref = refs
    for i in range(users_ref.shape[0] // chunk):
        rows = slice(i * chunk, (i + 1) * chunk)
        residual = jnp.concatenate(
            [
                jnp.concatenate([ref[r] for ref in residual_refs], axis=0)
                for r in range(i * chunk // tile, (i + 1) * chunk // tile)
            ],
            axis=1,
        )
        total = lax.dot_general(residual, items, BOTH_ROWS, preferred_element_type=F32)
        users = users_ref[rows, :]
        updated = users + 0.01 * (total - 0.05 * users)
        out_ref[rows, :] = updated
        if last:
            copies.append(pltpu.make_async_copy(out_ref.at[rows], out_hbm.at[rows], sent.at[i]))
            copies[-1].start()
        else:
            lower_users(updated, rows, low_ref, low_t_ref)
    for copy in copies:
        copy.wait()


def update_users(users, items, residuals, last):
    user_rows, width = users.shape
    tile = residuals[0].shape[-1]
    chunk = min(2 * tile, user_rows)
    item_rows = sum(block.shape[0] for block in items)
    full = jax.ShapeDtypeStruct(users.shape, F32)
    if last:
        out_shape, out_specs = [full], [HBM]
        scratch = [pltpu.VMEM(users.shape, F32), pltpu.SemaphoreType.DMA((user_rows // chunk,))]
    else:
        out_shape, out_specs, scratch = [full, *low_shapes(users)], [VMEM] * 3, []
    return pl.pallas_call(
        functools.partial(users_kernel, len(items), chunk, last),
        out_shape=out_shape,
        in_specs=[VMEM] * (1 + len(items) + len(residuals)),
        out_specs=out_specs,
        scratch_shapes=scratch,
        compiler_params=pltpu.CompilerParams(vmem_limit_bytes=12 * MIB),
        cost_estimate=pl.CostEstimate(
            flops=LATENCY_SCALE * 2 * user_rows * item_rows * width, bytes_accessed=4 * MIB, transcendentals=0
        ),
        name="users",
    )(users, *items, *residuals)


def updated_items(items, grad):
    return items + 0.003 * (grad - 0.05 * items)


def after(value, *earlier):
    return lax.optimization_barrier((value, *earlier))[0]


def paired_shards(user_factors, item_factors, tile_rows, tile_columns, tile_counts, ratings):
    step_total, tile = ratings.shape[2], ratings.shape[-1]
    per_shard = item_factors.shape[0] // tile
    column_tiles = per_shard * lax.axis_size("users")
    parts_rows = [slice(h * tile, (h + 1) * tile) for h in range(per_shard)]
    low = item_factors.astype(BF16)
    users_now, items_now = user_factors, item_factors
    held = {0: [low], 1: [route(low, 0, 1)], 2: [route(low, 0, 2)]}
    mark = []

    def ratings_of(step):
        dense = dense_ratings(
            step, per_shard, column_tiles, user_factors.shape[0],
            after(tile_rows, *mark), tile_columns, tile_counts, ratings, step > 0,
        )
        mark[:] = [dense]
        return dense

    dense = ratings_of(0)
    lowered = lower(after(user_factors, dense), tile)
    mark[:] = lowered[:1]
    for step in range(step_total):
        last = step == step_total - 1
        items_in, residuals, sums = [], [], []

        def run(d, block, first=0):
            blocks = block if isinstance(block, list) else [block]
            sizes = tuple(some.shape[0] for some in blocks)
            columns = tuple(
                (d + i) * per_shard + first + k for i, size in enumerate(sizes) for k in range(size // tile)
            )
            residual, *grads = terms(
                columns, sizes, lowered, dense, [after(blocks[0], *mark), *blocks[1:]]
            )
            mark[:] = grads[-1:]
            items_in.extend(blocks)
            residuals.append(residual)
            return grads

        def near():
            own, passed = run(0, [held[0][0], held[1][0]])
            return own + route(passed, 0, 1)

        if step == 0:
            near_sum = near()
        for p, block in enumerate(held[2]):
            first = p * block.shape[0] // tile
            shared = route(after(block, *mark), 0, 1)
            (passed,) = run(2, block, first)
            passed = route(passed, 0, 1)
            if step > 0 and p == len(held[2]) - 1:
                held[1] = [route(after(held[0][0], *mark), 0, 1)]
            for k in range(block.shape[0] // tile):
                h, rows = first + k, parts_rows[k]
                (own,) = run(3, shared[rows], h)
                own = lax.optimization_barrier(own + passed[rows])
                mark.append(own)
                sums.append(route(own, 0, 3))
        if step > 0:
            near_sum = near()
        blocks = list(items_in)
        blocks[0] = after(blocks[0], *mark)
        users_now, *lowered = update_users(users_now, blocks, residuals, last)
        if last:
            return users_now, updated_items(items_now, near_sum + jnp.concatenate(sums, axis=0))
        mark[:] = lowered[:1]
        dense = ratings_of(step + 1)
        parts, low_parts = [], []
        for h, rows in enumerate(parts_rows):
            base = updated_items(items_now[rows], after(near_sum, *parts)[rows])
            parts.append(lax.optimization_barrier(base) + 0.003 * sums[h])
            low_parts.append(parts[h].astype(BF16))
        held = {2: [route(low, 1, 2) for low in low_parts]}
        held[0] = [route(jnp.concatenate(low_parts, axis=0), 1, 0)]
        items_now = after(jnp.concatenate(parts, axis=0), *mark)
        items_now = route(items_now, 1, 0)


def gathered_shards(user_factors, item_factors, tile_rows, tile_columns, tile_counts, ratings):
    step_total, tile = ratings.shape[2], ratings.shape[-1]
    users_now, item_part = user_factors, item_factors
    for step in range(step_total):
        block = lax.all_gather(item_part.astype(BF16), "users", axis=0, tiled=True)
        column_tiles = block.shape[0] // tile
        dense = dense_ratings(
            step, 0, column_tiles, users_now.shape[0], tile_rows, tile_columns, tile_counts, ratings
        )
        lowered = lower(users_now, tile)
        residual, grad = terms(tuple(range(column_tiles)), block.shape[:1], lowered, dense, [block])
        grad_part = lax.psum_scatter(grad, "users", scatter_dimension=0, tiled=True)
        users_now = update_users(users_now, [block], [residual], True)[0]
        item_part = updated_items(item_part, grad_part)
        if step < step_total - 1:
            item_part = route(item_part, 1, 0)
    return users_now, item_part


def solution(mesh):
    placed = (
        P(("strata", "users"), None),
        P(("strata", "users"), None),
        P("strata", "users", None, None),
        P("strata", "users", None, None),
        P("strata", "users", None),
        P("strata", "users", None, None, None, None),
    )

    def shards(user_factors, item_factors, *lists):
        tile = lists[-1].shape[-1]
        paired = mesh.shape["users"] == 4 and item_factors.shape[0] % tile == 0
        body = paired_shards if paired else gathered_shards
        return body(user_factors, item_factors, *lists)

    return jax.shard_map(
        shards,
        mesh=mesh,
        in_specs=placed,
        out_specs=(P(("strata", "users"), None), P(("strata", "users"), None)),
        check_vma=False,
    )
```

time: 55.6 us -> 51.3 us (0.923)
  waiting for transfers between devices: 22.5 us -> 18.2 us
  Pallas kernels: 16.6 us -> 15.8 us
    ppermute x19, waiting for transfers between devices: 22.5 us -> 18.2 us  [route(): return lax.ppermute(block, ('strata', 'users'), pairs)]
    pallas_call x2, Pallas kernels: 4.53 us -> 3.42 us  [dense_ratings(): pl.pallas_call(functools.partial(dense_kernel, step, tiles_per_shard, gro...]
    add x4 -> x3, other arithmetic: 0.11 us -> 0.83 us  [updated_items(): return items + 0.003 * (grad - 0.05 * items)]
    concatenate x2 -> x1, other arithmetic: 0.74 us -> 0.02 us  [paired_shards(): items_now = after(jnp.concatenate(parts, axis=0), *mark)]
    pallas_call x10 -> x12, Pallas kernels: 12.1 us -> 12.4 us  [the longest x9 7.92 us: terms(): pl.pallas_call(functools.partial(terms_kernel, columns, sizes, min(CHUNK_...]
  transfers between devices with their start and end apart: 19 -> 19, of which waited for: 11 -> 6; matrix products, arithmetic and copies ran while one was open for 1% -> 0% of each run, Pallas kernels for 27% -> 31%
where the time goes in v3:
time: 51.3 us; the launch traced here: 51.1 us
  waiting for transfers between devices  18.2 us (35%)
  Pallas kernels  15.8 us (31%)
  starting transfers between devices  13.8 us (27%)
  other arithmetic  1.96 us (4%)
  between operations  0.91 us (2%)
    ppermute x19, waiting for transfers between devices, route(): return lax.ppermute(block, ('strata', 'users'), pairs)  18.2 us
    ppermute x19, starting transfers between devices, route(): return lax.ppermute(block, ('strata', 'users'), pairs)  13.8 us
    pallas_call x9, Pallas kernels, terms(): pl.pallas_call(functools.partial(terms_kernel, columns, sizes, min(CHUNK_...  7.92 us
    pallas_call x2, Pallas kernels, update_users(): pl.pallas_call(functools.partial(users_kernel, len(items), chunk, last),...  4.04 us
    pallas_call x2, Pallas kernels, dense_ratings(): pl.pallas_call(functools.partial(dense_kernel, step, tiles_per_shard, gro...  3.42 us
  transfers between devices with their start and end apart: 19, of which 6 were waited for; matrix products, arithmetic and copies ran while one was open for 0% of the time, Pallas kernels for 31%

profile of v3, /device:TPU:0, one launch (start us, length us, event | category | flops | bytes accessed | tf_op | source)
XLA Modules:
  0.0 51.1 jit_solution(16505515006816817185)
XLA Ops:
  0.6 1.0 %convert_element_type.9.refs_0_ = bf16[256,256]{1,0:T(8,128)(2,1)S(1)} convert(f32[256,256]{1,0:T(8,128)} %param.7) | non-fusion elementwise | flops 65536 | bytes 393216 | tf_op jit(solution)/shard_map/convert_element_type | solution.py:268
  1.6 0.0 copy-start
  1.6 0.6 %collective-permute-start.1 = (bf16[256,256]{1,0:T(8,128)(2,1)S(1)}, bf16[256,256]{1,0:T(8,128)(2,1)S(1)}, u32[]{:S(2)}, u32[]{:S(2)}) collective-permute-start(bf16[256,256]{1,0:T(8,128)(2,1)S(1)} %convert_element_type.9.refs_0_), channel_id=1, source_target_pairs={{0,1},{1,0},{2,3},{3,2},{4,5},{5,4},{6,7},{7,6},{8,9},{9,8},{10,11... | collective-permute-start | bytes 393224 | tf_op jit(solution)/shard_map/ppermute | solution.py:28
  2.2 2.6 %collective-permute-start = (bf16[256,256]{1,0:T(8,128)(2,1)S(1)}, bf16[256,256]{1,0:T(8,128)(2,1)S(1)}, u32[]{:S(2)}, u32[]{:S(2)}) collective-permute-start(bf16[256,256]{1,0:T(8,128)(2,1)S(1)} %convert_element_type.9.refs_0_), channel_id=1, source_target_pairs={{0,2},{1,3},{2,0},{3,1},{4,6},{5,7},{6,4},{7,5},{8,10},{9,11},{10,... | collective-permute-start | bytes 393224 | tf_op jit(solution)/shard_map/ppermute | solution.py:28
  4.8 2.2 %shard_map.77.dense_ref = bf16[8,16,128,128]{3,2,1,0:T(8,128)(2,1)S(1)} custom-call(s32[1,1,2]{2,1,0:T(1,128)} %counts_hbm.3, s32[1,1,2,64]{3,2,1,0:T(2,128)} %rows_hbm.1, s32[1,1,2,64]{3,2,1,0:T(2,128)} %columns_hbm.3, s32[1,1,2,64,128,128]{5,4,3,2,1,0:T(8,128)} %ratings.3), custom_call_target="tpu_custom_call" | custom-call | flops 2000000000 | bytes 8388608 | tf_op jit(solution)/shard_map/pallas_call | solution.py:134
  7.0 0.0 copy-done
  7.0 0.4 lower.1
  7.4 0.0 collective-permute-done.1.refs_1_
  7.4 1.6 %shard_map.78 = (bf16[16,512,128]{2,1,0:T(8,128)(2,1)S(1)}, f32[256,256]{1,0:T(8,128)S(1)}, f32[256,256]{1,0:T(8,128)S(1)}) custom-call(bf16[2048,256]{1,0:T(8,128)(2,1)S(1)} %get-tuple-element.44.users_ref, bf16[256,2048]{1,0:T(8,128)(2,1)S(1)} %get-tuple-element.45.users_t_ref, bf16[8,16,128,128]{3,2,1,0:T(8,128)(2,1)S(1)} %shard_map.77.dense_ref, ...), custom_call_target="tpu_custom_call" | custom-call | flops 3221225472 | bytes 1048576 | tf_op jit(solution)/shard_map/pallas_call | solution.py:186
  9.1 0.2 collective-permute-start.4
  9.3 0.0 collective-permute-done.refs_0_.refs_2_
  9.3 0.4 collective-permute-start.2
  9.7 1.0 %shard_map.79 = (bf16[16,256,128]{2,1,0:T(8,128)(2,1)S(1)}, f32[256,256]{1,0:T(8,128)S(1)}) custom-call(bf16[2048,256]{1,0:T(8,128)(2,1)S(1)} %get-tuple-element.44.users_ref, bf16[256,2048]{1,0:T(8,128)(2,1)S(1)} %get-tuple-element.45.users_t_ref, bf16[8,16,128,128]{3,2,1,0:T(8,128)(2,1)S(1)} %shard_map.77.dense_ref, ...), custom_call_target="tpu_custom_call" | custom-call | flops 1610612736 | bytes 1048576 | tf_op jit(solution)/shard_map/pallas_call | solution.py:186
  10.6 0.2 collective-permute-start.3
  10.8 0.0 collective-permute-done.2
  10.9 0.6 %shard_map.80 = (bf16[16,128,128]{2,1,0:T(8,128)(2,1)S(1)}, f32[128,256]{1,0:T(8,128)S(1)}) custom-call(bf16[2048,256]{1,0:T(8,128)(2,1)S(1)} %get-tuple-element.44.users_ref, bf16[256,2048]{1,0:T(8,128)(2,1)S(1)} %get-tuple-element.45.users_t_ref, bf16[8,16,128,128]{3,2,1,0:T(8,128)(2,1)S(1)} %shard_map.77.dense_ref, ...), custom_call_target="tpu_custom_call" | custom-call | flops 805306368 | bytes 1048576 | tf_op jit(solution)/shard_map/pallas_call | solution.py:186
  11.5 0.7 %collective-permute-done.3 = f32[256,256]{1,0:T(8,128)S(1)} collective-permute-done((f32[256,256]{1,0:T(8,128)S(1)}, f32[256,256]{1,0:T(8,128)S(1)}, u32[]{:S(2)}, u32[]{:S(2)}) %collective-permute-start.3) | collective-permute-done | bytes 262176 | tf_op jit(solution)/shard_map/ppermute | solution.py:28
  12.2 0.0 copy-start.1
  12.3 0.0 slice-start
  12.3 0.6 %shard_map.81 = (bf16[16,128,128]{2,1,0:T(8,128)(2,1)S(1)}, f32[128,256]{1,0:T(8,128)S(1)}) custom-call(bf16[2048,256]{1,0:T(8,128)(2,1)S(1)} %get-tuple-element.44.users_ref, bf16[256,2048]{1,0:T(8,128)(2,1)S(1)} %get-tuple-element.45.users_t_ref, bf16[8,16,128,128]{3,2,1,0:T(8,128)(2,1)S(1)} %shard_map.77.dense_ref, ...), custom_call_target="tpu_custom_call" | custom-call | flops 805306368 | bytes 1048576 | tf_op jit(solution)/shard_map/pallas_call | solution.py:186
  12.9 1.1 %collective-permute-start.7 = (f32[128,256]{1,0:T(8,128)S(1)}, f32[128,256]{1,0:T(8,128)S(1)}, u32[]{:S(2)}, u32[]{:S(2)}) collective-permute-start(f32[128,256]{1,0:T(8,128)S(1)} %slice_add_fusion), channel_id=1, source_target_pairs={{0,3},{1,2},{2,1},{3,0},{4,7},{5,6},{6,5},{7,4},{8,11},{9,10},{10,... | collective-permute-start | bytes 393224 | tf_op jit(solution)/shard_map/ppermute | solution.py:28
  14.0 0.7 %collective-permute-start.5 = (f32[128,256]{1,0:T(8,128)S(1)}, f32[128,256]{1,0:T(8,128)S(1)}, u32[]{:S(2)}, u32[]{:S(2)}) collective-permute-start(f32[128,256]{1,0:T(8,128)S(1)} %slice_add_fusion.1), channel_id=1, source_target_pairs={{0,3},{1,2},{2,1},{3,0},{4,7},{5,6},{6,5},{7,4},{8,11},{9,10},{10,... | collective-permute-start | bytes 393224 | tf_op jit(solution)/shard_map/ppermute | solution.py:28
  14.7 0.0 collective-permute-done.4
  14.8 0.0 copy-done.1
  14.8 0.0 slice-start.1
  14.8 1.8 %users.2 = (f32[2048,256]{1,0:T(8,128)S(1)}, bf16[2048,256]{1,0:T(8,128)(2,1)S(1)}, bf16[256,2048]{1,0:T(8,128)(2,1)S(1)}) custom-call(f32[2048,256]{1,0:T(8,128)S(1)} %copy-done, bf16[256,256]{1,0:T(8,128)(2,1)S(1)} %convert_element_type.9.refs_0_, bf16[256,256]{1,0:T(8,128)(2,1)S(1)} %collective-permute-done.1.refs_1_, ...), custom_call_target="tpu_custom_call" | custom-call | flops 3221225472 | bytes 4194304 | tf_op jit(solution)/shard_map/users/pallas_call | solution.py:241
  16.6 0.0 slice-done
  16.6 0.4 slice-done.1
  17.0 1.2 %shard_map.82.dense_ref = bf16[8,16,128,128]{3,2,1,0:T(8,128)(2,1)S(1)} custom-call(s32[1,1,2]{2,1,0:T(1,128)} %counts_hbm.3, s32[1,1,2,64]{3,2,1,0:T(2,128)} %rows_hbm.1, s32[1,1,2,64]{3,2,1,0:T(2,128)} %columns_hbm.3, s32[1,1,2,64,128,128]{5,4,3,2,1,0:T(8,128)S(1)} %bitcast.1), custom_call_target="tpu_custom_call" | custom-call | flops 2000000000 | bytes 8388608 | tf_op jit(solution)/shard_map/pallas_call | solution.py:134
  18.2 3.1 %collective-permute-done.5 = f32[128,256]{1,0:T(8,128)S(1)} collective-permute-done((f32[128,256]{1,0:T(8,128)S(1)}, f32[128,256]{1,0:T(8,128)S(1)}, u32[]{:S(2)}, u32[]{:S(2)}) %collective-permute-start.5) | collective-permute-done | bytes 131104 | tf_op jit(solution)/shard_map/ppermute | solution.py:28
  21.3 1.8 %collective-permute-start.6 = (bf16[128,256]{1,0:T(8,128)(2,1)S(1)}, bf16[128,256]{1,0:T(8,128)(2,1)S(1)}, u32[]{:S(2)}, u32[]{:S(2)}) collective-permute-start(bf16[128,256]{1,0:T(8,128)(2,1)S(1)} %get-tuple-element.86), channel_id=1, source_target_pairs={{0,6},{1,7},{2,4},{3,5},{4,10},{5,11},{6,8},{7,9},{8,14},{9,15},{1... | collective-permute-start | bytes 196616 | tf_op jit(solution)/shard_map/ppermute | solution.py:28
  23.1 0.0 collective-permute-done.7
  23.2 2.2 %collective-permute-start.9 = (bf16[128,256]{1,0:T(8,128)(2,1)S(1)}, bf16[128,256]{1,0:T(8,128)(2,1)S(1)}, u32[]{:S(2)}, u32[]{:S(2)}) collective-permute-start(bf16[128,256]{1,0:T(8,128)(2,1)S(1)} %get-tuple-element.84), channel_id=1, source_target_pairs={{0,6},{1,7},{2,4},{3,5},{4,10},{5,11},{6,8},{7,9},{8,14},{9,15},{1... | collective-permute-start | bytes 196616 | tf_op jit(solution)/shard_map/ppermute | solution.py:28
  25.4 3.8 %collective-permute-done.6.refs_0_ = bf16[128,256]{1,0:T(8,128)(2,1)S(1)} collective-permute-done((bf16[128,256]{1,0:T(8,128)(2,1)S(1)}, bf16[128,256]{1,0:T(8,128)(2,1)S(1)}, u32[]{:S(2)}, u32[]{:S(2)}) %collective-permute-start.6) | collective-permute-done | bytes 65568 | tf_op jit(solution)/shard_map/ppermute | solution.py:28
  29.2 0.0 collective-permute-start.10
  29.2 0.6 %shard_map.83 = (bf16[16,128,128]{2,1,0:T(8,128)(2,1)S(1)}, f32[128,256]{1,0:T(8,128)S(1)}) custom-call(bf16[2048,256]{1,0:T(8,128)(2,1)S(1)} %get-tuple-element.61.users_ref, bf16[256,2048]{1,0:T(8,128)(2,1)S(1)} %get-tuple-element.62.users_t_ref, bf16[8,16,128,128]{3,2,1,0:T(8,128)(2,1)S(1)} %shard_map.82.dense_ref, ...), custom_call_target="tpu_custom_call" | custom-call | flops 805306368 | bytes 1048576 | tf_op jit(solution)/shard_map/pallas_call | solution.py:186
  29.9 0.6 %collective-permute-start.11 = (f32[128,256]{1,0:T(8,128)S(1)}, f32[128,256]{1,0:T(8,128)S(1)}, u32[]{:S(2)}, u32[]{:S(2)}) collective-permute-start(f32[128,256]{1,0:T(8,128)S(1)} %get-tuple-element.66), channel_id=1, source_target_pairs={{0,1},{1,0},{2,3},{3,2},{4,5},{5,4},{6,7},{7,6},{8,9},{9,8},{10,11... | collective-permute-start | bytes 393224 | tf_op jit(solution)/shard_map/ppermute | solution.py:28
  30.4 0.1 collective-permute-start.8
  30.5 0.0 collective-permute-done.10.refs_0_.refs_1_
  30.5 0.6 %shard_map.84 = (bf16[16,128,128]{2,1,0:T(8,128)(2,1)S(1)}, f32[128,256]{1,0:T(8,128)S(1)}) custom-call(bf16[2048,256]{1,0:T(8,128)(2,1)S(1)} %get-tuple-element.61.users_ref, bf16[256,2048]{1,0:T(8,128)(2,1)S(1)} %get-tuple-element.62.users_t_ref, bf16[8,16,128,128]{3,2,1,0:T(8,128)(2,1)S(1)} %shard_map.82.dense_ref, ...), custom_call_target="tpu_custom_call" | custom-call | flops 805306368 | bytes 1048576 | tf_op jit(solution)/shard_map/pallas_call | solution.py:186
  31.1 0.3 collective-permute-done.11
  31.4 0.0 collective-permute-done.9.refs_0_.refs_2_
  31.4 0.4 collective-permute-start.12
  31.9 0.6 %shard_map.85 = (bf16[16,128,128]{2,1,0:T(8,128)(2,1)S(1)}, f32[128,256]{1,0:T(8,128)S(1)}) custom-call(bf16[2048,256]{1,0:T(8,128)(2,1)S(1)} %get-tuple-element.61.users_ref, bf16[256,2048]{1,0:T(8,128)(2,1)S(1)} %get-tuple-element.62.users_t_ref, bf16[8,16,128,128]{3,2,1,0:T(8,128)(2,1)S(1)} %shard_map.82.dense_ref, ...), custom_call_target="tpu_custom_call" | custom-call | flops 805306368 | bytes 1048576 | tf_op jit(solution)/shard_map/pallas_call | solution.py:186
  32.5 0.2 collective-permute-start.13
  32.7 5.9 %collective-permute-done.8.refs_0_.refs_4_ = bf16[256,256]{1,0:T(8,128)(2,1)S(1)} collective-permute-done((bf16[256,256]{1,0:T(8,128)(2,1)S(1)}, bf16[256,256]{1,0:T(8,128)(2,1)S(1)}, u32[]{:S(2)}, u32[]{:S(2)}) %collective-permute-start.8) | collective-permute-done | bytes 131104 | tf_op jit(solution)/shard_map/ppermute | solution.py:28
  38.6 0.0 collective-permute-start.14
  38.6 0.2 collective-permute-start.15
  38.9 1.1 %collective-permute-start.17 = (f32[128,256]{1,0:T(8,128)S(1)}, f32[128,256]{1,0:T(8,128)S(1)}, u32[]{:S(2)}, u32[]{:S(2)}) collective-permute-start(f32[128,256]{1,0:T(8,128)S(1)} %add.43), channel_id=1, source_target_pairs={{0,3},{1,2},{2,1},{3,0},{4,7},{5,6},{6,5},{7,4},{8,11},{9,10},{10,... | collective-permute-start | bytes 393224 | tf_op jit(solution)/shard_map/ppermute | solution.py:28
  40.0 0.0 collective-permute-done.12.refs_0_.refs_3_
  40.0 0.6 %shard_map.86 = (bf16[16,128,128]{2,1,0:T(8,128)(2,1)S(1)}, f32[128,256]{1,0:T(8,128)S(1)}) custom-call(bf16[2048,256]{1,0:T(8,128)(2,1)S(1)} %get-tuple-element.61.users_ref, bf16[256,2048]{1,0:T(8,128)(2,1)S(1)} %get-tuple-element.62.users_t_ref, bf16[8,16,128,128]{3,2,1,0:T(8,128)(2,1)S(1)} %shard_map.82.dense_ref, ...), custom_call_target="tpu_custom_call" | custom-call | flops 805306368 | bytes 1048576 | tf_op jit(solution)/shard_map/pallas_call | solution.py:186
  40.6 0.0 collective-permute-done.13
  40.7 0.8 %collective-permute-start.18 = (f32[128,256]{1,0:T(8,128)S(1)}, f32[128,256]{1,0:T(8,128)S(1)}, u32[]{:S(2)}, u32[]{:S(2)}) collective-permute-start(f32[128,256]{1,0:T(8,128)S(1)} %add.44), channel_id=1, source_target_pairs={{0,3},{1,2},{2,1},{3,0},{4,7},{5,6},{6,5},{7,4},{8,11},{9,10},{10,... | collective-permute-start | bytes 393224 | tf_op jit(solution)/shard_map/ppermute | solution.py:28
  41.4 0.0 collective-permute-done.14.refs_1_.refs_5_
  41.4 1.6 %shard_map.87 = (bf16[16,512,128]{2,1,0:T(8,128)(2,1)S(1)}, f32[256,256]{1,0:T(8,128)S(1)}, f32[256,256]{1,0:T(8,128)S(1)}) custom-call(bf16[2048,256]{1,0:T(8,128)(2,1)S(1)} %get-tuple-element.61.users_ref, bf16[256,2048]{1,0:T(8,128)(2,1)S(1)} %get-tuple-element.62.users_t_ref, bf16[8,16,128,128]{3,2,1,0:T(8,128)(2,1)S(1)} %shard_map.82.dense_ref, ...), custom_call_target="tpu_custom_call" | custom-call | flops 3221225472 | bytes 1048576 | tf_op jit(solution)/shard_map/pallas_call | solution.py:186
  43.1 0.6 %collective-permute-start.16 = (f32[256,256]{1,0:T(8,128)S(1)}, f32[256,256]{1,0:T(8,128)S(1)}, u32[]{:S(2)}, u32[]{:S(2)}) collective-permute-start(f32[256,256]{1,0:T(8,128)S(1)} %get-tuple-element.75), channel_id=1, source_target_pairs={{0,1},{1,0},{2,3},{3,2},{4,5},{5,4},{6,7},{7,6},{8,9},{9,8},{10,11... | collective-permute-start | bytes 786440 | tf_op jit(solution)/shard_map/ppermute | solution.py:28
  43.6 2.3 %users.3 = f32[2048,256]{1,0:T(8,128)} custom-call(f32[2048,256]{1,0:T(8,128)S(1)} %get-tuple-element.59.users_ref, bf16[128,256]{1,0:T(8,128)(2,1)S(1)} %collective-permute-done.6.refs_0_, bf16[128,256]{1,0:T(8,128)(2,1)S(1)} %collective-permute-done.10.refs_0_.refs_1_, bf16[128,256]{1,0:T(8,128)(2,1)S(1)} %collective-permute-done.9.refs_0_.refs_2_, ...), custom_call_target="tpu_custom_call" | custom-call | flops 3221225472 | bytes 4194304 | tf_op jit(solution)/shard_map/users/pallas_call | solution.py:241
  45.9 4.3 %collective-permute-done.15 = f32[256,256]{1,0:T(8,128)S(1)} collective-permute-done((f32[256,256]{1,0:T(8,128)S(1)}, f32[256,256]{1,0:T(8,128)S(1)}, u32[]{:S(2)}, u32[]{:S(2)}) %collective-permute-start.15) | collective-permute-done | bytes 262176 | tf_op jit(solution)/shard_map/ppermute | solution.py:28
  50.3 0.0 collective-permute-done.17
  50.3 0.0 collective-permute-done.18
  50.3 0.0 collective-permute-done.16
  50.3 0.8 %fusion.2 = f32[256,256]{1,0:T(8,128)} fusion(f32[256,256]{1,0:T(8,128)S(1)} %collective-permute-done.15, f32[128,256]{1,0:T(8,128)S(1)} %collective-permute-done.18, f32[128,256]{1,0:T(8,128)S(1)} %collective-permute-done.17, f32[256,256]{1,0:T(8,128)S(1)} %get-tuple-element.83, f32[256,256]{1,0:T(8,128)S(1)} %collective-permute-done.16), kind=kLoop, calls=%fused_computation.4 | loop fusion | flops 458752 | bytes 1310720 | tf_op jit(solution)/shard_map/add | solution.py:256
  (13 shorter events, 0.2 us)
Async XLA Ops:
  1.6 5.4 %copy-start = (f32[2048,256]{1,0:T(8,128)S(1)}, f32[2048,256]{1,0:T(8,128)}, u32[]{:S(2)}) copy-start(f32[2048,256]{1,0:T(8,128)} %users_ref.2) | copy-start | bytes 6291460
  1.6 5.8 %collective-permute-start.1 = (bf16[256,256]{1,0:T(8,128)(2,1)S(1)}, bf16[256,256]{1,0:T(8,128)(2,1)S(1)}, u32[]{:S(2)}, u32[]{:S(2)}) collective-permute-start(bf16[256,256]{1,0:T(8,128)(2,1)S(1)} %convert_element_type.9.refs_0_), channel_id=1, source_target_pairs={{0,1},{1,0},{2,3},{3,2},{4,5},{5,4},{6,7},{7,6},{8,9},{9,8},{10,11... | collective-permute-start | bytes 393224 | tf_op jit(solution)/shard_map/ppermute | solution.py:28
  2.2 7.1 %collective-permute-start = (bf16[256,256]{1,0:T(8,128)(2,1)S(1)}, bf16[256,256]{1,0:T(8,128)(2,1)S(1)}, u32[]{:S(2)}, u32[]{:S(2)}) collective-permute-start(bf16[256,256]{1,0:T(8,128)(2,1)S(1)} %convert_element_type.9.refs_0_), channel_id=1, source_target_pairs={{0,2},{1,3},{2,0},{3,1},{4,6},{5,7},{6,4},{7,5},{8,10},{9,11},{10,... | collective-permute-start | bytes 393224 | tf_op jit(solution)/shard_map/ppermute | solution.py:28
  9.1 5.7 %collective-permute-start.4 = (f32[256,256]{1,0:T(8,128)S(1)}, f32[256,256]{1,0:T(8,128)S(1)}, u32[]{:S(2)}, u32[]{:S(2)}) collective-permute-start(f32[256,256]{1,0:T(8,128)S(1)} %get-tuple-element.47), channel_id=1, source_target_pairs={{0,1},{1,0},{2,3},{3,2},{4,5},{5,4},{6,7},{7,6},{8,9},{9,8},{10,11... | collective-permute-start | bytes 786440 | tf_op jit(solution)/shard_map/ppermute | solution.py:28
  9.3 1.6 %collective-permute-start.2 = (bf16[256,256]{1,0:T(8,128)(2,1)S(1)}, bf16[256,256]{1,0:T(8,128)(2,1)S(1)}, u32[]{:S(2)}, u32[]{:S(2)}) collective-permute-start(bf16[256,256]{1,0:T(8,128)(2,1)S(1)} %collective-permute-done.refs_0_.refs_2_), channel_id=1, source_target_pairs={{0,1},{1,0},{2,3},{3,2},{4,5},{5,4},{6,7},{7,6},{8,9},{9,8},{10,11... | collective-permute-start | bytes 393224 | tf_op jit(solution)/shard_map/ppermute | solution.py:28
  10.6 1.6 %collective-permute-start.3 = (f32[256,256]{1,0:T(8,128)S(1)}, f32[256,256]{1,0:T(8,128)S(1)}, u32[]{:S(2)}, u32[]{:S(2)}) collective-permute-start(f32[256,256]{1,0:T(8,128)S(1)} %get-tuple-element.49), channel_id=1, source_target_pairs={{0,1},{1,0},{2,3},{3,2},{4,5},{5,4},{6,7},{7,6},{8,9},{9,8},{10,11... | collective-permute-start | bytes 786440 | tf_op jit(solution)/shard_map/ppermute | solution.py:28
  12.2 2.5 %copy-start.1 = (f32[256,256]{1,0:T(8,128)S(1)}, f32[256,256]{1,0:T(8,128)}, u32[]{:S(2)}) copy-start(f32[256,256]{1,0:T(8,128)} %param.7) | copy-start | bytes 786436
  12.3 4.3 %slice-start = ((s8[8388608]{0:T(1024)(128)(4,1)}), s8[4194304]{0:T(1024)(128)(4,1)S(1)}, s32[]{:S(2)}) async-start(s8[8388608]{0:T(1024)(128)(4,1)} %bitcast), calls=%async_computation | async-start | bytes 8388608
  12.9 10.2 %collective-permute-start.7 = (f32[128,256]{1,0:T(8,128)S(1)}, f32[128,256]{1,0:T(8,128)S(1)}, u32[]{:S(2)}, u32[]{:S(2)}) collective-permute-start(f32[128,256]{1,0:T(8,128)S(1)} %slice_add_fusion), channel_id=1, source_target_pairs={{0,3},{1,2},{2,1},{3,0},{4,7},{5,6},{6,5},{7,4},{8,11},{9,10},{10,... | collective-permute-start | bytes 393224 | tf_op jit(solution)/shard_map/ppermute | solution.py:28
  14.0 7.2 %collective-permute-start.5 = (f32[128,256]{1,0:T(8,128)S(1)}, f32[128,256]{1,0:T(8,128)S(1)}, u32[]{:S(2)}, u32[]{:S(2)}) collective-permute-start(f32[128,256]{1,0:T(8,128)S(1)} %slice_add_fusion.1), channel_id=1, source_target_pairs={{0,3},{1,2},{2,1},{3,0},{4,7},{5,6},{6,5},{7,4},{8,11},{9,10},{10,... | collective-permute-start | bytes 393224 | tf_op jit(solution)/shard_map/ppermute | solution.py:28
  14.8 2.2 %slice-start.1 = ((s8[8388608]{0:T(1024)(128)(4,1)}), s8[4194304]{0:T(1024)(128)(4,1)S(1)}, s32[]{:S(2)}) async-start(s8[8388608]{0:T(1024)(128)(4,1)} %bitcast), calls=%async_computation.1 | async-start | bytes 8388608
  21.3 7.9 %collective-permute-start.6 = (bf16[128,256]{1,0:T(8,128)(2,1)S(1)}, bf16[128,256]{1,0:T(8,128)(2,1)S(1)}, u32[]{:S(2)}, u32[]{:S(2)}) collective-permute-start(bf16[128,256]{1,0:T(8,128)(2,1)S(1)} %get-tuple-element.86), channel_id=1, source_target_pairs={{0,6},{1,7},{2,4},{3,5},{4,10},{5,11},{6,8},{7,9},{8,14},{9,15},{1... | collective-permute-start | bytes 196616 | tf_op jit(solution)/shard_map/ppermute | solution.py:28
  23.2 8.3 %collective-permute-start.9 = (bf16[128,256]{1,0:T(8,128)(2,1)S(1)}, bf16[128,256]{1,0:T(8,128)(2,1)S(1)}, u32[]{:S(2)}, u32[]{:S(2)}) collective-permute-start(bf16[128,256]{1,0:T(8,128)(2,1)S(1)} %get-tuple-element.84), channel_id=1, source_target_pairs={{0,6},{1,7},{2,4},{3,5},{4,10},{5,11},{6,8},{7,9},{8,14},{9,15},{1... | collective-permute-start | bytes 196616 | tf_op jit(solution)/shard_map/ppermute | solution.py:28
  29.2 1.3 %collective-permute-start.10 = (bf16[128,256]{1,0:T(8,128)(2,1)S(1)}, bf16[128,256]{1,0:T(8,128)(2,1)S(1)}, u32[]{:S(2)}, u32[]{:S(2)}) collective-permute-start(bf16[128,256]{1,0:T(8,128)(2,1)S(1)} %collective-permute-done.6.refs_0_), channel_id=1, source_target_pairs={{0,1},{1,0},{2,3},{3,2},{4,5},{5,4},{6,7},{7,6},{8,9},{9,8},{10,11... | collective-permute-start | bytes 196616 | tf_op jit(solution)/shard_map/ppermute | solution.py:28
  29.9 1.6 %collective-permute-start.11 = (f32[128,256]{1,0:T(8,128)S(1)}, f32[128,256]{1,0:T(8,128)S(1)}, u32[]{:S(2)}, u32[]{:S(2)}) collective-permute-start(f32[128,256]{1,0:T(8,128)S(1)} %get-tuple-element.66), channel_id=1, source_target_pairs={{0,1},{1,0},{2,3},{3,2},{4,5},{5,4},{6,7},{7,6},{8,9},{9,8},{10,11... | collective-permute-start | bytes 393224 | tf_op jit(solution)/shard_map/ppermute | solution.py:28
  30.4 8.2 %collective-permute-start.8 = (bf16[256,256]{1,0:T(8,128)(2,1)S(1)}, bf16[256,256]{1,0:T(8,128)(2,1)S(1)}, u32[]{:S(2)}, u32[]{:S(2)}) collective-permute-start(bf16[256,256]{1,0:T(8,128)(2,1)S(1)} %pad_maximum_fusion.1), channel_id=1, source_target_pairs={{0,4},{1,5},{2,6},{3,7},{4,8},{5,9},{6,10},{7,11},{8,12},{9,13},{1... | collective-permute-start | bytes 393224 | tf_op jit(solution)/shard_map/ppermute | solution.py:28
  31.4 8.6 %collective-permute-start.12 = (bf16[128,256]{1,0:T(8,128)(2,1)S(1)}, bf16[128,256]{1,0:T(8,128)(2,1)S(1)}, u32[]{:S(2)}, u32[]{:S(2)}) collective-permute-start(bf16[128,256]{1,0:T(8,128)(2,1)S(1)} %collective-permute-done.9.refs_0_.refs_2_), channel_id=1, source_target_pairs={{0,1},{1,0},{2,3},{3,2},{4,5},{5,4},{6,7},{7,6},{8,9},{9,8},{10,11... | collective-permute-start | bytes 196616 | tf_op jit(solution)/shard_map/ppermute | solution.py:28
  32.5 8.1 %collective-permute-start.13 = (f32[128,256]{1,0:T(8,128)S(1)}, f32[128,256]{1,0:T(8,128)S(1)}, u32[]{:S(2)}, u32[]{:S(2)}) collective-permute-start(f32[128,256]{1,0:T(8,128)S(1)} %get-tuple-element.70), channel_id=1, source_target_pairs={{0,1},{1,0},{2,3},{3,2},{4,5},{5,4},{6,7},{7,6},{8,9},{9,8},{10,11... | collective-permute-start | bytes 393224 | tf_op jit(solution)/shard_map/ppermute | solution.py:28
  38.6 2.8 %collective-permute-start.14 = (bf16[256,256]{1,0:T(8,128)(2,1)S(1)}, bf16[256,256]{1,0:T(8,128)(2,1)S(1)}, u32[]{:S(2)}, u32[]{:S(2)}) collective-permute-start(bf16[256,256]{1,0:T(8,128)(2,1)S(1)} %collective-permute-done.8.refs_0_.refs_4_), channel_id=1, source_target_pairs={{0,1},{1,0},{2,3},{3,2},{4,5},{5,4},{6,7},{7,6},{8,9},{9,8},{10,11... | collective-permute-start | bytes 393224 | tf_op jit(solution)/shard_map/ppermute | solution.py:28
  38.6 11.6 %collective-permute-start.15 = (f32[256,256]{1,0:T(8,128)S(1)}, f32[256,256]{1,0:T(8,128)S(1)}, u32[]{:S(2)}, u32[]{:S(2)}) collective-permute-start(f32[256,256]{1,0:T(8,128)S(1)} %pad_maximum_fusion), channel_id=1, source_target_pairs={{0,4},{1,5},{2,6},{3,7},{4,8},{5,9},{6,10},{7,11},{8,12},{9,13},{1... | collective-permute-start | bytes 786440 | tf_op jit(solution)/shard_map/ppermute | solution.py:28
  38.9 11.4 %collective-permute-start.17 = (f32[128,256]{1,0:T(8,128)S(1)}, f32[128,256]{1,0:T(8,128)S(1)}, u32[]{:S(2)}, u32[]{:S(2)}) collective-permute-start(f32[128,256]{1,0:T(8,128)S(1)} %add.43), channel_id=1, source_target_pairs={{0,3},{1,2},{2,1},{3,0},{4,7},{5,6},{6,5},{7,4},{8,11},{9,10},{10,... | collective-permute-start | bytes 393224 | tf_op jit(solution)/shard_map/ppermute | solution.py:28
  40.7 9.6 %collective-permute-start.18 = (f32[128,256]{1,0:T(8,128)S(1)}, f32[128,256]{1,0:T(8,128)S(1)}, u32[]{:S(2)}, u32[]{:S(2)}) collective-permute-start(f32[128,256]{1,0:T(8,128)S(1)} %add.44), channel_id=1, source_target_pairs={{0,3},{1,2},{2,1},{3,0},{4,7},{5,6},{6,5},{7,4},{8,11},{9,10},{10,... | collective-permute-start | bytes 393224 | tf_op jit(solution)/shard_map/ppermute | solution.py:28
  43.1 7.2 %collective-permute-start.16 = (f32[256,256]{1,0:T(8,128)S(1)}, f32[256,256]{1,0:T(8,128)S(1)}, u32[]{:S(2)}, u32[]{:S(2)}) collective-permute-start(f32[256,256]{1,0:T(8,128)S(1)} %get-tuple-element.75), channel_id=1, source_target_pairs={{0,1},{1,0},{2,3},{3,2},{4,5},{5,4},{6,7},{7,6},{8,9},{9,8},{10,11... | collective-permute-start | bytes 786440 | tf_op jit(solution)/shard_map/ppermute | solution.py:28

commit v4 on v3

--- a/solution.py
+++ b/solution.py
@@ -14,8 +14,9 @@
 HBM = pl.BlockSpec(memory_space=pltpu.HBM)
 BOTH_ROWS = (((0,), (0,)), ((), ()))
 MIB = 1 << 20
-CHUNK_TILES = 4
-LATENCY_SCALE = 3
+CHUNK_TILES = 2
+LOOKAHEAD = 2
+LATENCY_SCALES = (1, 3)
 
 
 def route(block, strata_shift, users_flip):
@@ -157,11 +158,11 @@
         return jnp.dot(items, users_t, preferred_element_type=F32)
 
     grad = None
-    ahead = predict(0)
+    ahead = [predict(i) for i in range(min(LOOKAHEAD, chunks))]
     for i in range(chunks):
-        predicted = ahead
-        if i + 1 < chunks:
-            ahead = predict(i + 1)
+        predicted = ahead.pop(0)
+        if i + LOOKAHEAD < chunks:
+            ahead.append(predict(i + LOOKAHEAD))
         residuals = []
         for q in range(per_chunk):
             r = i * per_chunk + q
@@ -179,7 +180,7 @@
         start += ref.shape[0]
 
 
-def terms(columns, sizes, lowered, dense, items):
+def terms(columns, sizes, lowered, dense, items, last):
     user_rows, width = lowered[0].shape
     tile = dense.shape[-1]
     rows = tile * len(columns)
@@ -191,7 +192,7 @@
         out_specs=[VMEM] * (1 + len(sizes)),
         compiler_params=pltpu.CompilerParams(vmem_limit_bytes=16 * MIB),
         cost_estimate=pl.CostEstimate(
-            flops=LATENCY_SCALE * 4 * user_rows * rows * width, bytes_accessed=MIB, transcendentals=0
+            flops=int(LATENCY_SCALES[last] * 4 * user_rows * rows * width), bytes_accessed=MIB, transcendentals=0
         ),
     )(*lowered, dense, *items)
 
@@ -230,7 +231,7 @@
 def update_users(users, items, residuals, last):
     user_rows, width = users.shape
     tile = residuals[0].shape[-1]
-    chunk = min(2 * tile, user_rows)
+    chunk = min((2 if last else 4) * tile, user_rows)
     item_rows = sum(block.shape[0] for block in items)
     full = jax.ShapeDtypeStruct(users.shape, F32)
     if last:
@@ -246,7 +247,7 @@
         scratch_shapes=scratch,
         compiler_params=pltpu.CompilerParams(vmem_limit_bytes=12 * MIB),
         cost_estimate=pl.CostEstimate(
-            flops=LATENCY_SCALE * 2 * user_rows * item_rows * width, bytes_accessed=4 * MIB, transcendentals=0
+            flops=int(LATENCY_SCALES[last] * 2 * user_rows * item_rows * width), bytes_accessed=4 * MIB, transcendentals=0
         ),
         name="users",
     )(users, *items, *residuals)
@@ -292,7 +293,7 @@
                 (d + i) * per_shard + first + k for i, size in enumerate(sizes) for k in range(size // tile)
             )
             residual, *grads = terms(
-                columns, sizes, lowered, dense, [after(blocks[0], *mark), *blocks[1:]]
+                columns, sizes, lowered, dense, [after(blocks[0], *mark), *blocks[1:]], last
             )
             mark[:] = grads[-1:]
             items_in.extend(blocks)
@@ -348,7 +349,7 @@
             step, 0, column_tiles, users_now.shape[0], tile_rows, tile_columns, tile_counts, ratings
         )
         lowered = lower(users_now, tile)
-        residual, grad = terms(tuple(range(column_tiles)), block.shape[:1], lowered, dense, [block])
+        residual, grad = terms(tuple(range(column_tiles)), block.shape[:1], lowered, dense, [block], True)
         grad_part = lax.psum_scatter(grad, "users", scatter_dimension=0, tiled=True)
         users_now = update_users(users_now, [block], [residual], True)[0]
         item_part = updated_items(item_part, grad_part)

time: 51.3 us -> 50.7 us (0.988)
  transfers between devices with their start and end apart: 19 -> 19, of which waited for: 6 -> 7; matrix products, arithmetic and copies ran while one was open for 0% -> 0% of each run, Pallas kernels for 31% -> 30%
where the time goes in v4:
time: 50.7 us; the launch traced here: 50.6 us
  waiting for transfers between devices  18.6 us (37%)
  Pallas kernels  15.4 us (30%)
  starting transfers between devices  13.7 us (27%)
  other arithmetic  1.96 us (4%)
  between operations  0.93 us (2%)
    ppermute x19, waiting for transfers between devices, route(): return lax.ppermute(block, ('strata', 'users'), pairs)  18.6 us
    ppermute x19, starting transfers between devices, route(): return lax.ppermute(block, ('strata', 'users'), pairs)  13.7 us
    pallas_call x9, Pallas kernels, terms(): pl.pallas_call(functools.partial(terms_kernel, columns, sizes, min(CHUNK_...  7.56 us
    pallas_call x2, Pallas kernels, update_users(): pl.pallas_call(functools.partial(users_kernel, len(items), chunk, last),...  4.02 us
    pallas_call x2, Pallas kernels, dense_ratings(): pl.pallas_call(functools.partial(dense_kernel, step, tiles_per_shard, gro...  3.43 us
  transfers between devices with their start and end apart: 19, of which 7 were waited for; matrix products, arithmetic and copies ran while one was open for 0% of the time, Pallas kernels for 30%

profile of v4, /device:TPU:0, one launch (start us, length us, event | category | flops | bytes accessed | tf_op | source)
XLA Modules:
  0.0 50.6 jit_solution(9383954203879419105)
XLA Ops:
  0.6 1.0 %convert_element_type.9.refs_0_ = bf16[256,256]{1,0:T(8,128)(2,1)S(1)} convert(f32[256,256]{1,0:T(8,128)} %param.7) | non-fusion elementwise | flops 65536 | bytes 393216 | tf_op jit(solution)/shard_map/convert_element_type | solution.py:269
  1.6 0.0 copy-start
  1.6 0.6 %collective-permute-start.1 = (bf16[256,256]{1,0:T(8,128)(2,1)S(1)}, bf16[256,256]{1,0:T(8,128)(2,1)S(1)}, u32[]{:S(2)}, u32[]{:S(2)}) collective-permute-start(bf16[256,256]{1,0:T(8,128)(2,1)S(1)} %convert_element_type.9.refs_0_), channel_id=1, source_target_pairs={{0,1},{1,0},{2,3},{3,2},{4,5},{5,4},{6,7},{7,6},{8,9},{9,8},{10,11... | collective-permute-start | bytes 393224 | tf_op jit(solution)/shard_map/ppermute | solution.py:29
  2.2 2.6 %collective-permute-start = (bf16[256,256]{1,0:T(8,128)(2,1)S(1)}, bf16[256,256]{1,0:T(8,128)(2,1)S(1)}, u32[]{:S(2)}, u32[]{:S(2)}) collective-permute-start(bf16[256,256]{1,0:T(8,128)(2,1)S(1)} %convert_element_type.9.refs_0_), channel_id=1, source_target_pairs={{0,2},{1,3},{2,0},{3,1},{4,6},{5,7},{6,4},{7,5},{8,10},{9,11},{10,... | collective-permute-start | bytes 393224 | tf_op jit(solution)/shard_map/ppermute | solution.py:29
  4.8 2.2 %shard_map.77.dense_ref = bf16[8,16,128,128]{3,2,1,0:T(8,128)(2,1)S(1)} custom-call(s32[1,1,2]{2,1,0:T(1,128)} %counts_hbm.3, s32[1,1,2,64]{3,2,1,0:T(2,128)} %rows_hbm.1, s32[1,1,2,64]{3,2,1,0:T(2,128)} %columns_hbm.3, s32[1,1,2,64,128,128]{5,4,3,2,1,0:T(8,128)} %ratings.3), custom_call_target="tpu_custom_call" | custom-call | flops 2000000000 | bytes 8388608 | tf_op jit(solution)/shard_map/pallas_call | solution.py:135
  7.0 0.0 copy-done
  7.0 0.4 lower.1
  7.4 0.0 collective-permute-done.1.refs_1_
  7.4 1.5 %shard_map.78 = (bf16[16,512,128]{2,1,0:T(8,128)(2,1)S(1)}, f32[256,256]{1,0:T(8,128)S(1)}, f32[256,256]{1,0:T(8,128)S(1)}) custom-call(bf16[2048,256]{1,0:T(8,128)(2,1)S(1)} %get-tuple-element.44.users_ref, bf16[256,2048]{1,0:T(8,128)(2,1)S(1)} %get-tuple-element.45.users_t_ref, bf16[8,16,128,128]{3,2,1,0:T(8,128)(2,1)S(1)} %shard_map.77.dense_ref, ...), custom_call_target="tpu_custom_call" | custom-call | flops 1073741824 | bytes 1048576 | tf_op jit(solution)/shard_map/pallas_call | solution.py:187
  9.0 0.0 collective-permute-done.refs_0_.refs_2_
  9.0 0.2 collective-permute-start.2
  9.2 0.9 %shard_map.79 = (bf16[16,256,128]{2,1,0:T(8,128)(2,1)S(1)}, f32[256,256]{1,0:T(8,128)S(1)}) custom-call(bf16[2048,256]{1,0:T(8,128)(2,1)S(1)} %get-tuple-element.44.users_ref, bf16[256,2048]{1,0:T(8,128)(2,1)S(1)} %get-tuple-element.45.users_t_ref, bf16[8,16,128,128]{3,2,1,0:T(8,128)(2,1)S(1)} %shard_map.77.dense_ref, ...), custom_call_target="tpu_custom_call" | custom-call | flops 536870912 | bytes 1048576 | tf_op jit(solution)/shard_map/pallas_call | solution.py:187
  10.1 0.4 collective-permute-start.3
  10.5 0.2 collective-permute-start.4
  10.7 0.0 collective-permute-done.2
  10.7 0.0 slice-start
  10.7 0.6 %shard_map.80 = (bf16[16,128,128]{2,1,0:T(8,128)(2,1)S(1)}, f32[128,256]{1,0:T(8,128)S(1)}) custom-call(bf16[2048,256]{1,0:T(8,128)(2,1)S(1)} %get-tuple-element.44.users_ref, bf16[256,2048]{1,0:T(8,128)(2,1)S(1)} %get-tuple-element.45.users_t_ref, bf16[8,16,128,128]{3,2,1,0:T(8,128)(2,1)S(1)} %shard_map.77.dense_ref, ...), custom_call_target="tpu_custom_call" | custom-call | flops 268435456 | bytes 1048576 | tf_op jit(solution)/shard_map/pallas_call | solution.py:187
  11.3 0.4 collective-permute-done.3
  11.7 0.0 copy-start.1
  11.7 0.0 slice-start.1
  11.7 0.6 %shard_map.81 = (bf16[16,128,128]{2,1,0:T(8,128)(2,1)S(1)}, f32[128,256]{1,0:T(8,128)S(1)}) custom-call(bf16[2048,256]{1,0:T(8,128)(2,1)S(1)} %get-tuple-element.44.users_ref, bf16[256,2048]{1,0:T(8,128)(2,1)S(1)} %get-tuple-element.45.users_t_ref, bf16[8,16,128,128]{3,2,1,0:T(8,128)(2,1)S(1)} %shard_map.77.dense_ref, ...), custom_call_target="tpu_custom_call" | custom-call | flops 268435456 | bytes 1048576 | tf_op jit(solution)/shard_map/pallas_call | solution.py:187
  12.4 1.6 %collective-permute-start.7 = (f32[128,256]{1,0:T(8,128)S(1)}, f32[128,256]{1,0:T(8,128)S(1)}, u32[]{:S(2)}, u32[]{:S(2)}) collective-permute-start(f32[128,256]{1,0:T(8,128)S(1)} %slice_add_fusion), channel_id=1, source_target_pairs={{0,3},{1,2},{2,1},{3,0},{4,7},{5,6},{6,5},{7,4},{8,11},{9,10},{10,... | collective-permute-start | bytes 393224 | tf_op jit(solution)/shard_map/ppermute | solution.py:29
  13.9 0.2 collective-permute-start.5
  14.2 0.0 collective-permute-done.4
  14.2 0.0 copy-done.1
  14.3 1.7 %users.2 = (f32[2048,256]{1,0:T(8,128)S(1)}, bf16[2048,256]{1,0:T(8,128)(2,1)S(1)}, bf16[256,2048]{1,0:T(8,128)(2,1)S(1)}) custom-call(f32[2048,256]{1,0:T(8,128)S(1)} %copy-done, bf16[256,256]{1,0:T(8,128)(2,1)S(1)} %convert_element_type.9.refs_0_, bf16[256,256]{1,0:T(8,128)(2,1)S(1)} %collective-permute-done.1.refs_1_, ...), custom_call_target="tpu_custom_call" | custom-call | flops 1073741824 | bytes 4194304 | tf_op jit(solution)/shard_map/users/pallas_call | solution.py:242
  16.0 0.0 slice-done
  16.0 0.0 slice-done.1
  16.0 1.2 %shard_map.82.dense_ref = bf16[8,16,128,128]{3,2,1,0:T(8,128)(2,1)S(1)} custom-call(s32[1,1,2]{2,1,0:T(1,128)} %counts_hbm.3, s32[1,1,2,64]{3,2,1,0:T(2,128)} %rows_hbm.1, s32[1,1,2,64]{3,2,1,0:T(2,128)} %columns_hbm.3, s32[1,1,2,64,128,128]{5,4,3,2,1,0:T(8,128)S(1)} %bitcast.1), custom_call_target="tpu_custom_call" | custom-call | flops 2000000000 | bytes 8388608 | tf_op jit(solution)/shard_map/pallas_call | solution.py:135
  17.2 3.3 %collective-permute-done.5 = f32[128,256]{1,0:T(8,128)S(1)} collective-permute-done((f32[128,256]{1,0:T(8,128)S(1)}, f32[128,256]{1,0:T(8,128)S(1)}, u32[]{:S(2)}, u32[]{:S(2)}) %collective-permute-start.5) | collective-permute-done | bytes 131104 | tf_op jit(solution)/shard_map/ppermute | solution.py:29
  20.6 2.5 %collective-permute-start.6 = (bf16[128,256]{1,0:T(8,128)(2,1)S(1)}, bf16[128,256]{1,0:T(8,128)(2,1)S(1)}, u32[]{:S(2)}, u32[]{:S(2)}) collective-permute-start(bf16[128,256]{1,0:T(8,128)(2,1)S(1)} %get-tuple-element.86), channel_id=1, source_target_pairs={{0,6},{1,7},{2,4},{3,5},{4,10},{5,11},{6,8},{7,9},{8,14},{9,15},{1... | collective-permute-start | bytes 196616 | tf_op jit(solution)/shard_map/ppermute | solution.py:29
  23.1 0.0 collective-permute-done.7
  23.1 1.5 %collective-permute-start.9 = (bf16[128,256]{1,0:T(8,128)(2,1)S(1)}, bf16[128,256]{1,0:T(8,128)(2,1)S(1)}, u32[]{:S(2)}, u32[]{:S(2)}) collective-permute-start(bf16[128,256]{1,0:T(8,128)(2,1)S(1)} %get-tuple-element.84), channel_id=1, source_target_pairs={{0,6},{1,7},{2,4},{3,5},{4,10},{5,11},{6,8},{7,9},{8,14},{9,15},{1... | collective-permute-start | bytes 196616 | tf_op jit(solution)/shard_map/ppermute | solution.py:29
  24.6 4.1 %collective-permute-done.6.refs_0_ = bf16[128,256]{1,0:T(8,128)(2,1)S(1)} collective-permute-done((bf16[128,256]{1,0:T(8,128)(2,1)S(1)}, bf16[128,256]{1,0:T(8,128)(2,1)S(1)}, u32[]{:S(2)}, u32[]{:S(2)}) %collective-permute-start.6) | collective-permute-done | bytes 65568 | tf_op jit(solution)/shard_map/ppermute | solution.py:29
  28.7 0.0 collective-permute-start.10
  28.7 0.6 %shard_map.83 = (bf16[16,128,128]{2,1,0:T(8,128)(2,1)S(1)}, f32[128,256]{1,0:T(8,128)S(1)}) custom-call(bf16[2048,256]{1,0:T(8,128)(2,1)S(1)} %get-tuple-element.61.users_ref, bf16[256,2048]{1,0:T(8,128)(2,1)S(1)} %get-tuple-element.62.users_t_ref, bf16[8,16,128,128]{3,2,1,0:T(8,128)(2,1)S(1)} %shard_map.82.dense_ref, ...), custom_call_target="tpu_custom_call" | custom-call | flops 805306368 | bytes 1048576 | tf_op jit(solution)/shard_map/pallas_call | solution.py:187
  29.3 0.6 %collective-permute-start.11 = (f32[128,256]{1,0:T(8,128)S(1)}, f32[128,256]{1,0:T(8,128)S(1)}, u32[]{:S(2)}, u32[]{:S(2)}) collective-permute-start(f32[128,256]{1,0:T(8,128)S(1)} %get-tuple-element.66), channel_id=1, source_target_pairs={{0,1},{1,0},{2,3},{3,2},{4,5},{5,4},{6,7},{7,6},{8,9},{9,8},{10,11... | collective-permute-start | bytes 393224 | tf_op jit(solution)/shard_map/ppermute | solution.py:29
  29.9 0.1 collective-permute-start.8
  30.0 0.0 collective-permute-done.10.refs_0_.refs_1_
  30.0 0.6 %shard_map.84 = (bf16[16,128,128]{2,1,0:T(8,128)(2,1)S(1)}, f32[128,256]{1,0:T(8,128)S(1)}) custom-call(bf16[2048,256]{1,0:T(8,128)(2,1)S(1)} %get-tuple-element.61.users_ref, bf16[256,2048]{1,0:T(8,128)(2,1)S(1)} %get-tuple-element.62.users_t_ref, bf16[8,16,128,128]{3,2,1,0:T(8,128)(2,1)S(1)} %shard_map.82.dense_ref, ...), custom_call_target="tpu_custom_call" | custom-call | flops 805306368 | bytes 1048576 | tf_op jit(solution)/shard_map/pallas_call | solution.py:187
  30.6 0.3 collective-permute-done.11
  30.9 0.1 collective-permute-done.9.refs_0_.refs_2_
  31.0 0.4 collective-permute-start.12
  31.4 0.6 %shard_map.85 = (bf16[16,128,128]{2,1,0:T(8,128)(2,1)S(1)}, f32[128,256]{1,0:T(8,128)S(1)}) custom-call(bf16[2048,256]{1,0:T(8,128)(2,1)S(1)} %get-tuple-element.61.users_ref, bf16[256,2048]{1,0:T(8,128)(2,1)S(1)} %get-tuple-element.62.users_t_ref, bf16[8,16,128,128]{3,2,1,0:T(8,128)(2,1)S(1)} %shard_map.82.dense_ref, ...), custom_call_target="tpu_custom_call" | custom-call | flops 805306368 | bytes 1048576 | tf_op jit(solution)/shard_map/pallas_call | solution.py:187
  32.0 0.2 collective-permute-start.13
  32.2 5.9 %collective-permute-done.8.refs_0_.refs_4_ = bf16[256,256]{1,0:T(8,128)(2,1)S(1)} collective-permute-done((bf16[256,256]{1,0:T(8,128)(2,1)S(1)}, bf16[256,256]{1,0:T(8,128)(2,1)S(1)}, u32[]{:S(2)}, u32[]{:S(2)}) %collective-permute-start.8) | collective-permute-done | bytes 131104 | tf_op jit(solution)/shard_map/ppermute | solution.py:29
  38.1 0.0 collective-permute-start.14
  38.1 0.2 collective-permute-start.15
  38.4 1.6 %collective-permute-start.17 = (f32[128,256]{1,0:T(8,128)S(1)}, f32[128,256]{1,0:T(8,128)S(1)}, u32[]{:S(2)}, u32[]{:S(2)}) collective-permute-start(f32[128,256]{1,0:T(8,128)S(1)} %add.43), channel_id=1, source_target_pairs={{0,3},{1,2},{2,1},{3,0},{4,7},{5,6},{6,5},{7,4},{8,11},{9,10},{10,... | collective-permute-start | bytes 393224 | tf_op jit(solution)/shard_map/ppermute | solution.py:29
  40.0 0.0 collective-permute-done.12.refs_0_.refs_3_
  40.0 0.6 %shard_map.86 = (bf16[16,128,128]{2,1,0:T(8,128)(2,1)S(1)}, f32[128,256]{1,0:T(8,128)S(1)}) custom-call(bf16[2048,256]{1,0:T(8,128)(2,1)S(1)} %get-tuple-element.61.users_ref, bf16[256,2048]{1,0:T(8,128)(2,1)S(1)} %get-tuple-element.62.users_t_ref, bf16[8,16,128,128]{3,2,1,0:T(8,128)(2,1)S(1)} %shard_map.82.dense_ref, ...), custom_call_target="tpu_custom_call" | custom-call | flops 805306368 | bytes 1048576 | tf_op jit(solution)/shard_map/pallas_call | solution.py:187
  40.6 0.0 collective-permute-done.13
  40.6 0.3 collective-permute-start.18
  40.9 0.0 collective-permute-done.14.refs_1_.refs_5_
  40.9 1.5 %shard_map.87 = (bf16[16,512,128]{2,1,0:T(8,128)(2,1)S(1)}, f32[256,256]{1,0:T(8,128)S(1)}, f32[256,256]{1,0:T(8,128)S(1)}) custom-call(bf16[2048,256]{1,0:T(8,128)(2,1)S(1)} %get-tuple-element.61.users_ref, bf16[256,2048]{1,0:T(8,128)(2,1)S(1)} %get-tuple-element.62.users_t_ref, bf16[8,16,128,128]{3,2,1,0:T(8,128)(2,1)S(1)} %shard_map.82.dense_ref, ...), custom_call_target="tpu_custom_call" | custom-call | flops 3221225472 | bytes 1048576 | tf_op jit(solution)/shard_map/pallas_call | solution.py:187
  42.4 0.6 %collective-permute-start.16 = (f32[256,256]{1,0:T(8,128)S(1)}, f32[256,256]{1,0:T(8,128)S(1)}, u32[]{:S(2)}, u32[]{:S(2)}) collective-permute-start(f32[256,256]{1,0:T(8,128)S(1)} %get-tuple-element.75), channel_id=1, source_target_pairs={{0,1},{1,0},{2,3},{3,2},{4,5},{5,4},{6,7},{7,6},{8,9},{9,8},{10,11... | collective-permute-start | bytes 786440 | tf_op jit(solution)/shard_map/ppermute | solution.py:29
  43.0 2.3 %users.3 = f32[2048,256]{1,0:T(8,128)} custom-call(f32[2048,256]{1,0:T(8,128)S(1)} %get-tuple-element.59.users_ref, bf16[128,256]{1,0:T(8,128)(2,1)S(1)} %collective-permute-done.6.refs_0_, bf16[128,256]{1,0:T(8,128)(2,1)S(1)} %collective-permute-done.10.refs_0_.refs_1_, bf16[128,256]{1,0:T(8,128)(2,1)S(1)} %collective-permute-done.9.refs_0_.refs_2_, ...), custom_call_target="tpu_custom_call" | custom-call | flops 3221225472 | bytes 4194304 | tf_op jit(solution)/shard_map/users/pallas_call | solution.py:242
  45.3 4.5 %collective-permute-done.15 = f32[256,256]{1,0:T(8,128)S(1)} collective-permute-done((f32[256,256]{1,0:T(8,128)S(1)}, f32[256,256]{1,0:T(8,128)S(1)}, u32[]{:S(2)}, u32[]{:S(2)}) %collective-permute-start.15) | collective-permute-done | bytes 262176 | tf_op jit(solution)/shard_map/ppermute | solution.py:29
  49.8 0.0 collective-permute-done.17
  49.8 0.0 collective-permute-done.18
  49.8 0.0 collective-permute-done.16
  49.8 0.8 %fusion.2 = f32[256,256]{1,0:T(8,128)} fusion(f32[256,256]{1,0:T(8,128)S(1)} %collective-permute-done.15, f32[128,256]{1,0:T(8,128)S(1)} %collective-permute-done.18, f32[128,256]{1,0:T(8,128)S(1)} %collective-permute-done.17, f32[256,256]{1,0:T(8,128)S(1)} %get-tuple-element.83, f32[256,256]{1,0:T(8,128)S(1)} %collective-permute-done.16), kind=kLoop, calls=%fused_computation.4 | loop fusion | flops 458752 | bytes 1310720 | tf_op jit(solution)/shard_map/add | solution.py:257
  (13 shorter events, 0.2 us)
Async XLA Ops:
  1.6 5.4 %copy-start = (f32[2048,256]{1,0:T(8,128)S(1)}, f32[2048,256]{1,0:T(8,128)}, u32[]{:S(2)}) copy-start(f32[2048,256]{1,0:T(8,128)} %users_ref.2) | copy-start | bytes 6291460
  1.6 5.8 %collective-permute-start.1 = (bf16[256,256]{1,0:T(8,128)(2,1)S(1)}, bf16[256,256]{1,0:T(8,128)(2,1)S(1)}, u32[]{:S(2)}, u32[]{:S(2)}) collective-permute-start(bf16[256,256]{1,0:T(8,128)(2,1)S(1)} %convert_element_type.9.refs_0_), channel_id=1, source_target_pairs={{0,1},{1,0},{2,3},{3,2},{4,5},{5,4},{6,7},{7,6},{8,9},{9,8},{10,11... | collective-permute-start | bytes 393224 | tf_op jit(solution)/shard_map/ppermute | solution.py:29
  2.2 6.8 %collective-permute-start = (bf16[256,256]{1,0:T(8,128)(2,1)S(1)}, bf16[256,256]{1,0:T(8,128)(2,1)S(1)}, u32[]{:S(2)}, u32[]{:S(2)}) collective-permute-start(bf16[256,256]{1,0:T(8,128)(2,1)S(1)} %convert_element_type.9.refs_0_), channel_id=1, source_target_pairs={{0,2},{1,3},{2,0},{3,1},{4,6},{5,7},{6,4},{7,5},{8,10},{9,11},{10,... | collective-permute-start | bytes 393224 | tf_op jit(solution)/shard_map/ppermute | solution.py:29
  9.0 1.7 %collective-permute-start.2 = (bf16[256,256]{1,0:T(8,128)(2,1)S(1)}, bf16[256,256]{1,0:T(8,128)(2,1)S(1)}, u32[]{:S(2)}, u32[]{:S(2)}) collective-permute-start(bf16[256,256]{1,0:T(8,128)(2,1)S(1)} %collective-permute-done.refs_0_.refs_2_), channel_id=1, source_target_pairs={{0,1},{1,0},{2,3},{3,2},{4,5},{5,4},{6,7},{7,6},{8,9},{9,8},{10,11... | collective-permute-start | bytes 393224 | tf_op jit(solution)/shard_map/ppermute | solution.py:29
  10.1 1.6 %collective-permute-start.3 = (f32[256,256]{1,0:T(8,128)S(1)}, f32[256,256]{1,0:T(8,128)S(1)}, u32[]{:S(2)}, u32[]{:S(2)}) collective-permute-start(f32[256,256]{1,0:T(8,128)S(1)} %get-tuple-element.49), channel_id=1, source_target_pairs={{0,1},{1,0},{2,3},{3,2},{4,5},{5,4},{6,7},{7,6},{8,9},{9,8},{10,11... | collective-permute-start | bytes 786440 | tf_op jit(solution)/shard_map/ppermute | solution.py:29
  10.5 3.7 %collective-permute-start.4 = (f32[256,256]{1,0:T(8,128)S(1)}, f32[256,256]{1,0:T(8,128)S(1)}, u32[]{:S(2)}, u32[]{:S(2)}) collective-permute-start(f32[256,256]{1,0:T(8,128)S(1)} %get-tuple-element.47), channel_id=1, source_target_pairs={{0,1},{1,0},{2,3},{3,2},{4,5},{5,4},{6,7},{7,6},{8,9},{9,8},{10,11... | collective-permute-start | bytes 786440 | tf_op jit(solution)/shard_map/ppermute | solution.py:29
  10.7 5.3 %slice-start = ((s8[8388608]{0:T(1024)(128)(4,1)}), s8[4194304]{0:T(1024)(128)(4,1)S(1)}, s32[]{:S(2)}) async-start(s8[8388608]{0:T(1024)(128)(4,1)} %bitcast), calls=%async_computation | async-start | bytes 8388608
  11.7 2.5 %copy-start.1 = (f32[256,256]{1,0:T(8,128)S(1)}, f32[256,256]{1,0:T(8,128)}, u32[]{:S(2)}) copy-start(f32[256,256]{1,0:T(8,128)} %param.7) | copy-start | bytes 786436
  11.7 4.3 %slice-start.1 = ((s8[8388608]{0:T(1024)(128)(4,1)}), s8[4194304]{0:T(1024)(128)(4,1)S(1)}, s32[]{:S(2)}) async-start(s8[8388608]{0:T(1024)(128)(4,1)} %bitcast), calls=%async_computation.1 | async-start | bytes 8388608
  12.4 10.7 %collective-permute-start.7 = (f32[128,256]{1,0:T(8,128)S(1)}, f32[128,256]{1,0:T(8,128)S(1)}, u32[]{:S(2)}, u32[]{:S(2)}) collective-permute-start(f32[128,256]{1,0:T(8,128)S(1)} %slice_add_fusion), channel_id=1, source_target_pairs={{0,3},{1,2},{2,1},{3,0},{4,7},{5,6},{6,5},{7,4},{8,11},{9,10},{10,... | collective-permute-start | bytes 393224 | tf_op jit(solution)/shard_map/ppermute | solution.py:29
  13.9 6.6 %collective-permute-start.5 = (f32[128,256]{1,0:T(8,128)S(1)}, f32[128,256]{1,0:T(8,128)S(1)}, u32[]{:S(2)}, u32[]{:S(2)}) collective-permute-start(f32[128,256]{1,0:T(8,128)S(1)} %slice_add_fusion.1), channel_id=1, source_target_pairs={{0,3},{1,2},{2,1},{3,0},{4,7},{5,6},{6,5},{7,4},{8,11},{9,10},{10,... | collective-permute-start | bytes 393224 | tf_op jit(solution)/shard_map/ppermute | solution.py:29
  20.6 8.2 %collective-permute-start.6 = (bf16[128,256]{1,0:T(8,128)(2,1)S(1)}, bf16[128,256]{1,0:T(8,128)(2,1)S(1)}, u32[]{:S(2)}, u32[]{:S(2)}) collective-permute-start(bf16[128,256]{1,0:T(8,128)(2,1)S(1)} %get-tuple-element.86), channel_id=1, source_target_pairs={{0,6},{1,7},{2,4},{3,5},{4,10},{5,11},{6,8},{7,9},{8,14},{9,15},{1... | collective-permute-start | bytes 196616 | tf_op jit(solution)/shard_map/ppermute | solution.py:29
  23.1 7.9 %collective-permute-start.9 = (bf16[128,256]{1,0:T(8,128)(2,1)S(1)}, bf16[128,256]{1,0:T(8,128)(2,1)S(1)}, u32[]{:S(2)}, u32[]{:S(2)}) collective-permute-start(bf16[128,256]{1,0:T(8,128)(2,1)S(1)} %get-tuple-element.84), channel_id=1, source_target_pairs={{0,6},{1,7},{2,4},{3,5},{4,10},{5,11},{6,8},{7,9},{8,14},{9,15},{1... | collective-permute-start | bytes 196616 | tf_op jit(solution)/shard_map/ppermute | solution.py:29
  28.7 1.3 %collective-permute-start.10 = (bf16[128,256]{1,0:T(8,128)(2,1)S(1)}, bf16[128,256]{1,0:T(8,128)(2,1)S(1)}, u32[]{:S(2)}, u32[]{:S(2)}) collective-permute-start(bf16[128,256]{1,0:T(8,128)(2,1)S(1)} %collective-permute-done.6.refs_0_), channel_id=1, source_target_pairs={{0,1},{1,0},{2,3},{3,2},{4,5},{5,4},{6,7},{7,6},{8,9},{9,8},{10,11... | collective-permute-start | bytes 196616 | tf_op jit(solution)/shard_map/ppermute | solution.py:29
  29.3 1.6 %collective-permute-start.11 = (f32[128,256]{1,0:T(8,128)S(1)}, f32[128,256]{1,0:T(8,128)S(1)}, u32[]{:S(2)}, u32[]{:S(2)}) collective-permute-start(f32[128,256]{1,0:T(8,128)S(1)} %get-tuple-element.66), channel_id=1, source_target_pairs={{0,1},{1,0},{2,3},{3,2},{4,5},{5,4},{6,7},{7,6},{8,9},{9,8},{10,11... | collective-permute-start | bytes 393224 | tf_op jit(solution)/shard_map/ppermute | solution.py:29
  29.9 8.2 %collective-permute-start.8 = (bf16[256,256]{1,0:T(8,128)(2,1)S(1)}, bf16[256,256]{1,0:T(8,128)(2,1)S(1)}, u32[]{:S(2)}, u32[]{:S(2)}) collective-permute-start(bf16[256,256]{1,0:T(8,128)(2,1)S(1)} %pad_maximum_fusion.1), channel_id=1, source_target_pairs={{0,4},{1,5},{2,6},{3,7},{4,8},{5,9},{6,10},{7,11},{8,12},{9,13},{1... | collective-permute-start | bytes 393224 | tf_op jit(solution)/shard_map/ppermute | solution.py:29
  31.0 9.0 %collective-permute-start.12 = (bf16[128,256]{1,0:T(8,128)(2,1)S(1)}, bf16[128,256]{1,0:T(8,128)(2,1)S(1)}, u32[]{:S(2)}, u32[]{:S(2)}) collective-permute-start(bf16[128,256]{1,0:T(8,128)(2,1)S(1)} %collective-permute-done.9.refs_0_.refs_2_), channel_id=1, source_target_pairs={{0,1},{1,0},{2,3},{3,2},{4,5},{5,4},{6,7},{7,6},{8,9},{9,8},{10,11... | collective-permute-start | bytes 196616 | tf_op jit(solution)/shard_map/ppermute | solution.py:29
  32.0 8.6 %collective-permute-start.13 = (f32[128,256]{1,0:T(8,128)S(1)}, f32[128,256]{1,0:T(8,128)S(1)}, u32[]{:S(2)}, u32[]{:S(2)}) collective-permute-start(f32[128,256]{1,0:T(8,128)S(1)} %get-tuple-element.70), channel_id=1, source_target_pairs={{0,1},{1,0},{2,3},{3,2},{4,5},{5,4},{6,7},{7,6},{8,9},{9,8},{10,11... | collective-permute-start | bytes 393224 | tf_op jit(solution)/shard_map/ppermute | solution.py:29
  38.1 2.8 %collective-permute-start.14 = (bf16[256,256]{1,0:T(8,128)(2,1)S(1)}, bf16[256,256]{1,0:T(8,128)(2,1)S(1)}, u32[]{:S(2)}, u32[]{:S(2)}) collective-permute-start(bf16[256,256]{1,0:T(8,128)(2,1)S(1)} %collective-permute-done.8.refs_0_.refs_4_), channel_id=1, source_target_pairs={{0,1},{1,0},{2,3},{3,2},{4,5},{5,4},{6,7},{7,6},{8,9},{9,8},{10,11... | collective-permute-start | bytes 393224 | tf_op jit(solution)/shard_map/ppermute | solution.py:29
  38.1 11.6 %collective-permute-start.15 = (f32[256,256]{1,0:T(8,128)S(1)}, f32[256,256]{1,0:T(8,128)S(1)}, u32[]{:S(2)}, u32[]{:S(2)}) collective-permute-start(f32[256,256]{1,0:T(8,128)S(1)} %pad_maximum_fusion), channel_id=1, source_target_pairs={{0,4},{1,5},{2,6},{3,7},{4,8},{5,9},{6,10},{7,11},{8,12},{9,13},{1... | collective-permute-start | bytes 786440 | tf_op jit(solution)/shard_map/ppermute | solution.py:29
  38.4 11.4 %collective-permute-start.17 = (f32[128,256]{1,0:T(8,128)S(1)}, f32[128,256]{1,0:T(8,128)S(1)}, u32[]{:S(2)}, u32[]{:S(2)}) collective-permute-start(f32[128,256]{1,0:T(8,128)S(1)} %add.43), channel_id=1, source_target_pairs={{0,3},{1,2},{2,1},{3,0},{4,7},{5,6},{6,5},{7,4},{8,11},{9,10},{10,... | collective-permute-start | bytes 393224 | tf_op jit(solution)/shard_map/ppermute | solution.py:29
  40.6 9.2 %collective-permute-start.18 = (f32[128,256]{1,0:T(8,128)S(1)}, f32[128,256]{1,0:T(8,128)S(1)}, u32[]{:S(2)}, u32[]{:S(2)}) collective-permute-start(f32[128,256]{1,0:T(8,128)S(1)} %add.44), channel_id=1, source_target_pairs={{0,3},{1,2},{2,1},{3,0},{4,7},{5,6},{6,5},{7,4},{8,11},{9,10},{10,... | collective-permute-start | bytes 393224 | tf_op jit(solution)/shard_map/ppermute | solution.py:29
  42.4 7.4 %collective-permute-start.16 = (f32[256,256]{1,0:T(8,128)S(1)}, f32[256,256]{1,0:T(8,128)S(1)}, u32[]{:S(2)}, u32[]{:S(2)}) collective-permute-start(f32[256,256]{1,0:T(8,128)S(1)} %get-tuple-element.75), channel_id=1, source_target_pairs={{0,1},{1,0},{2,3},{3,2},{4,5},{5,4},{6,7},{7,6},{8,9},{9,8},{10,11... | collective-permute-start | bytes 786440 | tf_op jit(solution)/shard_map/ppermute | solution.py:29

commit v5 on v4

--- a/solution.py
+++ b/solution.py
@@ -122,7 +122,7 @@
     step, tiles_per_shard, column_tiles, user_rows, tile_rows, tile_columns, tile_counts, ratings, fetched=False
 ):
     slots, tile = ratings.shape[3], ratings.shape[4]
-    group = slot_group(slots)
+    group = slot_group(slots) * (2 if fetched and slots % 16 == 0 else 1)
     lists = (tile_counts, tile_rows, tile_columns)
     scratch = [pltpu.SMEM(some.shape, jnp.int32) for some in lists] + [pltpu.SemaphoreType.DMA((3,))]
     if not fetched:
@@ -231,7 +231,7 @@
 def update_users(users, items, residuals, last):
     user_rows, width = users.shape
     tile = residuals[0].shape[-1]
-    chunk = min((2 if last else 4) * tile, user_rows)
+    chunk = min((1 if last else 4) * tile, user_rows)
     item_rows = sum(block.shape[0] for block in items)
     full = jax.ShapeDtypeStruct(users.shape, F32)
     if last:
@@ -311,11 +311,11 @@
             shared = route(after(block, *mark), 0, 1)
             (passed,) = run(2, block, first)
             passed = route(passed, 0, 1)
-            if step > 0 and p == len(held[2]) - 1:
-                held[1] = [route(after(held[0][0], *mark), 0, 1)]
             for k in range(block.shape[0] // tile):
                 h, rows = first + k, parts_rows[k]
                 (own,) = run(3, shared[rows], h)
+                if step > 0 and h == per_shard - 1:
+                    held[1] = [route(after(held[0][0], *mark), 0, 1)]
                 own = lax.optimization_barrier(own + passed[rows])
                 mark.append(own)
                 sums.append(route(own, 0, 3))
@@ -370,7 +370,8 @@
 
     def shards(user_factors, item_factors, *lists):
         tile = lists[-1].shape[-1]
-        paired = mesh.shape["users"] == 4 and item_factors.shape[0] % tile == 0
+        per_shard, rest = divmod(item_factors.shape[0], tile)
+        paired = mesh.shape["users"] == 4 and rest == 0 and per_shard.bit_count() == 1
         body = paired_shards if paired else gathered_shards
         return body(user_factors, item_factors, *lists)
 

time: 50.7 us -> 50.7 us (level)
  transfers between devices with their start and end apart: 19 -> 19, of which waited for: 7 -> 8; matrix products, arithmetic and copies ran while one was open for 0% -> 0% of each run, Pallas kernels for 30% -> 30%
where the time goes in v5:
time: 50.7 us; the launch traced here: 50.6 us
  waiting for transfers between devices  18.7 us (37%)
  Pallas kernels  15.3 us (30%)
  starting transfers between devices  13.7 us (27%)
  other arithmetic  1.96 us (4%)
  between operations  0.91 us (2%)
    ppermute x19, waiting for transfers between devices, route(): return lax.ppermute(block, ('strata', 'users'), pairs)  18.7 us
    ppermute x19, starting transfers between devices, route(): return lax.ppermute(block, ('strata', 'users'), pairs)  13.7 us
    pallas_call x9, Pallas kernels, terms(): pl.pallas_call(functools.partial(terms_kernel, columns, sizes, min(CHUNK_...  7.55 us
    pallas_call x2, Pallas kernels, update_users(): pl.pallas_call(functools.partial(users_kernel, len(items), chunk, last),...  3.93 us
    pallas_call x2, Pallas kernels, dense_ratings(): pl.pallas_call(functools.partial(dense_kernel, step, tiles_per_shard, gro...  3.4 us
  transfers between devices with their start and end apart: 19, of which 8 were waited for; matrix products, arithmetic and copies ran while one was open for 0% of the time, Pallas kernels for 30%

profile of v5, /device:TPU:0, one launch (start us, length us, event | category | flops | bytes accessed | tf_op | source)
XLA Modules:
  0.0 50.6 jit_solution(10527152401603477962)
XLA Ops:
  0.6 1.0 %convert_element_type.9.refs_0_ = bf16[256,256]{1,0:T(8,128)(2,1)S(1)} convert(f32[256,256]{1,0:T(8,128)} %param.7) | non-fusion elementwise | flops 65536 | bytes 393216 | tf_op jit(solution)/shard_map/convert_element_type | solution.py:269
  1.6 0.0 copy-start
  1.6 0.6 %collective-permute-start.1 = (bf16[256,256]{1,0:T(8,128)(2,1)S(1)}, bf16[256,256]{1,0:T(8,128)(2,1)S(1)}, u32[]{:S(2)}, u32[]{:S(2)}) collective-permute-start(bf16[256,256]{1,0:T(8,128)(2,1)S(1)} %convert_element_type.9.refs_0_), channel_id=1, source_target_pairs={{0,1},{1,0},{2,3},{3,2},{4,5},{5,4},{6,7},{7,6},{8,9},{9,8},{10,11... | collective-permute-start | bytes 393224 | tf_op jit(solution)/shard_map/ppermute | solution.py:29
  2.2 2.6 %collective-permute-start = (bf16[256,256]{1,0:T(8,128)(2,1)S(1)}, bf16[256,256]{1,0:T(8,128)(2,1)S(1)}, u32[]{:S(2)}, u32[]{:S(2)}) collective-permute-start(bf16[256,256]{1,0:T(8,128)(2,1)S(1)} %convert_element_type.9.refs_0_), channel_id=1, source_target_pairs={{0,2},{1,3},{2,0},{3,1},{4,6},{5,7},{6,4},{7,5},{8,10},{9,11},{10,... | collective-permute-start | bytes 393224 | tf_op jit(solution)/shard_map/ppermute | solution.py:29
  4.8 2.2 %shard_map.77.dense_ref = bf16[8,16,128,128]{3,2,1,0:T(8,128)(2,1)S(1)} custom-call(s32[1,1,2]{2,1,0:T(1,128)} %counts_hbm.3, s32[1,1,2,64]{3,2,1,0:T(2,128)} %rows_hbm.1, s32[1,1,2,64]{3,2,1,0:T(2,128)} %columns_hbm.3, s32[1,1,2,64,128,128]{5,4,3,2,1,0:T(8,128)} %ratings.3), custom_call_target="tpu_custom_call" | custom-call | flops 2000000000 | bytes 8388608 | tf_op jit(solution)/shard_map/pallas_call | solution.py:135
  7.0 0.0 copy-done
  7.0 0.4 lower.1
  7.4 0.0 collective-permute-done.1.refs_1_
  7.4 1.5 %shard_map.78 = (bf16[16,512,128]{2,1,0:T(8,128)(2,1)S(1)}, f32[256,256]{1,0:T(8,128)S(1)}, f32[256,256]{1,0:T(8,128)S(1)}) custom-call(bf16[2048,256]{1,0:T(8,128)(2,1)S(1)} %get-tuple-element.44.users_ref, bf16[256,2048]{1,0:T(8,128)(2,1)S(1)} %get-tuple-element.45.users_t_ref, bf16[8,16,128,128]{3,2,1,0:T(8,128)(2,1)S(1)} %shard_map.77.dense_ref, ...), custom_call_target="tpu_custom_call" | custom-call | flops 1073741824 | bytes 1048576 | tf_op jit(solution)/shard_map/pallas_call | solution.py:187
  9.0 0.0 collective-permute-done.refs_0_.refs_2_
  9.0 0.2 collective-permute-start.2
  9.2 0.9 %shard_map.79 = (bf16[16,256,128]{2,1,0:T(8,128)(2,1)S(1)}, f32[256,256]{1,0:T(8,128)S(1)}) custom-call(bf16[2048,256]{1,0:T(8,128)(2,1)S(1)} %get-tuple-element.44.users_ref, bf16[256,2048]{1,0:T(8,128)(2,1)S(1)} %get-tuple-element.45.users_t_ref, bf16[8,16,128,128]{3,2,1,0:T(8,128)(2,1)S(1)} %shard_map.77.dense_ref, ...), custom_call_target="tpu_custom_call" | custom-call | flops 536870912 | bytes 1048576 | tf_op jit(solution)/shard_map/pallas_call | solution.py:187
  10.1 0.4 collective-permute-start.3
  10.5 0.2 collective-permute-start.4
  10.7 0.0 collective-permute-done.2
  10.7 0.0 slice-start
  10.7 0.6 %shard_map.80 = (bf16[16,128,128]{2,1,0:T(8,128)(2,1)S(1)}, f32[128,256]{1,0:T(8,128)S(1)}) custom-call(bf16[2048,256]{1,0:T(8,128)(2,1)S(1)} %get-tuple-element.44.users_ref, bf16[256,2048]{1,0:T(8,128)(2,1)S(1)} %get-tuple-element.45.users_t_ref, bf16[8,16,128,128]{3,2,1,0:T(8,128)(2,1)S(1)} %shard_map.77.dense_ref, ...), custom_call_target="tpu_custom_call" | custom-call | flops 268435456 | bytes 1048576 | tf_op jit(solution)/shard_map/pallas_call | solution.py:187
  11.3 0.4 collective-permute-done.3
  11.7 0.0 copy-start.1
  11.7 0.0 slice-start.1
  11.7 0.6 %shard_map.81 = (bf16[16,128,128]{2,1,0:T(8,128)(2,1)S(1)}, f32[128,256]{1,0:T(8,128)S(1)}) custom-call(bf16[2048,256]{1,0:T(8,128)(2,1)S(1)} %get-tuple-element.44.users_ref, bf16[256,2048]{1,0:T(8,128)(2,1)S(1)} %get-tuple-element.45.users_t_ref, bf16[8,16,128,128]{3,2,1,0:T(8,128)(2,1)S(1)} %shard_map.77.dense_ref, ...), custom_call_target="tpu_custom_call" | custom-call | flops 268435456 | bytes 1048576 | tf_op jit(solution)/shard_map/pallas_call | solution.py:187
  12.4 1.6 %collective-permute-start.7 = (f32[128,256]{1,0:T(8,128)S(1)}, f32[128,256]{1,0:T(8,128)S(1)}, u32[]{:S(2)}, u32[]{:S(2)}) collective-permute-start(f32[128,256]{1,0:T(8,128)S(1)} %slice_add_fusion), channel_id=1, source_target_pairs={{0,3},{1,2},{2,1},{3,0},{4,7},{5,6},{6,5},{7,4},{8,11},{9,10},{10,... | collective-permute-start | bytes 393224 | tf_op jit(solution)/shard_map/ppermute | solution.py:29
  13.9 0.2 collective-permute-start.5
  14.2 0.0 collective-permute-done.4
  14.2 0.0 copy-done.1
  14.3 1.7 %users.2 = (f32[2048,256]{1,0:T(8,128)S(1)}, bf16[2048,256]{1,0:T(8,128)(2,1)S(1)}, bf16[256,2048]{1,0:T(8,128)(2,1)S(1)}) custom-call(f32[2048,256]{1,0:T(8,128)S(1)} %copy-done, bf16[256,256]{1,0:T(8,128)(2,1)S(1)} %convert_element_type.9.refs_0_, bf16[256,256]{1,0:T(8,128)(2,1)S(1)} %collective-permute-done.1.refs_1_, ...), custom_call_target="tpu_custom_call" | custom-call | flops 1073741824 | bytes 4194304 | tf_op jit(solution)/shard_map/users/pallas_call | solution.py:242
  16.0 0.0 slice-done
  16.0 0.0 slice-done.1
  16.0 1.2 %shard_map.82.dense_ref = bf16[8,16,128,128]{3,2,1,0:T(8,128)(2,1)S(1)} custom-call(s32[1,1,2]{2,1,0:T(1,128)} %counts_hbm.3, s32[1,1,2,64]{3,2,1,0:T(2,128)} %rows_hbm.1, s32[1,1,2,64]{3,2,1,0:T(2,128)} %columns_hbm.3, s32[1,1,2,64,128,128]{5,4,3,2,1,0:T(8,128)S(1)} %bitcast.1), custom_call_target="tpu_custom_call" | custom-call | flops 2000000000 | bytes 8388608 | tf_op jit(solution)/shard_map/pallas_call | solution.py:135
  17.2 3.3 %collective-permute-done.5 = f32[128,256]{1,0:T(8,128)S(1)} collective-permute-done((f32[128,256]{1,0:T(8,128)S(1)}, f32[128,256]{1,0:T(8,128)S(1)}, u32[]{:S(2)}, u32[]{:S(2)}) %collective-permute-start.5) | collective-permute-done | bytes 131104 | tf_op jit(solution)/shard_map/ppermute | solution.py:29
  20.6 2.5 %collective-permute-start.6 = (bf16[128,256]{1,0:T(8,128)(2,1)S(1)}, bf16[128,256]{1,0:T(8,128)(2,1)S(1)}, u32[]{:S(2)}, u32[]{:S(2)}) collective-permute-start(bf16[128,256]{1,0:T(8,128)(2,1)S(1)} %get-tuple-element.86), channel_id=1, source_target_pairs={{0,6},{1,7},{2,4},{3,5},{4,10},{5,11},{6,8},{7,9},{8,14},{9,15},{1... | collective-permute-start | bytes 196616 | tf_op jit(solution)/shard_map/ppermute | solution.py:29
  23.1 0.0 collective-permute-done.7
  23.1 1.5 %collective-permute-start.9 = (bf16[128,256]{1,0:T(8,128)(2,1)S(1)}, bf16[128,256]{1,0:T(8,128)(2,1)S(1)}, u32[]{:S(2)}, u32[]{:S(2)}) collective-permute-start(bf16[128,256]{1,0:T(8,128)(2,1)S(1)} %get-tuple-element.84), channel_id=1, source_target_pairs={{0,6},{1,7},{2,4},{3,5},{4,10},{5,11},{6,8},{7,9},{8,14},{9,15},{1... | collective-permute-start | bytes 196616 | tf_op jit(solution)/shard_map/ppermute | solution.py:29
  24.6 4.1 %collective-permute-done.6.refs_0_ = bf16[128,256]{1,0:T(8,128)(2,1)S(1)} collective-permute-done((bf16[128,256]{1,0:T(8,128)(2,1)S(1)}, bf16[128,256]{1,0:T(8,128)(2,1)S(1)}, u32[]{:S(2)}, u32[]{:S(2)}) %collective-permute-start.6) | collective-permute-done | bytes 65568 | tf_op jit(solution)/shard_map/ppermute | solution.py:29
  28.7 0.0 collective-permute-start.10
  28.7 0.6 %shard_map.83 = (bf16[16,128,128]{2,1,0:T(8,128)(2,1)S(1)}, f32[128,256]{1,0:T(8,128)S(1)}) custom-call(bf16[2048,256]{1,0:T(8,128)(2,1)S(1)} %get-tuple-element.61.users_ref, bf16[256,2048]{1,0:T(8,128)(2,1)S(1)} %get-tuple-element.62.users_t_ref, bf16[8,16,128,128]{3,2,1,0:T(8,128)(2,1)S(1)} %shard_map.82.dense_ref, ...), custom_call_target="tpu_custom_call" | custom-call | flops 805306368 | bytes 1048576 | tf_op jit(solution)/shard_map/pallas_call | solution.py:187
  29.3 0.6 %collective-permute-start.11 = (f32[128,256]{1,0:T(8,128)S(1)}, f32[128,256]{1,0:T(8,128)S(1)}, u32[]{:S(2)}, u32[]{:S(2)}) collective-permute-start(f32[128,256]{1,0:T(8,128)S(1)} %get-tuple-element.66), channel_id=1, source_target_pairs={{0,1},{1,0},{2,3},{3,2},{4,5},{5,4},{6,7},{7,6},{8,9},{9,8},{10,11... | collective-permute-start | bytes 393224 | tf_op jit(solution)/shard_map/ppermute | solution.py:29
  29.9 0.1 collective-permute-start.8
  30.0 0.0 collective-permute-done.10.refs_0_.refs_1_
  30.0 0.6 %shard_map.84 = (bf16[16,128,128]{2,1,0:T(8,128)(2,1)S(1)}, f32[128,256]{1,0:T(8,128)S(1)}) custom-call(bf16[2048,256]{1,0:T(8,128)(2,1)S(1)} %get-tuple-element.61.users_ref, bf16[256,2048]{1,0:T(8,128)(2,1)S(1)} %get-tuple-element.62.users_t_ref, bf16[8,16,128,128]{3,2,1,0:T(8,128)(2,1)S(1)} %shard_map.82.dense_ref, ...), custom_call_target="tpu_custom_call" | custom-call | flops 805306368 | bytes 1048576 | tf_op jit(solution)/shard_map/pallas_call | solution.py:187
  30.6 0.3 collective-permute-done.11
  30.9 0.1 collective-permute-done.9.refs_0_.refs_2_
  31.0 0.4 collective-permute-start.12
  31.4 0.6 %shard_map.85 = (bf16[16,128,128]{2,1,0:T(8,128)(2,1)S(1)}, f32[128,256]{1,0:T(8,128)S(1)}) custom-call(bf16[2048,256]{1,0:T(8,128)(2,1)S(1)} %get-tuple-element.61.users_ref, bf16[256,2048]{1,0:T(8,128)(2,1)S(1)} %get-tuple-element.62.users_t_ref, bf16[8,16,128,128]{3,2,1,0:T(8,128)(2,1)S(1)} %shard_map.82.dense_ref, ...), custom_call_target="tpu_custom_call" | custom-call | flops 805306368 | bytes 1048576 | tf_op jit(solution)/shard_map/pallas_call | solution.py:187
  32.0 0.2 collective-permute-start.13
  32.2 0.1 collective-permute-done.12.refs_0_.refs_3_
  32.3 0.6 %shard_map.86 = (bf16[16,128,128]{2,1,0:T(8,128)(2,1)S(1)}, f32[128,256]{1,0:T(8,128)S(1)}) custom-call(bf16[2048,256]{1,0:T(8,128)(2,1)S(1)} %get-tuple-element.61.users_ref, bf16[256,2048]{1,0:T(8,128)(2,1)S(1)} %get-tuple-element.62.users_t_ref, bf16[8,16,128,128]{3,2,1,0:T(8,128)(2,1)S(1)} %shard_map.82.dense_ref, ...), custom_call_target="tpu_custom_call" | custom-call | flops 805306368 | bytes 1048576 | tf_op jit(solution)/shard_map/pallas_call | solution.py:187
  32.9 5.2 %collective-permute-done.8.refs_0_.refs_4_ = bf16[256,256]{1,0:T(8,128)(2,1)S(1)} collective-permute-done((bf16[256,256]{1,0:T(8,128)(2,1)S(1)}, bf16[256,256]{1,0:T(8,128)(2,1)S(1)}, u32[]{:S(2)}, u32[]{:S(2)}) %collective-permute-start.8) | collective-permute-done | bytes 131104 | tf_op jit(solution)/shard_map/ppermute | solution.py:29
  38.1 0.0 collective-permute-start.14
  38.1 0.2 collective-permute-start.15
  38.4 1.6 %collective-permute-start.17 = (f32[128,256]{1,0:T(8,128)S(1)}, f32[128,256]{1,0:T(8,128)S(1)}, u32[]{:S(2)}, u32[]{:S(2)}) collective-permute-start(f32[128,256]{1,0:T(8,128)S(1)} %add.43), channel_id=1, source_target_pairs={{0,3},{1,2},{2,1},{3,0},{4,7},{5,6},{6,5},{7,4},{8,11},{9,10},{10,... | collective-permute-start | bytes 393224 | tf_op jit(solution)/shard_map/ppermute | solution.py:29
  40.0 0.0 collective-permute-done.13
  40.0 0.3 collective-permute-start.18
  40.3 0.0 collective-permute-done.14.refs_1_.refs_5_
  40.3 1.5 %shard_map.87 = (bf16[16,512,128]{2,1,0:T(8,128)(2,1)S(1)}, f32[256,256]{1,0:T(8,128)S(1)}, f32[256,256]{1,0:T(8,128)S(1)}) custom-call(bf16[2048,256]{1,0:T(8,128)(2,1)S(1)} %get-tuple-element.61.users_ref, bf16[256,2048]{1,0:T(8,128)(2,1)S(1)} %get-tuple-element.62.users_t_ref, bf16[8,16,128,128]{3,2,1,0:T(8,128)(2,1)S(1)} %shard_map.82.dense_ref, ...), custom_call_target="tpu_custom_call" | custom-call | flops 3221225472 | bytes 1048576 | tf_op jit(solution)/shard_map/pallas_call | solution.py:187
  41.8 0.6 %collective-permute-start.16 = (f32[256,256]{1,0:T(8,128)S(1)}, f32[256,256]{1,0:T(8,128)S(1)}, u32[]{:S(2)}, u32[]{:S(2)}) collective-permute-start(f32[256,256]{1,0:T(8,128)S(1)} %get-tuple-element.75), channel_id=1, source_target_pairs={{0,1},{1,0},{2,3},{3,2},{4,5},{5,4},{6,7},{7,6},{8,9},{9,8},{10,11... | collective-permute-start | bytes 786440 | tf_op jit(solution)/shard_map/ppermute | solution.py:29
  42.4 2.2 %users.3 = f32[2048,256]{1,0:T(8,128)} custom-call(f32[2048,256]{1,0:T(8,128)S(1)} %get-tuple-element.59.users_ref, bf16[128,256]{1,0:T(8,128)(2,1)S(1)} %collective-permute-done.6.refs_0_, bf16[128,256]{1,0:T(8,128)(2,1)S(1)} %collective-permute-done.10.refs_0_.refs_1_, bf16[128,256]{1,0:T(8,128)(2,1)S(1)} %collective-permute-done.9.refs_0_.refs_2_, ...), custom_call_target="tpu_custom_call" | custom-call | flops 3221225472 | bytes 4194304 | tf_op jit(solution)/shard_map/users/pallas_call | solution.py:242
  44.6 5.2 %collective-permute-done.15 = f32[256,256]{1,0:T(8,128)S(1)} collective-permute-done((f32[256,256]{1,0:T(8,128)S(1)}, f32[256,256]{1,0:T(8,128)S(1)}, u32[]{:S(2)}, u32[]{:S(2)}) %collective-permute-start.15) | collective-permute-done | bytes 262176 | tf_op jit(solution)/shard_map/ppermute | solution.py:29
  49.8 0.0 collective-permute-done.17
  49.8 0.0 collective-permute-done.18
  49.8 0.0 collective-permute-done.16
  49.8 0.8 %fusion.2 = f32[256,256]{1,0:T(8,128)} fusion(f32[256,256]{1,0:T(8,128)S(1)} %collective-permute-done.15, f32[128,256]{1,0:T(8,128)S(1)} %collective-permute-done.18, f32[128,256]{1,0:T(8,128)S(1)} %collective-permute-done.17, f32[256,256]{1,0:T(8,128)S(1)} %get-tuple-element.83, f32[256,256]{1,0:T(8,128)S(1)} %collective-permute-done.16), kind=kLoop, calls=%fused_computation.4 | loop fusion | flops 458752 | bytes 1310720 | tf_op jit(solution)/shard_map/add | solution.py:257
  (13 shorter events, 0.2 us)
Async XLA Ops:
  1.6 5.4 %copy-start = (f32[2048,256]{1,0:T(8,128)S(1)}, f32[2048,256]{1,0:T(8,128)}, u32[]{:S(2)}) copy-start(f32[2048,256]{1,0:T(8,128)} %users_ref.2) | copy-start | bytes 6291460
  1.6 5.8 %collective-permute-start.1 = (bf16[256,256]{1,0:T(8,128)(2,1)S(1)}, bf16[256,256]{1,0:T(8,128)(2,1)S(1)}, u32[]{:S(2)}, u32[]{:S(2)}) collective-permute-start(bf16[256,256]{1,0:T(8,128)(2,1)S(1)} %convert_element_type.9.refs_0_), channel_id=1, source_target_pairs={{0,1},{1,0},{2,3},{3,2},{4,5},{5,4},{6,7},{7,6},{8,9},{9,8},{10,11... | collective-permute-start | bytes 393224 | tf_op jit(solution)/shard_map/ppermute | solution.py:29
  2.2 6.8 %collective-permute-start = (bf16[256,256]{1,0:T(8,128)(2,1)S(1)}, bf16[256,256]{1,0:T(8,128)(2,1)S(1)}, u32[]{:S(2)}, u32[]{:S(2)}) collective-permute-start(bf16[256,256]{1,0:T(8,128)(2,1)S(1)} %convert_element_type.9.refs_0_), channel_id=1, source_target_pairs={{0,2},{1,3},{2,0},{3,1},{4,6},{5,7},{6,4},{7,5},{8,10},{9,11},{10,... | collective-permute-start | bytes 393224 | tf_op jit(solution)/shard_map/ppermute | solution.py:29
  9.0 1.7 %collective-permute-start.2 = (bf16[256,256]{1,0:T(8,128)(2,1)S(1)}, bf16[256,256]{1,0:T(8,128)(2,1)S(1)}, u32[]{:S(2)}, u32[]{:S(2)}) collective-permute-start(bf16[256,256]{1,0:T(8,128)(2,1)S(1)} %collective-permute-done.refs_0_.refs_2_), channel_id=1, source_target_pairs={{0,1},{1,0},{2,3},{3,2},{4,5},{5,4},{6,7},{7,6},{8,9},{9,8},{10,11... | collective-permute-start | bytes 393224 | tf_op jit(solution)/shard_map/ppermute | solution.py:29
  10.1 1.6 %collective-permute-start.3 = (f32[256,256]{1,0:T(8,128)S(1)}, f32[256,256]{1,0:T(8,128)S(1)}, u32[]{:S(2)}, u32[]{:S(2)}) collective-permute-start(f32[256,256]{1,0:T(8,128)S(1)} %get-tuple-element.49), channel_id=1, source_target_pairs={{0,1},{1,0},{2,3},{3,2},{4,5},{5,4},{6,7},{7,6},{8,9},{9,8},{10,11... | collective-permute-start | bytes 786440 | tf_op jit(solution)/shard_map/ppermute | solution.py:29
  10.5 3.7 %collective-permute-start.4 = (f32[256,256]{1,0:T(8,128)S(1)}, f32[256,256]{1,0:T(8,128)S(1)}, u32[]{:S(2)}, u32[]{:S(2)}) collective-permute-start(f32[256,256]{1,0:T(8,128)S(1)} %get-tuple-element.47), channel_id=1, source_target_pairs={{0,1},{1,0},{2,3},{3,2},{4,5},{5,4},{6,7},{7,6},{8,9},{9,8},{10,11... | collective-permute-start | bytes 786440 | tf_op jit(solution)/shard_map/ppermute | solution.py:29
  10.7 5.3 %slice-start = ((s8[8388608]{0:T(1024)(128)(4,1)}), s8[4194304]{0:T(1024)(128)(4,1)S(1)}, s32[]{:S(2)}) async-start(s8[8388608]{0:T(1024)(128)(4,1)} %bitcast), calls=%async_computation | async-start | bytes 8388608
  11.7 2.5 %copy-start.1 = (f32[256,256]{1,0:T(8,128)S(1)}, f32[256,256]{1,0:T(8,128)}, u32[]{:S(2)}) copy-start(f32[256,256]{1,0:T(8,128)} %param.7) | copy-start | bytes 786436
  11.7 4.3 %slice-start.1 = ((s8[8388608]{0:T(1024)(128)(4,1)}), s8[4194304]{0:T(1024)(128)(4,1)S(1)}, s32[]{:S(2)}) async-start(s8[8388608]{0:T(1024)(128)(4,1)} %bitcast), calls=%async_computation.1 | async-start | bytes 8388608
  12.4 10.7 %collective-permute-start.7 = (f32[128,256]{1,0:T(8,128)S(1)}, f32[128,256]{1,0:T(8,128)S(1)}, u32[]{:S(2)}, u32[]{:S(2)}) collective-permute-start(f32[128,256]{1,0:T(8,128)S(1)} %slice_add_fusion), channel_id=1, source_target_pairs={{0,3},{1,2},{2,1},{3,0},{4,7},{5,6},{6,5},{7,4},{8,11},{9,10},{10,... | collective-permute-start | bytes 393224 | tf_op jit(solution)/shard_map/ppermute | solution.py:29
  13.9 6.6 %collective-permute-start.5 = (f32[128,256]{1,0:T(8,128)S(1)}, f32[128,256]{1,0:T(8,128)S(1)}, u32[]{:S(2)}, u32[]{:S(2)}) collective-permute-start(f32[128,256]{1,0:T(8,128)S(1)} %slice_add_fusion.1), channel_id=1, source_target_pairs={{0,3},{1,2},{2,1},{3,0},{4,7},{5,6},{6,5},{7,4},{8,11},{9,10},{10,... | collective-permute-start | bytes 393224 | tf_op jit(solution)/shard_map/ppermute | solution.py:29
  20.6 8.2 %collective-permute-start.6 = (bf16[128,256]{1,0:T(8,128)(2,1)S(1)}, bf16[128,256]{1,0:T(8,128)(2,1)S(1)}, u32[]{:S(2)}, u32[]{:S(2)}) collective-permute-start(bf16[128,256]{1,0:T(8,128)(2,1)S(1)} %get-tuple-element.86), channel_id=1, source_target_pairs={{0,6},{1,7},{2,4},{3,5},{4,10},{5,11},{6,8},{7,9},{8,14},{9,15},{1... | collective-permute-start | bytes 196616 | tf_op jit(solution)/shard_map/ppermute | solution.py:29
  23.1 7.9 %collective-permute-start.9 = (bf16[128,256]{1,0:T(8,128)(2,1)S(1)}, bf16[128,256]{1,0:T(8,128)(2,1)S(1)}, u32[]{:S(2)}, u32[]{:S(2)}) collective-permute-start(bf16[128,256]{1,0:T(8,128)(2,1)S(1)} %get-tuple-element.84), channel_id=1, source_target_pairs={{0,6},{1,7},{2,4},{3,5},{4,10},{5,11},{6,8},{7,9},{8,14},{9,15},{1... | collective-permute-start | bytes 196616 | tf_op jit(solution)/shard_map/ppermute | solution.py:29
  28.7 1.3 %collective-permute-start.10 = (bf16[128,256]{1,0:T(8,128)(2,1)S(1)}, bf16[128,256]{1,0:T(8,128)(2,1)S(1)}, u32[]{:S(2)}, u32[]{:S(2)}) collective-permute-start(bf16[128,256]{1,0:T(8,128)(2,1)S(1)} %collective-permute-done.6.refs_0_), channel_id=1, source_target_pairs={{0,1},{1,0},{2,3},{3,2},{4,5},{5,4},{6,7},{7,6},{8,9},{9,8},{10,11... | collective-permute-start | bytes 196616 | tf_op jit(solution)/shard_map/ppermute | solution.py:29
  29.3 1.6 %collective-permute-start.11 = (f32[128,256]{1,0:T(8,128)S(1)}, f32[128,256]{1,0:T(8,128)S(1)}, u32[]{:S(2)}, u32[]{:S(2)}) collective-permute-start(f32[128,256]{1,0:T(8,128)S(1)} %get-tuple-element.66), channel_id=1, source_target_pairs={{0,1},{1,0},{2,3},{3,2},{4,5},{5,4},{6,7},{7,6},{8,9},{9,8},{10,11... | collective-permute-start | bytes 393224 | tf_op jit(solution)/shard_map/ppermute | solution.py:29
  29.9 8.2 %collective-permute-start.8 = (bf16[256,256]{1,0:T(8,128)(2,1)S(1)}, bf16[256,256]{1,0:T(8,128)(2,1)S(1)}, u32[]{:S(2)}, u32[]{:S(2)}) collective-permute-start(bf16[256,256]{1,0:T(8,128)(2,1)S(1)} %pad_maximum_fusion.1), channel_id=1, source_target_pairs={{0,4},{1,5},{2,6},{3,7},{4,8},{5,9},{6,10},{7,11},{8,12},{9,13},{1... | collective-permute-start | bytes 393224 | tf_op jit(solution)/shard_map/ppermute | solution.py:29
  31.0 1.3 %collective-permute-start.12 = (bf16[128,256]{1,0:T(8,128)(2,1)S(1)}, bf16[128,256]{1,0:T(8,128)(2,1)S(1)}, u32[]{:S(2)}, u32[]{:S(2)}) collective-permute-start(bf16[128,256]{1,0:T(8,128)(2,1)S(1)} %collective-permute-done.9.refs_0_.refs_2_), channel_id=1, source_target_pairs={{0,1},{1,0},{2,3},{3,2},{4,5},{5,4},{6,7},{7,6},{8,9},{9,8},{10,11... | collective-permute-start | bytes 196616 | tf_op jit(solution)/shard_map/ppermute | solution.py:29
  32.0 8.0 %collective-permute-start.13 = (f32[128,256]{1,0:T(8,128)S(1)}, f32[128,256]{1,0:T(8,128)S(1)}, u32[]{:S(2)}, u32[]{:S(2)}) collective-permute-start(f32[128,256]{1,0:T(8,128)S(1)} %get-tuple-element.70), channel_id=1, source_target_pairs={{0,1},{1,0},{2,3},{3,2},{4,5},{5,4},{6,7},{7,6},{8,9},{9,8},{10,11... | collective-permute-start | bytes 393224 | tf_op jit(solution)/shard_map/ppermute | solution.py:29
  38.1 2.2 %collective-permute-start.14 = (bf16[256,256]{1,0:T(8,128)(2,1)S(1)}, bf16[256,256]{1,0:T(8,128)(2,1)S(1)}, u32[]{:S(2)}, u32[]{:S(2)}) collective-permute-start(bf16[256,256]{1,0:T(8,128)(2,1)S(1)} %collective-permute-done.8.refs_0_.refs_4_), channel_id=1, source_target_pairs={{0,1},{1,0},{2,3},{3,2},{4,5},{5,4},{6,7},{7,6},{8,9},{9,8},{10,11... | collective-permute-start | bytes 393224 | tf_op jit(solution)/shard_map/ppermute | solution.py:29
  38.1 11.6 %collective-permute-start.15 = (f32[256,256]{1,0:T(8,128)S(1)}, f32[256,256]{1,0:T(8,128)S(1)}, u32[]{:S(2)}, u32[]{:S(2)}) collective-permute-start(f32[256,256]{1,0:T(8,128)S(1)} %pad_maximum_fusion), channel_id=1, source_target_pairs={{0,4},{1,5},{2,6},{3,7},{4,8},{5,9},{6,10},{7,11},{8,12},{9,13},{1... | collective-permute-start | bytes 786440 | tf_op jit(solution)/shard_map/ppermute | solution.py:29
  38.4 11.4 %collective-permute-start.17 = (f32[128,256]{1,0:T(8,128)S(1)}, f32[128,256]{1,0:T(8,128)S(1)}, u32[]{:S(2)}, u32[]{:S(2)}) collective-permute-start(f32[128,256]{1,0:T(8,128)S(1)} %add.43), channel_id=1, source_target_pairs={{0,3},{1,2},{2,1},{3,0},{4,7},{5,6},{6,5},{7,4},{8,11},{9,10},{10,... | collective-permute-start | bytes 393224 | tf_op jit(solution)/shard_map/ppermute | solution.py:29
  40.0 9.8 %collective-permute-start.18 = (f32[128,256]{1,0:T(8,128)S(1)}, f32[128,256]{1,0:T(8,128)S(1)}, u32[]{:S(2)}, u32[]{:S(2)}) collective-permute-start(f32[128,256]{1,0:T(8,128)S(1)} %add.44), channel_id=1, source_target_pairs={{0,3},{1,2},{2,1},{3,0},{4,7},{5,6},{6,5},{7,4},{8,11},{9,10},{10,... | collective-permute-start | bytes 393224 | tf_op jit(solution)/shard_map/ppermute | solution.py:29
  41.8 8.0 %collective-permute-start.16 = (f32[256,256]{1,0:T(8,128)S(1)}, f32[256,256]{1,0:T(8,128)S(1)}, u32[]{:S(2)}, u32[]{:S(2)}) collective-permute-start(f32[256,256]{1,0:T(8,128)S(1)} %get-tuple-element.75), channel_id=1, source_target_pairs={{0,1},{1,0},{2,3},{3,2},{4,5},{5,4},{6,7},{7,6},{8,9},{9,8},{10,11... | collective-permute-start | bytes 786440 | tf_op jit(solution)/shard_map/ppermute | solution.py:29
